TPU v7x, 32 devices: a whole 2x2x4 slice. The times are simulated.
32 devices in a mesh: dp: 2 (over x), tp: 4 (over z), cp: 4 (over y, core).
Axes of the slice: x: 2, y: 2, z: 4, core: 2. Of those that a mesh axis runs over, the one named last changes fastest.
Arguments:
- x_in: bfloat16 [12, 1536, 2048], P('dp', 'cp'), parts along dimension 0
- segment_ids: int32 [12, 1536], P('dp', 'cp'), parts along dimension 0
- positions: int32 [12, 1536], P('dp', 'cp'), parts along dimension 0
- w_query: bfloat16 [2048, 2048], P(None, 'tp')
- w_key: bfloat16 [2048, 2048], P(None, 'tp')
- w_value: bfloat16 [2048, 2048], P(None, 'tp')
- w_out: bfloat16 [2048, 2048], P('tp')
- norm_gain: float32 [2048], replicated
- grad_out: bfloat16 [12, 1536, 2048], P('dp', 'cp'), parts along dimension 0
Outputs:
- output 1: bfloat16 [12, 1536, 2048], P('dp', 'cp'), parts along dimension 0
- output 2: bfloat16 [12, 1536, 2048], P('dp', 'cp'), parts along dimension 0
- output 3: float32 [4096], P('dp'), parts along dimension 0
- output 4: float32 [4096, 2048], P('dp', 'tp'), parts along dimension 0
- output 5: float32 [4096, 2048], P('dp', 'tp'), parts along dimension 0
- output 6: float32 [4096, 2048], P('dp', 'tp'), parts along dimension 0
- output 7: float32 [4096, 2048], P(('dp', 'tp')), parts along dimension 0
There are 2 independent parts. A program takes and returns all parts, laid end to end along the dimension named above; an argument that names none is the same for every part.
All inputs are finite; a program needn't handle non-finite values.
Results may differ from a plain program's by a relative error of at most 0.00969891.
Values are sent between devices in bfloat16 or wider.
A program may use at most 1 GiB of HBM per device.

v0:
```python
import jax
import jax.numpy as jnp
from jax import lax
from jax.sharding import PartitionSpec as P

HEAD_DIM = 128
ROPE_THETA = 8000000.0
LN_EPS = 1e-5
NEG_BIG = -1e30
SCALE = HEAD_DIM ** -0.5


def layer_norm(x_in, norm_gain):
    x_f32 = x_in.astype(jnp.float32)
    centred = x_f32 - jnp.mean(x_f32, axis=-1, keepdims=True)
    inv_std = lax.rsqrt(jnp.mean(centred * centred, axis=-1, keepdims=True) + LN_EPS)
    x_hat = centred * inv_std
    return x_f32, (x_hat * norm_gain).astype(jnp.bfloat16), x_hat, inv_std


def layer_norm_grad(grad_norm, x_hat, inv_std, norm_gain):
    d_hat = grad_norm * norm_gain
    return inv_std * (d_hat - jnp.mean(d_hat, axis=-1, keepdims=True) - x_hat * jnp.mean(d_hat * x_hat, axis=-1, keepdims=True))


def rope_tables(pos_ids):
    inv_freq = ROPE_THETA ** (-jnp.arange(0, HEAD_DIM, 2).astype(jnp.float32) / HEAD_DIM)
    angles = pos_ids.astype(jnp.float32)[:, :, None] * inv_freq
    return jnp.cos(angles)[:, :, None, :], jnp.sin(angles)[:, :, None, :]


def rotate(vec_in, cos_t, sin_t, sign_val):
    pair_view = vec_in.reshape(vec_in.shape[:-1] + (HEAD_DIM // 2, 2))
    even_part = pair_view[..., 0]
    odd_part = pair_view[..., 1]
    sin_s = sign_val * sin_t
    return jnp.stack([even_part * cos_t - odd_part * sin_s, even_part * sin_s + odd_part * cos_t], axis=-1).reshape(vec_in.shape)


def solution(mesh):
    cp_size = mesh.shape["cp"]

    def device_step(x_in, segment_ids, positions, w_query, w_key, w_value, w_out, norm_gain, grad_out):
        batch_rows, seq_dev = x_in.shape[0], x_in.shape[1]
        hidden = w_query.shape[1]
        head_shape = (batch_rows, seq_dev, hidden // HEAD_DIM, HEAD_DIM)
        flat_shape = (batch_rows, seq_dev, hidden)
        rank = lax.axis_index("cp")
        x_f32, normed, x_hat, inv_std = layer_norm(x_in, norm_gain)
        cos_t, sin_t = rope_tables(positions)
        q_rot = rotate(jnp.dot(normed, w_query, preferred_element_type=jnp.float32).reshape(head_shape), cos_t, sin_t, 1.0).astype(jnp.bfloat16)
        k_rot = rotate(jnp.dot(normed, w_key, preferred_element_type=jnp.float32).reshape(head_shape), cos_t, sin_t, 1.0).astype(jnp.bfloat16)
        v_val = jnp.dot(normed, w_value, preferred_element_type=jnp.float32).astype(jnp.bfloat16).reshape(head_shape)
        k_all = lax.all_gather(k_rot, "cp", axis=1, tiled=True)
        v_all = lax.all_gather(v_val, "cp", axis=1, tiled=True)
        seg_all = lax.all_gather(segment_ids, "cp", axis=1, tiled=True)
        query_index = rank * seq_dev + jnp.arange(seq_dev)
        key_index = jnp.arange(seq_dev * cp_size)
        allowed = ((key_index[None, :] <= query_index[:, None])[None] & (segment_ids[:, :, None] == seg_all[:, None, :]))[:, None]
        scores = jnp.where(allowed, jnp.einsum("bqhe,bkhe->bhqk", q_rot, k_all, preferred_element_type=jnp.float32) * SCALE, NEG_BIG)
        exp_scores = jnp.exp(scores - jnp.max(scores, axis=-1, keepdims=True))
        attn_prob = exp_scores / jnp.sum(exp_scores, axis=-1, keepdims=True)
        prob_low = attn_prob.astype(jnp.bfloat16)
        attn_out = jnp.einsum("bhqk,bkhe->bqhe", prob_low, v_all, preferred_element_type=jnp.float32).astype(jnp.bfloat16).reshape(flat_shape)
        out_sum = lax.psum(jnp.dot(attn_out, w_out, preferred_element_type=jnp.float32), "tp")
        y_out = (x_f32 + out_sum).astype(jnp.bfloat16)
        grad_heads = jnp.einsum("bsd,fd->bsf", grad_out, w_out, preferred_element_type=jnp.float32).astype(jnp.bfloat16).reshape(head_shape)
        grad_wo = lax.psum(jnp.einsum("bsf,bsd->fd", attn_out, grad_out, preferred_element_type=jnp.float32), "cp")
        grad_prob = jnp.einsum("bqhe,bkhe->bhqk", grad_heads, v_all, preferred_element_type=jnp.float32)
        grad_score = (attn_prob * (grad_prob - jnp.sum(attn_prob * grad_prob, axis=-1, keepdims=True))).astype(jnp.bfloat16)
        dq_raw = jnp.einsum("bhqk,bkhe->bqhe", grad_score, k_all, preferred_element_type=jnp.float32) * SCALE
        dk_part = (jnp.einsum("bhqk,bqhe->bkhe", grad_score, q_rot, preferred_element_type=jnp.float32) * SCALE).astype(jnp.bfloat16)
        dv_part = jnp.einsum("bhqk,bqhe->bkhe", prob_low, grad_heads, preferred_element_type=jnp.float32).astype(jnp.bfloat16)
        dk_own = lax.psum_scatter(dk_part, "cp", scatter_dimension=1, tiled=True)
        dv_own = lax.psum_scatter(dv_part, "cp", scatter_dimension=1, tiled=True)
        dq_pre = rotate(dq_raw, cos_t, sin_t, -1.0).astype(jnp.bfloat16).reshape(flat_shape)
        dk_pre = rotate(dk_own.astype(jnp.float32), cos_t, sin_t, -1.0).astype(jnp.bfloat16).reshape(flat_shape)
        dv_pre = dv_own.reshape(flat_shape)
        grad_wq = lax.psum(jnp.einsum("bsd,bsf->df", normed, dq_pre, preferred_element_type=jnp.float32), "cp")
        grad_wk = lax.psum(jnp.einsum("bsd,bsf->df", normed, dk_pre, preferred_element_type=jnp.float32), "cp")
        grad_wv = lax.psum(jnp.einsum("bsd,bsf->df", normed, dv_pre, preferred_element_type=jnp.float32), "cp")
        grad_norm = lax.psum(jnp.einsum("bsf,df->bsd", dq_pre, w_query, preferred_element_type=jnp.float32) + jnp.einsum("bsf,df->bsd", dk_pre, w_key, preferred_element_type=jnp.float32) + jnp.einsum("bsf,df->bsd", dv_pre, w_value, preferred_element_type=jnp.float32), "tp")
        grad_gain = lax.psum(jnp.sum(grad_norm * x_hat, axis=(0, 1)), "cp")
        grad_x = (grad_out.astype(jnp.float32) + layer_norm_grad(grad_norm, x_hat, inv_std, norm_gain)).astype(jnp.bfloat16)
        return y_out, grad_x, grad_gain, grad_wq, grad_wk, grad_wv, grad_wo

    in_specs = (P("dp", "cp", None), P("dp", "cp"), P("dp", "cp"), P(None, "tp"), P(None, "tp"), P(None, "tp"), P("tp", None), P(None), P("dp", "cp", None))
    out_specs = (P("dp", "cp", None), P("dp", "cp", None), P("dp"), P("dp", "tp"), P("dp", "tp"), P("dp", "tp"), P(("dp", "tp"), None))
    return jax.shard_map(device_step, mesh=mesh, in_specs=in_specs, out_specs=out_specs, check_vma=False)
```

profile of v0, /device:TPU:0, one launch (start us, length us, event | category | flops | bytes accessed | tf_op | source)
XLA Modules:
  0.0 2144.7 jit_solution(6329940746965310969)
XLA Ops:
  16.4 8.6 fusion.39
  25.0 6.7 reshape_reshape.6
  31.7 10.9 fusion.35
  42.6 6.7 reshape_reshape.7
  52.5 14.5 subtract_convert_fusion.3
  67.1 23.0 %pad_maximum_fusion = (bf16[6,384,4,64,2]{1,4,3,2,0:T(2,128)(2,1)}, bf16[6,384,4,64,2]{1,4,3,2,0:T(2,128)(2,1)S(1)}) fusion(bf16[6,384,4,64,1]{1,4,3,2,0:T(2,128)(2,1)S(1)} %get-tuple-element.23, bf16[6,384,4,64,1]{1,4,3,2,0:T(2,128)(2,1)S(1)} %get-tuple-element.22, bf16[6,384,4,64,1]{1,4,3,2,0:T(2,128)(2,1)S(1)} %get-tuple-element.28, ...), kind=kLoop, calls=%fused_computation.44 | loop fusion | flops 9437184 | bytes 9437184 | tf_op jit(solution)/shard_map/stack | solution.py:37
  94.5 5.4 copy.61
  99.9 9.6 fusion.44
  113.8 6.1 copy.58
  119.9 10.1 fusion.47
  134.3 6.9 all_gather.10
  145.4 22.1 %all-gather.5.cloned.1.call-done = bf16[6,1536,4,128]{3,1,2,0:T(8,128)(2,1)} async-done(((bf16[6,384,4,128]{3,1,2,0:T(8,128)(2,1)}), bf16[6,1536,4,128]{3,1,2,0:T(8,128)(2,1)}) %all-gather.5.cloned.1.call-update) | async-done | bytes 9437200 | tf_op jit(solution)/shard_map/all_gather | solution.py:54
  167.6 28.6 %fusion.69 = (f32[6,4,384]{2,1,0:T(4,128)S(1)}, f32[6,4,384,1536]{3,2,1,0:T(8,128)}) fusion(bf16[6,1536,4,128]{3,1,2,0:T(8,128)(2,1)} %all-gather.5.cloned.1.call-done, pred[6,384,1536]{2,1,0:T(8,128)(4,1)} %compare_and_fusion, bf16[6,384,4,128]{1,2,3,0:T(4,128)(2,1)} %bitcast.91), kind=kOutput, calls=%fused_computation.90 | convolution fusion | flops 3680503296 | bytes 71995392 | tf_op jit(solution)/shard_map/sub | solution.py:61
  196.2 38.0 %all-gather.3.cloned.1.call-done = bf16[6,1536,4,128]{1,3,2,0:T(8,128)(2,1)} async-done(((bf16[6,384,4,128]{1,3,2,0:T(8,128)(2,1)}), bf16[6,1536,4,128]{1,3,2,0:T(8,128)(2,1)}) %all-gather.3.cloned.1.call-update) | async-done | bytes 9437200 | tf_op jit(solution)/shard_map/all_gather | solution.py:55
  234.2 42.9 %multiply_reduce_fusion = (f32[6,4,384]{2,1,0:T(4,128)S(1)}, f32[6,4,384,1536]{3,2,1,0:T(8,128)}) fusion(f32[6,4,384,1536]{3,2,1,0:T(8,128)} %get-tuple-element.34, f32[6,4,384]{2,1,0:T(4,128)S(1)} %get-tuple-element.33, bf16[6,384,4,128]{1,3,2,0:T(8,128)(2,1)} %bitcast.99, bf16[6,1536,4,128]{1,3,2,0:T(8,128)(2,1)} %all-gather.3.cloned.1.call-done), kind=kOutput, calls=%fused_computation.2 | convolution fusion | flops 3666336768 | bytes 125116416 | tf_op jit(solution)/shard_map/bqhe,bkhe->bhqk/dot_general | solution.py:69
  277.1 44.9 %multiply_convert_fusion = bf16[6,4,384,1536]{3,2,1,0:T(8,128)(2,1)} fusion(f32[6,4,384,1536]{3,2,1,0:T(8,128)} %get-tuple-element.36, f32[6,4,384]{2,1,0:T(4,128)S(1)} %get-tuple-element.35, f32[6,4,384,1536]{3,2,1,0:T(8,128)} %get-tuple-element.34, f32[6,4,384]{2,1,0:T(4,128)S(1)} %get-tuple-element.33), kind=kLoop, calls=%fused_computation.1 | loop fusion | flops 56623104 | bytes 141631488 | tf_op jit(solution)/shard_map/convert_element_type | solution.py:70
  321.9 15.2 fusion.26
  337.2 15.3 copy.93
  352.5 15.9 reshape.129
  368.6 23.8 %convert_bitcast_fusion = bf16[6,1536,4,128]{1,3,2,0:T(8,128)(2,1)} fusion(bf16[6,384,4,128]{1,3,2,0:T(8,128)(2,1)} %bitcast.100, f32[6,4,384,1536]{3,2,1,0:T(8,128)} %get-tuple-element.34, f32[6,4,384]{2,1,0:T(4,128)S(1)} %get-tuple-element.33), kind=kOutput, calls=%fused_computation.38 | convolution fusion | flops 3656908800 | bytes 68456448 | tf_op jit(solution)/shard_map/bhqk,bqhe->bkhe/dot_general | solution.py:73
  392.4 15.4 copy.95
  407.9 15.9 reshape.131
  423.9 17.8 multiply_bitcast_fusion
  441.7 6.7 reshape.115
  448.4 23.8 %fusion.50 = bf16[6,4,128,384]{3,2,1,0:T(8,128)(2,1)} fusion(bf16[6,1536,4,128]{1,3,2,0:T(8,128)(2,1)} %all-gather.3.cloned.1.call-done, f32[6,4,384,1536]{3,2,1,0:T(8,128)} %get-tuple-element.34, f32[6,4,384]{2,1,0:T(4,128)S(1)} %get-tuple-element.33), kind=kOutput, calls=%fused_computation.74 | convolution fusion | flops 3653369856 | bytes 68456448 | tf_op jit(solution)/shard_map/bhqk,bkhe->bqhe/dot_general | solution.py:64
  472.1 10.6 fusion.31
  482.8 5.5 reshape.130
  488.2 5.3 copy.94
  493.6 6.3 reshape.120
  499.9 15.3 subtract_convert_fusion
  515.2 6.7 pad_maximum_fusion.3
  521.9 6.5 convert_element_type.91
  528.5 9.7 pad_maximum_fusion.2
  538.2 6.1 convert_element_type.88
  544.3 5.5 reshape.132
  549.8 5.3 copy.96
  555.1 11.2 fusion.33
  566.4 9.3 fusion.37
  575.7 21.1 add_add_fusion
  596.9 9.8 convolution_bitcast_fusion
  606.7 11.8 convolution_bitcast_fusion.2
  618.5 8.4 convolution_bitcast_fusion.3
  626.9 8.6 convolution_bitcast_fusion.1
  635.6 1197.3 %all-reduce.7.cloned.1.call-done = (f32[6,384,2048]{2,1,0:T(8,128)}, f32[6,384,2048]{2,1,0:T(8,128)}) async-done(((f32[6,384,2048]{2,1,0:T(8,128)}, f32[6,384,2048]{2,1,0:T(8,128)}), (f32[6,384,2048]{2,1,0:T(8,128)}, f32[6,384,2048]{2,1,0:T(8,128)})) %all-reduce.7.cloned.1.call-update) | async-done | bytes 37748752 | tf_op jit(solution)/shard_map/psum | solution.py:65
  1832.9 12.6 fusion.19
  1845.5 7.7 psum.51
  1853.2 25.0 %fusion.18 = (bf16[6,384,2048]{2,1,0:T(8,128)(2,1)}, bf16[6,384,2048]{2,1,0:T(8,128)(2,1)}) fusion(bf16[6,384,2048]{2,1,0:T(8,128)(2,1)} %param.9, bf16[6,384,2048]{2,1,0:T(8,128)(2,1)} %param.17, f32[6,384,2048]{2,1,0:T(8,128)} %get-tuple-element.15, f32[6,384]{1,0:T(8,128)S(1)} %broadcast_multiply_fusion.1, f32[6,384]{1,0:T(8,128)S(1)} %broadcast_multiply_fusion.2, ...), kind=kLoop, calls=%fused_computation.25 | loop fusion | flops 61341696 | bytes 75542528 | tf_op jit(solution)/shard_map/convert_element_type | solution.py:84
  1878.2 245.2 %all-reduce.5.cloned.1.call-done = (f32[2048,512]{1,0:T(8,128)}, f32[2048,512]{1,0:T(8,128)}, f32[2048,512]{1,0:T(8,128)}, f32[512,2048]{1,0:T(8,128)}) async-done(((f32[2048,512]{1,0:T(8,128)}, f32[2048,512]{1,0:T(8,128)}, f32[2048,512]{1,0:T(8,128)}, f32[512,2048]{1,0:T(8,128)}), (f32[2048,512]{1,0:T(8,128)}, f32[2048,512]{1,0:T(8,128)}, f32[2048,512]{1,0:T(8,128)}, ...) | async-done | bytes 16777232 | tf_op jit(solution)/shard_map/psum | solution.py:79
  (88 shorter events, 44.4 us)
Async XLA Ops:
  7.2 112.8 %copy-start = (bf16[512,2048]{1,0:T(8,128)(2,1)S(1)}, bf16[512,2048]{1,0:T(8,128)(2,1)}, u32[]{:S(2)}) copy-start(bf16[512,2048]{1,0:T(8,128)(2,1)} %param.15) | copy-start | bytes 6291460
  7.2 160.4 %all-gather.5.cloned.1.call-start = ((), (), s32[]{:S(2)}) async-start(), calls=%async_computation.3 | async-start | bytes 11796480 | tf_op jit(solution)/shard_map/all_gather | solution.py:54
  7.2 6.5 copy-start.1
  13.7 86.1 %copy-start.14 = (f32[6,384]{1,0:T(8,128)}, f32[6,384]{1,0:T(8,128)S(1)}, u32[]{:S(2)}) copy-start(f32[6,384]{1,0:T(8,128)S(1)} %broadcast_multiply_fusion.3) | copy-start | bytes 27652
  13.7 2.6 copy-start.19
  13.8 2.7 copy-start.22
  16.4 83.5 %copy-start.16 = (f32[6,384]{1,0:T(8,128)}, f32[6,384]{1,0:T(8,128)S(1)}, u32[]{:S(2)}) copy-start(f32[6,384]{1,0:T(8,128)S(1)} %add_rsqrt_fusion) | copy-start | bytes 27652
  42.6 6.7 copy-start.21
  52.5 14.5 copy-start.4
  99.8 134.3 %all-gather.3.cloned.1.call-start = ((), (), s32[]{:S(2)}) async-start(), calls=%async_computation.2 | async-start | bytes 11796480 | tf_op jit(solution)/shard_map/all_gather | solution.py:55
  113.8 369.0 %reduce-scatter.7.cloned.1.call-start = ((), (), s32[]{:S(2)}) async-start(), calls=%async_computation.4 | async-start | bytes 11796480
  130.0 4.3 copy-start.18
  368.4 175.9 %reduce-scatter.9.cloned.1.call-start = ((), (), s32[]{:S(2)}) async-start(), calls=%async_computation.5 | async-start | bytes 11796480
  423.8 1409.1 %all-reduce.7.cloned.1.call-start = ((), (), s32[]{:S(2)}) async-start(), calls=%async_computation.7 | async-start | bytes 75497472 | tf_op jit(solution)/shard_map/psum | solution.py:65
  493.6 6.3 copy-start.5
  493.6 6.3 copy-start.9
  555.1 11.2 copy-start.11
  555.1 11.2 copy-start.23
  566.4 9.3 copy-start.2
  566.4 9.3 copy-start.13
  596.8 9.9 copy-start.15
  596.8 9.9 copy-start.17
  596.8 9.9 copy-start.20
  596.8 1526.6 %all-reduce.5.cloned.1.call-start = ((), (), s32[]{:S(2)}) async-start(), calls=%async_computation.6 | async-start | bytes 33554432 | tf_op jit(solution)/shard_map/psum | solution.py:79
  596.9 9.8 copy-start.10
  596.9 21.6 %slice-start = ((s8[9437184]{0:T(1024)(128)(4,1)}), s8[4194304]{0:T(1024)(128)(4,1)S(1)}, s32[]{:S(2)}) async-start(s8[9437184]{0:T(1024)(128)(4,1)} %bitcast.87), calls=%async_computation.8 | async-start | bytes 8388608
  606.7 11.8 slice-start.1
  606.7 11.8 slice-start.2
  606.7 11.8 copy-start.12
  618.5 8.4 copy-start.3
  2123.4 4.8 copy-start.8
  2128.2 3.7 copy-start.7
  2131.9 3.7 copy-start.6
Sparse Core Ops, SparseCore 0:
  100.0 67.5 all-gather.4
  169.7 64.4 all-gather.2
  368.5 77.0 reduce-scatter.6
  448.7 77.0 reduce-scatter.8
  596.9 1235.9 all-reduce.6
  1836.1 287.2 all-reduce.4
where the time goes:
time: 2150 us; the launch traced here: 2140 us
  waiting for transfers between devices  1500 us (70%)
  matrix products  282 us (13%)
  other arithmetic  167 us (8%)
  local copies, waits for them, and re-layouts  163 us (8%)
    psum x1, waiting for transfers between devices, device_step(): lax.psum(jnp.dot(attn_out, w_out, preferred_element_type=jnp.float32), 'tp')  1200 us
    psum x1, waiting for transfers between devices, device_step(): lax.psum(jnp.einsum('bsd,bsf->df', normed, dq_pre, preferred_element_type...  245 us
    unnamed x66, local copies, waits for them, and re-layouts  99.9 us
    convert_element_type x1, other arithmetic, device_step(): (attn_prob * (grad_prob - jnp.sum(attn_prob * grad_prob, axis=-1, keepdim...  44.9 us
  transfers between devices with their start and end apart: 6, of which 4 were waited for; matrix products, arithmetic and copies ran while one was open for 15% of the time, Pallas kernels for 0%

commit v1 on v0

v1 whole, which is shorter than its diff:
```python
import functools
import math

import jax
import jax.numpy as jnp
from jax import lax
from jax.experimental import pallas as pl
from jax.experimental.pallas import tpu as pltpu
from jax.sharding import PartitionSpec as P

HEAD_DIM = 128
ROPE_THETA = 8000000.0
LN_EPS = 1e-5
NEG_BIG = -1e30
SCALE = HEAD_DIM ** -0.5
EXP2_SCALE = SCALE * math.log2(math.e)
F32 = jnp.float32
BF16 = jnp.bfloat16
NT = (((1,), (1,)), ((), ()))


def dot_nn(a, b):
    return jnp.dot(a, b, preferred_element_type=F32)


def dot_nt(a, b):
    return lax.dot_general(a, b, NT, preferred_element_type=F32)


def dot_tn(a, b):
    return lax.dot_general(a, b, (((0,), (0,)), ((), ())), preferred_element_type=F32)


def swap_pairs(t, sign):
    lane = lax.broadcasted_iota(jnp.int32, t.shape, 1)
    even = (lane % 2) == 0
    up = pltpu.roll(t, HEAD_DIM - 1, 1)
    down = pltpu.roll(t, 1, 1)
    return jnp.where(even, -up, down) if sign > 0 else jnp.where(even, up, -down)


def rope(t, cos_t, sin_t, sign):
    return t * cos_t + swap_pairs(t, sign) * sin_t


def proj_kernel(x_ref, dy_ref, cos_ref, sin_ref, gain_ref, wq_ref, wk_ref, wv_ref, wo_ref, n_ref, q_ref, kv_ref, do_ref):
    x = x_ref[...].astype(F32)
    centred = x - jnp.mean(x, axis=-1, keepdims=True)
    inv_std = lax.rsqrt(jnp.mean(centred * centred, axis=-1, keepdims=True) + LN_EPS)
    normed = ((centred * inv_std) * gain_ref[...]).astype(BF16)
    n_ref[...] = normed
    cos_t = cos_ref[...]
    sin_t = sin_ref[...]

    def put_rope(dst, raw):
        for h in range(raw.shape[1] // HEAD_DIM):
            cols = slice(h * HEAD_DIM, (h + 1) * HEAD_DIM)
            dst[:, cols] = rope(raw[:, cols], cos_t, sin_t, 1.0).astype(BF16)

    put_rope(kv_ref.at[0], dot_nn(normed, wk_ref[...]))
    kv_ref[1] = dot_nn(normed, wv_ref[...]).astype(BF16)
    put_rope(q_ref, dot_nn(normed, wq_ref[...]))
    do_ref[...] = dot_nt(dy_ref[...], wo_ref[...]).astype(BF16)


def project(x, dy, cos_t, sin_t, gain, wq, wk, wv, wo, rows):
    tokens, d_model = x.shape
    hidden = wq.shape[1]
    whole = pl.BlockSpec(memory_space=pltpu.VMEM)
    tile = lambda width: pl.BlockSpec((rows, width), lambda i: (i, 0))
    return pl.pallas_call(
        proj_kernel,
        grid=(tokens // rows,),
        in_specs=[tile(d_model), tile(d_model), tile(HEAD_DIM), tile(HEAD_DIM), whole, whole, whole, whole, whole],
        out_specs=[tile(d_model), tile(hidden), pl.BlockSpec((2, rows, hidden), lambda i: (0, i, 0)), tile(hidden)],
        out_shape=[
            jax.ShapeDtypeStruct((tokens, d_model), BF16),
            jax.ShapeDtypeStruct((tokens, hidden), BF16),
            jax.ShapeDtypeStruct((2, tokens, hidden), BF16),
            jax.ShapeDtypeStruct((tokens, hidden), BF16),
        ],
        compiler_params=pltpu.CompilerParams(dimension_semantics=("arbitrary",), vmem_limit_bytes=60 << 20),
        cost_estimate=pl.CostEstimate(flops=8 * tokens * d_model * hidden, bytes_accessed=8 * tokens * d_model + 8 * d_model * hidden, transcendentals=0),
        name="project",
    )(x, dy, cos_t, sin_t, gain, wq, wk, wv, wo)


SUB = 128


def attn_kernel(info_ref, start_ref, cos_ref, sin_ref, q_ref, do_ref, kv0_ref, kv1_ref, kv2_ref, kv3_ref,
                o_ref, dq_ref, g0_ref, g1_ref, g2_ref, g3_ref, s_scr, dp_scr, m_scr, l_scr, d_scr, ot_scr, dqt_scr):
    b = pl.program_id(0)
    rank = info_ref[0]
    first = info_ref[1 + b]
    seq = q_ref.shape[0]
    kvs = (kv0_ref, kv1_ref, kv2_ref, kv3_ref)
    grads = (g0_ref, g1_ref, g2_ref, g3_ref)
    q = q_ref[...]
    do = do_ref[...]
    start = start_ref[0]
    subs = range(0, seq, SUB)

    def piece_of(slot):
        return rank ^ slot if slot else rank

    def live(slot):
        piece = piece_of(slot)
        return jnp.logical_and(piece < rank, first < (piece + 1) * seq)

    def each(body):
        body(0)
        for slot in (1, 2, 3):
            pl.when(live(slot))(functools.partial(body, slot))

    m_scr[...] = jnp.full(m_scr.shape, NEG_BIG, F32)
    l_scr[...] = jnp.zeros_like(l_scr)
    d_scr[...] = jnp.zeros_like(d_scr)
    ot_scr[...] = jnp.zeros_like(ot_scr)
    dqt_scr[...] = jnp.zeros_like(dqt_scr)

    def scores(slot):
        base = piece_of(slot) * seq
        for s in subs:
            raw = dot_nt(kvs[slot][0, s:s + SUB, :], q)
            local = lax.broadcasted_iota(jnp.int32, raw.shape, 0) + s
            allowed = (local + base) >= start
            if slot == 0:
                allowed = jnp.logical_and(allowed, local <= lax.broadcasted_iota(jnp.int32, raw.shape, 1))
            raw = jnp.where(allowed, raw, NEG_BIG)
            s_scr[slot, s:s + SUB, :] = raw
            m_scr[...] = jnp.maximum(m_scr[...], jnp.max(raw, axis=0, keepdims=True))

    each(scores)

    def exps(slot):
        for s in subs:
            e = jnp.exp2((s_scr[slot, s:s + SUB, :] - m_scr[...]) * EXP2_SCALE)
            s_scr[slot, s:s + SUB, :] = e
            l_scr[...] += jnp.sum(e, axis=0, keepdims=True)

    each(exps)
    l_scr[...] = 1.0 / l_scr[...]

    def values(slot):
        for s in subs:
            v = kvs[slot][1, s:s + SUB, :]
            prob = s_scr[slot, s:s + SUB, :] * l_scr[...]
            low = prob.astype(BF16)
            dp = dot_nt(v, do)
            s_scr[slot, s:s + SUB, :] = prob
            dp_scr[slot, s:s + SUB, :] = dp
            d_scr[...] += jnp.sum(prob * dp, axis=0, keepdims=True)
            grads[slot][1, s:s + SUB, :] = dot_nn(low, do).astype(BF16)
            ot_scr[...] += dot_nn(v.T, low)

    each(values)

    def keys(slot):
        for s in subs:
            k = kvs[slot][0, s:s + SUB, :]
            ds = (s_scr[slot, s:s + SUB, :] * (dp_scr[slot, s:s + SUB, :] - d_scr[...])).astype(BF16)
            grads[slot][0, s:s + SUB, :] = (dot_nn(ds, q) * SCALE).astype(BF16)
            dqt_scr[...] += dot_nn(k.T, ds)

    each(keys)
    for slot in (1, 2, 3):
        @pl.when(jnp.logical_not(live(slot)))
        def _(slot=slot):
            grads[slot][...] = jnp.zeros_like(grads[slot])

    o_ref[...] = ot_scr[...].T.astype(BF16)
    dq = dqt_scr[...].T * SCALE
    dq_ref[...] = rope(dq, cos_ref[...], sin_ref[...], -1.0).astype(BF16)


def attend(info, start, cos_t, sin_t, q, do, kvs, seq):
    tokens, hidden = q.shape
    batch, heads = tokens // seq, hidden // HEAD_DIM
    tile = pl.BlockSpec((seq, HEAD_DIM), lambda b, h, _: (b, h))
    table = pl.BlockSpec((seq, HEAD_DIM), lambda b, h, _: (b, 0))
    pair = pl.BlockSpec((2, seq, HEAD_DIM), lambda b, h, _: (0, b, h))
    return pl.pallas_call(
        attn_kernel,
        grid_spec=pltpu.PrefetchScalarGridSpec(
            num_scalar_prefetch=1,
            grid=(batch, heads),
            in_specs=[pl.BlockSpec((1, 1, seq), lambda b, h, _: (b, 0, 0)), table, table, tile, tile, pair, pair, pair, pair],
            out_specs=[tile, tile, pair, pair, pair, pair],
            scratch_shapes=[
                pltpu.VMEM((4, seq, seq), F32),
                pltpu.VMEM((4, seq, seq), F32),
                pltpu.VMEM((1, seq), F32),
                pltpu.VMEM((1, seq), F32),
                pltpu.VMEM((1, seq), F32),
                pltpu.VMEM((HEAD_DIM, seq), F32),
                pltpu.VMEM((HEAD_DIM, seq), F32),
            ],
        ),
        out_shape=[jax.ShapeDtypeStruct((tokens, hidden), BF16)] * 2 + [jax.ShapeDtypeStruct((2, tokens, hidden), BF16)] * 4,
        compiler_params=pltpu.CompilerParams(dimension_semantics=("arbitrary", "arbitrary"), vmem_limit_bytes=48 << 20),
        cost_estimate=pl.CostEstimate(flops=48 * tokens * seq * hidden, bytes_accessed=36 * tokens * hidden, transcendentals=4 * tokens * seq * heads),
        name="attend",
    )(info, start, cos_t, sin_t, q, do, *kvs)


def out_kernel(x_ref, o_ref, w_ref, y_ref):
    total = x_ref[...].astype(F32)
    parts = dot_nn(o_ref[0], w_ref[0])
    for t in range(1, o_ref.shape[0]):
        parts += dot_nn(o_ref[t], w_ref[t])
    y_ref[...] = (total + parts).astype(BF16)


def out_project(x, o_all, w_all, rows):
    tokens, d_model = x.shape
    tp, _, hidden = o_all.shape
    return pl.pallas_call(
        out_kernel,
        grid=(tokens // rows,),
        in_specs=[pl.BlockSpec((rows, d_model), lambda i: (i, 0)), pl.BlockSpec((tp, rows, hidden), lambda i: (0, i, 0)), pl.BlockSpec(memory_space=pltpu.VMEM)],
        out_specs=pl.BlockSpec((rows, d_model), lambda i: (i, 0)),
        out_shape=jax.ShapeDtypeStruct((tokens, d_model), BF16),
        compiler_params=pltpu.CompilerParams(dimension_semantics=("arbitrary",), vmem_limit_bytes=48 << 20),
        cost_estimate=pl.CostEstimate(flops=2 * tokens * tp * hidden * d_model, bytes_accessed=8 * tokens * d_model, transcendentals=0),
        name="out_project",
    )(x, o_all, w_all)


def dn_kernel(dq_ref, dkv_ref, wq_ref, wk_ref, wv_ref, dn_ref):
    dn = dot_nt(dq_ref[...], wq_ref[...]) + dot_nt(dkv_ref[0], wk_ref[...]) + dot_nt(dkv_ref[1], wv_ref[...])
    dn_ref[...] = dn.astype(BF16)


def norm_partial(dq, dkv, wq, wk, wv, rows):
    tokens, hidden = dq.shape
    d_model = wq.shape[0]
    whole = pl.BlockSpec(memory_space=pltpu.VMEM)
    return pl.pallas_call(
        dn_kernel,
        grid=(tokens // rows,),
        in_specs=[pl.BlockSpec((rows, hidden), lambda i: (i, 0)), pl.BlockSpec((2, rows, hidden), lambda i: (0, i, 0)), whole, whole, whole],
        out_specs=pl.BlockSpec((rows, d_model), lambda i: (i, 0)),
        out_shape=jax.ShapeDtypeStruct((tokens, d_model), BF16),
        compiler_params=pltpu.CompilerParams(dimension_semantics=("arbitrary",), vmem_limit_bytes=48 << 20),
        cost_estimate=pl.CostEstimate(flops=6 * tokens * hidden * d_model, bytes_accessed=2 * tokens * (d_model + 3 * hidden), transcendentals=0),
        name="norm_partial",
    )(dq, dkv, wq, wk, wv)


def solution(mesh):
    cp_size = mesh.shape["cp"]
    tp_size = mesh.shape["tp"]

    def device_step(x_in, segment_ids, positions, w_query, w_key, w_value, w_out, norm_gain, grad_out):
        batch, seq, d_model = x_in.shape
        hidden = w_query.shape[1]
        tokens = batch * seq
        rank = lax.axis_index("cp")
        core = rank % 2
        x = x_in.reshape(tokens, d_model)
        dy = grad_out.reshape(tokens, d_model)

        inv_freq = ROPE_THETA ** (-jnp.arange(0, HEAD_DIM, 2).astype(F32) / HEAD_DIM)
        angles = positions.reshape(tokens, 1).astype(F32) * jnp.repeat(inv_freq, 2)[None, :]
        cos_t, sin_t = jnp.cos(angles), jnp.sin(angles)
        start = (rank * seq + jnp.arange(seq, dtype=jnp.int32))[None, :] - positions
        info = jnp.concatenate([jnp.full((1,), rank, jnp.int32), start[:, 0]])

        w_all = lax.all_gather(w_out, "tp", axis=0)
        rows = min(384, tokens)
        normed, q, kv, do = project(x, dy, cos_t, sin_t, norm_gain.reshape(1, d_model), w_query, w_key, w_value, w_out, rows)

        def perm(value, pairs):
            return lax.ppermute(value, "cp", pairs)

        from_chip = perm(kv, [(0, 2), (1, 3)])
        from_partner = perm(kv, [(0, 1), (2, 3)])
        from_far = perm(from_chip, [(2, 3), (3, 2)])
        o, dq, g_own, g_partner, g_chip, g_far = attend(info, start.reshape(batch, 1, seq), cos_t, sin_t, q, do, (kv, from_partner, from_chip, from_far), seq)
        o_all = lax.all_gather(o, "tp", axis=0)

        far_sum = perm(g_far, [(2, 3), (3, 2)])
        chip_sum = (g_chip.astype(F32) + far_sum.astype(F32)).astype(BF16)
        partner_in = perm(g_partner, [(1, 0), (3, 2)])
        chip_in = perm(chip_sum, [(2, 0), (3, 1)])
        dkv_sum = (g_own.astype(F32) + partner_in.astype(F32) + chip_in.astype(F32)).astype(BF16)
        dk_f32 = dkv_sum[0].astype(F32)
        lane = lax.broadcasted_iota(jnp.int32, (tokens, hidden), 1)
        swapped = jnp.where(lane % 2 == 0, jnp.roll(dk_f32, -1, 1), -jnp.roll(dk_f32, 1, 1))
        wide = lambda t: jnp.tile(t, (1, hidden // HEAD_DIM))
        dk = (dk_f32 * wide(cos_t) + swapped * wide(sin_t)).astype(BF16)
        dkv = jnp.stack([dk, dkv_sum[1]])

        dn_part = norm_partial(dq, dkv, w_query, w_key, w_value, rows)
        dn = lax.psum_scatter(dn_part, "tp", scatter_dimension=0, tiled=True).astype(F32)
        quarter = tokens // tp_size
        here = lax.axis_index("tp") * quarter
        x_q = lax.dynamic_slice(x, (here, 0), (quarter, d_model)).astype(F32)
        dy_q = lax.dynamic_slice(dy, (here, 0), (quarter, d_model)).astype(F32)
        centred = x_q - jnp.mean(x_q, axis=-1, keepdims=True)
        inv_std = lax.rsqrt(jnp.mean(centred * centred, axis=-1, keepdims=True) + LN_EPS)
        x_hat = centred * inv_std
        d_hat = dn * norm_gain
        dx = inv_std * (d_hat - jnp.mean(d_hat, axis=-1, keepdims=True) - x_hat * jnp.mean(d_hat * x_hat, axis=-1, keepdims=True))
        grad_x_q = (dy_q + dx).astype(BF16)
        grad_x = lax.all_gather(grad_x_q, "tp", axis=0, tiled=True)
        grad_gain = lax.psum(jnp.sum(dn * x_hat, axis=0), ("tp", "cp"))

        def tn(a, b):
            return lax.dot_general(a, b, (((0,), (0,)), ((), ())), preferred_element_type=F32)

        def reduce_cp(part):
            half = part.shape[0] // 2
            away = lax.dynamic_slice(part, ((1 - core) * half, 0), (half, part.shape[1]))
            mine = lax.dynamic_slice(part, (core * half, 0), (half, part.shape[1]))
            mine = (mine + perm(away, [(0, 1), (1, 0), (2, 3), (3, 2)])).astype(BF16)
            other = perm(mine, [(0, 2), (2, 0), (1, 3), (3, 1)])
            total = mine.astype(F32) + other.astype(F32)
            rest = perm(total, [(0, 1), (1, 0), (2, 3), (3, 2)])
            return jnp.where(core == 0, jnp.concatenate([total, rest]), jnp.concatenate([rest, total]))

        grad_wo = reduce_cp(tn(o, dy))
        grad_wq = reduce_cp(tn(normed, dq))
        grad_wk = reduce_cp(tn(normed, dkv[0]))
        grad_wv = reduce_cp(tn(normed, dkv[1]))
        y_out = out_project(x, o_all, w_all, rows)
        return y_out.reshape(x_in.shape), grad_x.reshape(x_in.shape), grad_gain, grad_wq, grad_wk, grad_wv, grad_wo

    in_specs = (P("dp", "cp", None), P("dp", "cp"), P("dp", "cp"), P(None, "tp"), P(None, "tp"), P(None, "tp"), P("tp", None), P(None), P("dp", "cp", None))
    out_specs = (P("dp", "cp", None), P("dp", "cp", None), P("dp"), P("dp", "tp"), P("dp", "tp"), P("dp", "tp"), P(("dp", "tp"), None))
    return jax.shard_map(device_step, mesh=mesh, in_specs=in_specs, out_specs=out_specs, check_vma=False)
```

time: 2150 us -> 1130 us (0.53)
  waiting for transfers between devices: 1500 us -> 737 us
  matrix products: 282 us -> 40.4 us
  Pallas kernels: 0 us -> 119 us
  local copies, waits for them, and re-layouts: 163 us -> 60.4 us
  other arithmetic: 167 us -> 90.5 us
    psum x2 -> x0, waiting for transfers between devices: 1440 us -> none  [the longest x1 1200 us: device_step(): lax.psum(jnp.dot(attn_out, w_out, preferred_element_type=jnp.float32), 'tp')]
    ppermute x0 -> x18, waiting for transfers between devices: none -> 306 us  [perm(): return lax.ppermute(value, 'cp', pairs)]
    all_gather x2 -> x3, waiting for transfers between devices: 60.1 us -> 286 us  [the longest x1 167 us: device_step(): o_all = lax.all_gather(o, 'tp', axis=0)]
    dot_general x17 -> x4, matrix products: 253 us -> 40.4 us  [tn(): lax.dot_general(a, b, (((0,), (0,)), ((), ())), preferred_element_type=F32)]
    reduce_scatter x0 -> x1, waiting for transfers between devices: none -> 143 us  [device_step(): lax.psum_scatter(dn_part, 'tp', scatter_dimension=0, tiled=True).astype(F32)]
    pallas_call x0 -> x4, Pallas kernels: none -> 119 us  [the longest x1 41.7 us: attend(): pl.pallas_call(attn_kernel, grid_spec=pltpu.PrefetchScalarGridSpec(num_sc...]
    unnamed x66 -> x43, local copies, waits for them, and re-layouts: 99.9 us -> 20.5 us
    another operation x5 -> x1, other arithmetic: 69.3 us -> 2.81 us  [device_step(): dkv = jnp.stack([dk, dkv_sum[1]])]
  transfers between devices with their start and end apart: 6 -> 22, of which waited for: 4 -> 10; matrix products, arithmetic and copies ran while one was open for 15% -> 11% of each run, Pallas kernels for 0% -> 2%
where the time goes in v1:
time: 1130 us; the launch traced here: 1110 us
  waiting for transfers between devices  737 us (65%)
  Pallas kernels  119 us (11%)
  other arithmetic  90.5 us (8%)
  local copies, waits for them, and re-layouts  60.4 us (5%)
  matrix products  40.4 us (4%)
  blocking collectives  33.1 us (3%)
  starting transfers between devices  18.1 us (2%)
  between operations  14.6 us (1%)
    ppermute x18, waiting for transfers between devices, perm(): return lax.ppermute(value, 'cp', pairs)  306 us
    all_gather x1, waiting for transfers between devices, device_step(): o_all = lax.all_gather(o, 'tp', axis=0)  167 us
    reduce_scatter x1, waiting for transfers between devices, device_step(): lax.psum_scatter(dn_part, 'tp', scatter_dimension=0, tiled=True).astype(F32)  143 us
    all_gather x1, waiting for transfers between devices, device_step(): grad_x = lax.all_gather(grad_x_q, 'tp', axis=0, tiled=True)  95.9 us
    pallas_call x1, Pallas kernels, attend(): pl.pallas_call(attn_kernel, grid_spec=pltpu.PrefetchScalarGridSpec(num_sc...  41.7 us
    dot_general x4, matrix products, tn(): lax.dot_general(a, b, (((0,), (0,)), ((), ())), preferred_element_type=F32)  40.4 us
    psum x1, blocking collectives, device_step(): grad_gain = lax.psum(jnp.sum(dn * x_hat, axis=0), ('tp', 'cp'))  33.1 us
    pallas_call x1, Pallas kernels, project(): pl.pallas_call(proj_kernel, grid=(tokens // rows,), in_specs=[tile(d_mode...  31.9 us
  transfers between devices with their start and end apart: 22, of which 10 were waited for; matrix products, arithmetic and copies ran while one was open for 11% of the time, Pallas kernels for 2%

profile of v1, /device:TPU:0, one launch (start us, length us, event | category | flops | bytes accessed | tf_op | source)
XLA Modules:
  0.0 1113.2 jit_solution(6503109248284473200)
XLA Ops:
  8.3 6.2 multiply_sine_fusion
  14.5 31.9 %project.1 = (bf16[2304,2048]{1,0:T(8,128)(2,1)}, bf16[2304,512]{1,0:T(8,128)(2,1)}, bf16[2,2304,512]{2,1,0:T(8,128)(2,1)}, bf16[2304,512]{1,0:T(8,128)(2,1)}) custom-call(bf16[2304,2048]{1,0:T(8,128)(2,1)} %bitcast.50, bf16[2304,2048]{1,0:T(8,128)(2,1)} %bitcast.57, f32[2304,128]{1,0:T(8,128)} %get-tuple-element.41.cos_ref, ...), custom_call_target="tpu_custom_call" | custom-call | flops 19327352832 | bytes 46137344 | tf_op jit(solution)/shard_map/project/pallas_call | solution.py:71
  46.4 5.3 collective-permute-start.1
  53.4 99.0 %collective-permute-done.1.kv2_ref = bf16[2,2304,512]{2,1,0:T(8,128)(2,1)S(1)} collective-permute-done((bf16[2,2304,512]{2,1,0:T(8,128)(2,1)}, bf16[2,2304,512]{2,1,0:T(8,128)(2,1)S(1)}, u32[]{:S(2)}, u32[]{:S(2)}) %collective-permute-start.1) | collective-permute-done | bytes 4718624 | tf_op jit(solution)/shard_map/ppermute | solution.py:275
  153.6 2.4 copy-done.16
  157.4 41.7 %attend.1 = (bf16[2304,512]{1,0:T(8,128)(2,1)}, bf16[2304,512]{1,0:T(8,128)(2,1)}, bf16[2,2304,512]{2,1,0:T(8,128)(2,1)}, bf16[2,2304,512]{2,1,0:T(8,128)(2,1)},...) custom-call(s32[7]{0:T(128)S(1)} %pad_add_fusion.info_ref, s32[6,1,384]{2,1,0:T(1,128)S(1)} %reshape.279.start_ref, ...), custom_call_target="tpu_custom_call" | custom-call | flops 21743271936 | bytes 42467328 | tf_op jit(solution)/shard_map/attend/pallas_call | solution.py:183
  201.4 5.9 add_convert_fusion.1
  209.1 2.9 tile.22
  211.9 6.5 tile.23
  218.5 2.8 tile.24
  221.3 6.5 tile.25
  227.8 5.2 collective-permute-done.3
  233.1 159.9 %collective-permute-done.5 = bf16[2,2304,512]{2,1,0:T(8,128)(2,1)} collective-permute-done((bf16[2,2304,512]{2,1,0:T(8,128)(2,1)}, bf16[2,2304,512]{2,1,0:T(8,128)(2,1)}, u32[]{:S(2)}, u32[]{:S(2)}) %collective-permute-start.5) | collective-permute-done | bytes 4718624 | tf_op jit(solution)/shard_map/ppermute | solution.py:275
  393.0 7.1 add_convert_fusion
  400.1 3.4 convert_bitcast_fusion
  403.5 12.2 %fusion.34 = (f32[2304,511]{1,0:T(8,128)}, f32[1,2304,511]{2,1,0:T(8,128)}, f32[1,2304,511]{2,1,0:T(8,128)}, f32[2304,511]{1,0:T(8,128)}) fusion(f32[2304,512]{1,0:T(8,128)} %get-tuple-element.38), kind=kLoop, calls=%fused_computation.82 | loop fusion | bytes 28256256 | tf_op jit(solution)/shard_map/jit(_roll_static)/slice | solution.py:290
  415.6 3.7 fusion.33
  419.3 7.7 fusion.12
  427.1 2.8 pad_maximum_fusion.dkv_ref
  431.0 19.1 %norm_partial.1 = bf16[2304,2048]{1,0:T(8,128)(2,1)} custom-call(bf16[2304,512]{1,0:T(8,128)(2,1)} %get-tuple-element.21.dq_ref, bf16[2,2304,512]{2,1,0:T(8,128)(2,1)} %pad_maximum_fusion.dkv_ref, bf16[2048,512]{1,0:T(8,128)(2,1)S(1)} %copy-done.2, bf16[2048,512]{1,0:T(8,128)(2,1)S(1)} %copy-done.3, bf16[2048,512]{1,0:T(8,128)(2,1)} %wv_ref.3), custom_call_target="tpu_custom_call" | custom-call | flops 14495514624 | bytes 16515072 | tf_op jit(solution)/shard_map/norm_partial/pallas_call | solution.py:239
  451.8 2.1 convert_reduce_fusion
  453.9 2.4 fusion.10
  456.3 8.4 fusion.37
  464.7 2.0 copy-done.7
  466.9 143.5 %reduce-scatter.2.cloned.1.call-done = bf16[576,2048]{1,0:T(8,128)(2,1)} async-done(((bf16[2304,2048]{1,0:T(8,128)(2,1)}), bf16[576,2048]{1,0:T(8,128)(2,1)}) %reduce-scatter.2.cloned.1.call-update) | async-done | bytes 2359312 | tf_op jit(solution)/shard_map/reduce_scatter | solution.py:296
  610.4 4.6 fusion.14
  615.0 4.9 fusion.9
  620.0 8.4 fusion.36
  628.4 2.0 copy-done.11
  631.9 2.6 add_convert_fusion.2
  636.1 3.7 add_convert_fusion.5
  641.2 7.8 fusion.20
  652.8 15.7 %fusion.18 = f32[2048,512]{1,0:T(8,128)} fusion(bf16[2304,2048]{1,0:T(8,128)(2,1)} %get-tuple-element.26, f32[288,8,4,128]{3,2,1,0:T(4,128)} %bitcast.49, f32[288,8,4,128]{3,2,1,0:T(4,128)S(1)} %bitcast.48, f32[2304,1]{1,0:T(8,128)} %get-tuple-element.33, f32[2304,511]{1,0:T(8,128)} %get-tuple-element.37, f32[2304,511]{1,0:T(8,128)} %get-tuple-element.34, ...), kind=kOutput, calls=%fused_computation.39 | convolution fusion | flops 4844814336 | bytes 36040192 | tf_op jit(solution)/shard_map/dot_general | solution.py:311
  672.7 10.0 collective-permute-done.7
  682.7 3.2 convert_add_fusion.3
  691.2 5.0 maximum_select_fusion.5
  696.2 6.6 maximum_select_fusion.2
  702.8 11.1 collective-permute-done.13
  715.5 20.4 %collective-permute-done.10 = bf16[1024,512]{1,0:T(8,128)(2,1)} collective-permute-done((bf16[1024,512]{1,0:T(8,128)(2,1)}, bf16[1024,512]{1,0:T(8,128)(2,1)}, u32[]{:S(2)}, u32[]{:S(2)}) %collective-permute-start.10) | collective-permute-done | bytes 1048608 | tf_op jit(solution)/shard_map/ppermute | solution.py:275
  735.9 3.2 convert_add_fusion.2
  739.1 23.2 %all-gather.10.cloned.1.call-done = bf16[2048,2048]{1,0:T(8,128)(2,1)} async-done(((bf16[512,2048]{1,0:T(8,128)(2,1)}), bf16[2048,2048]{1,0:T(8,128)(2,1)}) %all-gather.10.cloned.1.call-update) | async-done | bytes 8388624 | tf_op jit(solution)/shard_map/all_gather | solution.py:270
  762.2 167.4 %all-gather.8.cloned.1.call-done = bf16[9216,512]{1,0:T(8,128)(2,1)} async-done(((bf16[2304,512]{1,0:T(8,128)(2,1)}), bf16[9216,512]{1,0:T(8,128)(2,1)}) %all-gather.8.cloned.1.call-update) | async-done | bytes 9437200 | tf_op jit(solution)/shard_map/all_gather | solution.py:281
  929.7 26.5 %out_project.1 = bf16[2304,2048]{1,0:T(8,128)(2,1)} custom-call(bf16[2304,2048]{1,0:T(8,128)(2,1)} %bitcast.55, bf16[4,2304,512]{2,1,0:T(8,128)(2,1)} %bitcast.61, bf16[4,512,2048]{2,1,0:T(8,128)(2,1)} %bitcast.62), custom_call_target="tpu_custom_call" | custom-call | flops 19327352832 | bytes 37748736 | tf_op jit(solution)/shard_map/out_project/pallas_call | solution.py:218
  956.2 5.3 maximum_select_fusion.4
  961.4 6.5 maximum_select_fusion.3
  967.9 33.1 %psum.7 = f32[2048]{0:T(1024)} all-reduce(f32[2048]{0:T(1024)S(1)} %get-tuple-element.27), channel_id=1, replica_groups=mesh['dp'=2,'tp'=4,'cp'=4] {'tp','cp'}, use_global_device_ids=true, to_apply=%region_6.7 | all-reduce | flops 2048 | bytes 16384 | tf_op jit(solution)/shard_map/psum | solution.py:308
  1001.0 95.9 %all-gather.6.cloned.1.call-done = bf16[2304,2048]{1,0:T(8,128)(2,1)} async-done(((bf16[576,2048]{1,0:T(8,128)(2,1)}), bf16[2304,2048]{1,0:T(8,128)(2,1)}) %all-gather.6.cloned.1.call-update) | async-done | bytes 9437200 | tf_op jit(solution)/shard_map/all_gather | solution.py:307
  1096.9 9.4 copy.22
  (101 shorter events, 31.7 us)
Async XLA Ops:
  7.2 603.2 %reduce-scatter.2.cloned.1.call-start = ((), (), s32[]{:S(2)}) async-start(), calls=%async_computation.1 | async-start | bytes 11796480 | tf_op jit(solution)/shard_map/reduce_scatter | solution.py:296
  14.5 143.0 %copy-start = (f32[2304,128]{1,0:T(8,128)S(1)}, f32[2304,128]{1,0:T(8,128)}, u32[]{:S(2)}) copy-start(f32[2304,128]{1,0:T(8,128)} %get-tuple-element.40.sin_ref) | copy-start | bytes 3538948
  14.5 143.0 %copy-start.1 = (f32[2304,128]{1,0:T(8,128)S(1)}, f32[2304,128]{1,0:T(8,128)}, u32[]{:S(2)}) copy-start(f32[2304,128]{1,0:T(8,128)} %get-tuple-element.41.cos_ref) | copy-start | bytes 3538948
  46.4 106.0 %collective-permute-start.1 = (bf16[2,2304,512]{2,1,0:T(8,128)(2,1)}, bf16[2,2304,512]{2,1,0:T(8,128)(2,1)S(1)}, u32[]{:S(2)}, u32[]{:S(2)}) collective-permute-start(bf16[2,2304,512]{2,1,0:T(8,128)(2,1)} %get-tuple-element.19.kv0_ref), channel_id=1, source_target_pairs={{0,2},{1,3},{4,6},{5,7},{8,10},{9,11},{12,14},{13,15},{16,18},{17,... | collective-permute-start | bytes 14155784 | tf_op jit(solution)/shard_map/ppermute | solution.py:275
  51.7 101.9 %collective-permute-start = (bf16[2,2304,512]{2,1,0:T(8,128)(2,1)}, bf16[2,2304,512]{2,1,0:T(8,128)(2,1)S(1)}, u32[]{:S(2)}, u32[]{:S(2)}) collective-permute-start(bf16[2,2304,512]{2,1,0:T(8,128)(2,1)} %get-tuple-element.19.kv0_ref), channel_id=1, source_target_pairs={{0,1},{2,3},{4,5},{6,7},{8,9},{10,11},{12,13},{14,15},{16,17},{18,... | collective-permute-start | bytes 14155784 | tf_op jit(solution)/shard_map/ppermute | solution.py:275
  152.4 3.6 copy-start.14
  152.4 1.2 collective-permute-start.2
  153.6 3.8 copy-start.15
  153.6 2.4 copy-start.16
  199.2 2.3 collective-permute-start.4
  200.1 33.0 %collective-permute-start.3 = (bf16[2,2304,512]{2,1,0:T(8,128)(2,1)}, bf16[2,2304,512]{2,1,0:T(8,128)(2,1)}, u32[]{:S(2)}, u32[]{:S(2)}) collective-permute-start(bf16[2,2304,512]{2,1,0:T(8,128)(2,1)} %get-tuple-element.23), channel_id=1, source_target_pairs={{1,0},{3,2},{5,4},{7,6},{9,8},{11,10},{13,12},{15,14},{17,16},{19,... | collective-permute-start | bytes 14155784 | tf_op jit(solution)/shard_map/ppermute | solution.py:275
  207.3 185.7 %collective-permute-start.5 = (bf16[2,2304,512]{2,1,0:T(8,128)(2,1)}, bf16[2,2304,512]{2,1,0:T(8,128)(2,1)}, u32[]{:S(2)}, u32[]{:S(2)}) collective-permute-start(bf16[2,2304,512]{2,1,0:T(8,128)(2,1)} %add_convert_fusion.1), channel_id=1, source_target_pairs={{2,0},{3,1},{6,4},{7,5},{10,8},{11,9},{14,12},{15,13},{18,16},{19,... | collective-permute-start | bytes 14155784 | tf_op jit(solution)/shard_map/ppermute | solution.py:275
  400.1 3.4 copy-start.4
  415.6 3.7 copy-start.5
  427.0 2.8 copy-start.2
  427.0 3.9 copy-start.3
  450.1 312.2 %all-gather.10.cloned.1.call-start = ((), (), s32[]{:S(2)}) async-start(), calls=%async_computation.4 | async-start | bytes 10485760 | tf_op jit(solution)/shard_map/all_gather | solution.py:270
  450.8 478.8 %all-gather.8.cloned.1.call-start = ((), (), s32[]{:S(2)}) async-start(), calls=%async_computation.3 | async-start | bytes 11796480 | tf_op jit(solution)/shard_map/all_gather | solution.py:281
  451.6 645.3 %all-gather.6.cloned.1.call-start = ((), (), s32[]{:S(2)}) async-start(), calls=%async_computation.2 | async-start | bytes 11796480 | tf_op jit(solution)/shard_map/all_gather | solution.py:307
  464.7 2.0 copy-start.7
  466.7 143.7 %copy-start.13 = (f32[2048]{0:T(1024)S(1)}, f32[2048]{0:T(1024)}, u32[]{:S(2)}) copy-start(f32[2048]{0:T(1024)} %param.15) | copy-start | bytes 24580
  466.9 165.1 %collective-permute-start.15 = (f32[256,2048]{1,0:T(8,128)S(1)}, f32[256,2048]{1,0:T(8,128)}, u32[]{:S(2)}, u32[]{:S(2)}) collective-permute-start(f32[256,2048]{1,0:T(8,128)S(1)} %constant_dynamic-slice_fusion), channel_id=1, source_target_pairs={{0,1},{1,0},{2,3},{3,2},{4,5},{5,4},{6,7},{7,6},{8,9},{9,8},{10,11... | collective-permute-start | bytes 6291464 | tf_op jit(solution)/shard_map/ppermute | solution.py:275
  610.4 4.6 copy-start.6
  628.4 2.0 copy-start.11
  631.9 4.2 collective-permute-start.6
  631.9 9.3 slice-start
  631.9 9.3 slice-start.1
  634.6 36.1 %collective-permute-start.16 = (bf16[256,2048]{1,0:T(8,128)(2,1)S(1)}, bf16[256,2048]{1,0:T(8,128)(2,1)}, u32[]{:S(2)}, u32[]{:S(2)}) collective-permute-start(bf16[256,2048]{1,0:T(8,128)(2,1)S(1)} %add_convert_fusion.2), channel_id=1, source_target_pairs={{0,2},{2,0},{1,3},{3,1},{4,6},{6,4},{5,7},{7,5},{8,10},{10,8},{9,1... | collective-permute-start | bytes 3145736 | tf_op jit(solution)/shard_map/ppermute | solution.py:275
  636.1 16.5 %slice-start.2 = ((s8[4718592]{0:T(1024)(128)(4,1)}), s8[4194304]{0:T(1024)(128)(4,1)S(1)}, s32[]{:S(2)}) async-start(s8[4718592]{0:T(1024)(128)(4,1)} %bitcast.46), calls=%async_computation.7 | async-start | bytes 8388608
  639.8 12.8 %slice-start.3 = ((s8[4718592]{0:T(1024)(128)(4,1)}), s8[524288]{0:T(1024)(128)(4,1)S(1)}, s32[]{:S(2)}) async-start(s8[4718592]{0:T(1024)(128)(4,1)} %bitcast.46), calls=%async_computation.8 | async-start | bytes 1048576
  639.8 42.8 %collective-permute-start.7 = (bf16[1024,512]{1,0:T(8,128)(2,1)}, bf16[1024,512]{1,0:T(8,128)(2,1)}, u32[]{:S(2)}, u32[]{:S(2)}) collective-permute-start(bf16[1024,512]{1,0:T(8,128)(2,1)} %add_convert_fusion.5), channel_id=1, source_target_pairs={{0,2},{2,0},{1,3},{3,1},{4,6},{6,4},{5,7},{7,5},{8,10},{10,8},{9,1... | collective-permute-start | bytes 3145736 | tf_op jit(solution)/shard_map/ppermute | solution.py:275
  649.1 2.0 copy-start.9
  651.1 1.7 copy-start.12
  652.6 33.3 %collective-permute-start.12 = (f32[1024,512]{1,0:T(8,128)}, f32[1024,512]{1,0:T(8,128)}, u32[]{:S(2)}, u32[]{:S(2)}) collective-permute-start(f32[1024,512]{1,0:T(8,128)} %constant_dynamic-slice_fusion.1), channel_id=1, source_target_pairs={{0,1},{1,0},{2,3},{3,2},{4,5},{5,4},{6,7},{7,6},{8,9},{9,8},{10,11... | collective-permute-start | bytes 6291464 | tf_op jit(solution)/shard_map/ppermute | solution.py:275
  670.3 15.6 %copy-start.10 = (f32[2048,512]{1,0:T(8,128)S(1)}, f32[2048,512]{1,0:T(8,128)}, u32[]{:S(2)}) copy-start(f32[2048,512]{1,0:T(8,128)} %copy-done.9) | copy-start | bytes 12582916
  670.3 19.1 %collective-permute-start.9 = (f32[1024,512]{1,0:T(8,128)S(1)}, f32[1024,512]{1,0:T(8,128)S(1)}, u32[]{:S(2)}, u32[]{:S(2)}) collective-permute-start(f32[1024,512]{1,0:T(8,128)S(1)} %constant_dynamic-slice_fusion.2), channel_id=1, source_target_pairs={{0,1},{1,0},{2,3},{3,2},{4,5},{5,4},{6,7},{7,6},{8,9},{9,8},{10,11... | collective-permute-start | bytes 6291464 | tf_op jit(solution)/shard_map/ppermute | solution.py:275
  672.5 16.9 %copy-start.8 = (f32[2048,512]{1,0:T(8,128)S(1)}, f32[2048,512]{1,0:T(8,128)}, u32[]{:S(2)}) copy-start(f32[2048,512]{1,0:T(8,128)} %fusion.18) | copy-start | bytes 12582916
  672.5 18.7 %collective-permute-start.17 = (f32[256,2048]{1,0:T(8,128)S(1)}, f32[256,2048]{1,0:T(8,128)}, u32[]{:S(2)}, u32[]{:S(2)}) collective-permute-start(f32[256,2048]{1,0:T(8,128)S(1)} %convert_add_fusion), channel_id=1, source_target_pairs={{0,1},{1,0},{2,3},{3,2},{4,5},{5,4},{6,7},{7,6},{8,9},{9,8},{10,11... | collective-permute-start | bytes 6291464 | tf_op jit(solution)/shard_map/ppermute | solution.py:275
  685.8 10.4 collective-permute-start.8
  687.8 26.1 %collective-permute-start.13 = (bf16[1024,512]{1,0:T(8,128)(2,1)S(1)}, bf16[1024,512]{1,0:T(8,128)(2,1)}, u32[]{:S(2)}, u32[]{:S(2)}) collective-permute-start(bf16[1024,512]{1,0:T(8,128)(2,1)S(1)} %add_convert_fusion.3), channel_id=1, source_target_pairs={{0,2},{2,0},{1,3},{3,1},{4,6},{6,4},{5,7},{7,5},{8,10},{10,8},{9,1... | collective-permute-start | bytes 3145736 | tf_op jit(solution)/shard_map/ppermute | solution.py:275
  690.7 45.2 %collective-permute-start.10 = (bf16[1024,512]{1,0:T(8,128)(2,1)}, bf16[1024,512]{1,0:T(8,128)(2,1)}, u32[]{:S(2)}, u32[]{:S(2)}) collective-permute-start(bf16[1024,512]{1,0:T(8,128)(2,1)} %add_convert_fusion.4), channel_id=1, source_target_pairs={{0,2},{2,0},{1,3},{3,1},{4,6},{6,4},{5,7},{7,5},{8,10},{10,8},{9,1... | collective-permute-start | bytes 3145736 | tf_op jit(solution)/shard_map/ppermute | solution.py:275
  715.4 240.7 %collective-permute-start.14 = (f32[1024,512]{1,0:T(8,128)S(1)}, f32[1024,512]{1,0:T(8,128)}, u32[]{:S(2)}, u32[]{:S(2)}) collective-permute-start(f32[1024,512]{1,0:T(8,128)S(1)} %convert_add_fusion.1), channel_id=1, source_target_pairs={{0,1},{1,0},{2,3},{3,2},{4,5},{5,4},{6,7},{7,6},{8,9},{9,8},{10,11... | collective-permute-start | bytes 6291464 | tf_op jit(solution)/shard_map/ppermute | solution.py:275
  739.1 222.3 %collective-permute-start.11 = (f32[1024,512]{1,0:T(8,128)}, f32[1024,512]{1,0:T(8,128)}, u32[]{:S(2)}, u32[]{:S(2)}) collective-permute-start(f32[1024,512]{1,0:T(8,128)} %convert_add_fusion.2), channel_id=1, source_target_pairs={{0,1},{1,0},{2,3},{3,2},{4,5},{5,4},{6,7},{7,6},{8,9},{9,8},{10,11... | collective-permute-start | bytes 6291464 | tf_op jit(solution)/shard_map/ppermute | solution.py:275
Sparse Core Ops, SparseCore 0:
  450.2 160.1 reduce-scatter.1
  612.0 150.2 all-gather.9
  764.4 165.2 all-gather.7
  931.1 165.7 all-gather.5

commit v2 on v1

--- a/solution.py
+++ b/solution.py
@@ -86,6 +86,7 @@
 
 
 SUB = 128
+ROWS = 48
 
 
 def attn_kernel(info_ref, start_ref, cos_ref, sin_ref, q_ref, do_ref, kv0_ref, kv1_ref, kv2_ref, kv3_ref,
@@ -204,48 +205,328 @@
     )(info, start, cos_t, sin_t, q, do, *kvs)
 
 
-def out_kernel(x_ref, o_ref, w_ref, y_ref):
-    total = x_ref[...].astype(F32)
-    parts = dot_nn(o_ref[0], w_ref[0])
-    for t in range(1, o_ref.shape[0]):
-        parts += dot_nn(o_ref[t], w_ref[t])
-    y_ref[...] = (total + parts).astype(BF16)
-
-
-def out_project(x, o_all, w_all, rows):
-    tokens, d_model = x.shape
-    tp, _, hidden = o_all.shape
+MESH = pl.DeviceIdType.MESH
+
+
+def back_kernel(groups, rows, tp, cp, dq_hbm, dkv_hbm, x_hbm, dy_hbm, o_hbm, wq_ref, wk_ref, wv_ref, wo_ref, gain_ref,
+                gx_hbm, y_hbm, gg_ref, part, rs_r, rs_l, send_r, send_l, tot, gx_buf, dq_in, dkv_in, o_in, x_in, dy_in, y_buf, gain_all,
+                in_sem, y_sem, own_sem, rss_r, rss_l, rsr_r, rsr_l, ag0_r, ag0_l, agf_r, agf_l, agr_r, agr_l, gs_sem, gr_sem):
+    z = lax.axis_index("tp")
+    r = lax.axis_index("cp")
+    last = tp - 1
+    slots = tp - 1
+    span = tp * rows
+    d_model = x_hbm.shape[1]
+    chunk = min(512, d_model)
+
+    barrier = pltpu.get_barrier_semaphore()
+    peers = [(dt, dc) for dt in range(tp) for dc in range(cp) if dt or dc]
+    for dt, dc in peers:
+        pl.semaphore_signal(barrier, inc=1, device_id={"tp": lax.rem(z + dt, tp), "cp": lax.rem(r + dc, cp)}, device_id_type=MESH)
+    pl.semaphore_wait(barrier, len(peers))
+
+    def remote(src, dst, ssem, rsem, dev):
+        return pltpu.make_async_remote_copy(src_ref=src, dst_ref=dst, send_sem=ssem, recv_sem=rsem, device_id=dev, device_id_type=MESH)
+
+    def move(dir_right):
+        return {"tp": jnp.where(z < last, z + 1, z)} if dir_right else {"tp": jnp.where(z > 0, z - 1, z)}
+
+    right, left = move(True), move(False)
+
+    def group_rows(i):
+        return pl.ds(pl.multiple_of(i * span, span), span)
+
+    def tile_rows(i, owner):
+        return pl.ds(pl.multiple_of(i * span + owner * rows, rows), rows)
+
+    def inputs(i, slot):
+        g = group_rows(i)
+        return [
+            pltpu.make_async_copy(dq_hbm.at[g, :], dq_in.at[slot], in_sem.at[slot, 0]),
+            pltpu.make_async_copy(dkv_hbm.at[:, g, :], dkv_in.at[slot], in_sem.at[slot, 1]),
+            pltpu.make_async_copy(o_hbm.at[:, g, :], o_in.at[slot], in_sem.at[slot, 2]),
+            pltpu.make_async_copy(x_hbm.at[g, :], x_in.at[slot], in_sem.at[slot, 3]),
+            pltpu.make_async_copy(dy_hbm.at[tile_rows(i, z), :], dy_in.at[slot], in_sem.at[slot, 4]),
+        ]
+
+    def y_copy(i, slot):
+        return pltpu.make_async_copy(y_buf.at[slot], y_hbm.at[group_rows(i), :], y_sem.at[slot])
+
+    def rs_copy(i, s, to_right):
+        if to_right:
+            return remote(send_r.at[s], rs_r.at[i, s], rss_r.at[s], rsr_r.at[i, s], right)
+        return remote(send_l.at[s], rs_l.at[i, s], rss_l.at[s], rsr_l.at[i, s], left)
+
+    def rs_send(i, cur, s):
+        for to_right in (True, False):
+            far = z if to_right else last - z
+            owner = (z + slots - s) if to_right else (z - slots + s)
+            buf, held = (send_r, rs_r) if to_right else (send_l, rs_l)
+
+            @pl.when(jnp.logical_and(i < groups, jnp.logical_and(far <= s, far < last)))
+            def _(to_right=to_right, far=far, owner=owner, buf=buf, held=held):
+                @pl.when(i > 0)
+                def _():
+                    rs_copy(i - 1, s, to_right).wait_send()
+
+                mine = pl.ds(pl.multiple_of(owner * rows, rows), rows)
+                if s == 0:
+                    buf[s] = part[cur, mine, :].astype(BF16)
+                else:
+                    @pl.when(far == 0)
+                    def _():
+                        buf[s] = part[cur, mine, :].astype(BF16)
+
+                    @pl.when(far > 0)
+                    def _():
+                        rs_copy(i, s - 1, to_right).wait_recv()
+                        buf[s] = (part[cur, mine, :] + held[i, s - 1].astype(F32)).astype(BF16)
+
+                rs_copy(i, s, to_right).start()
+
+    def ag_own(i, slot, to_right):
+        src = gx_buf.at[slot]
+        dst = gx_hbm.at[tile_rows(i, z), :]
+        if to_right:
+            return remote(src, dst, ag0_r.at[slot], agr_r.at[i, 0], right)
+        return remote(src, dst, ag0_l.at[slot], agr_l.at[i, 0], left)
+
+    def own_copy(i, slot):
+        return pltpu.make_async_copy(gx_buf.at[slot], gx_hbm.at[tile_rows(i, z), :], own_sem.at[slot])
+
+    def ag_forward(i, a, to_right):
+        owner = z - a if to_right else z + a
+        tile = gx_hbm.at[tile_rows(i, owner), :]
+        if to_right:
+            return remote(tile, tile, agf_r.at[a], agr_r.at[i, a], right)
+        return remote(tile, tile, agf_l.at[a], agr_l.at[i, a], left)
+
+    def ag_wait(i, a, to_right):
+        tile = gx_hbm.at[tile_rows(i, 0), :]
+        sem = agr_r.at[i, a] if to_right else agr_l.at[i, a]
+        remote(tile, tile, agf_r.at[a], sem, right).wait_recv()
+
+    def ag_step(i, a):
+        for to_right in (True, False):
+            far = z if to_right else last - z
+
+            @pl.when(jnp.logical_and(jnp.logical_and(i >= 0, i < groups), far >= a))
+            def _(to_right=to_right, far=far):
+                ag_wait(i, a - 1, to_right)
+                if a < slots:
+                    @pl.when(far < last)
+                    def _():
+                        @pl.when(i > 0)
+                        def _():
+                            ag_forward(i - 1, a, to_right).wait_send()
+
+                        ag_forward(i, a, to_right).start()
+
+    def ag_first(i, slot):
+        own_copy(i, slot).start()
+        for to_right in (True, False):
+            far = z if to_right else last - z
+
+            @pl.when(far < last)
+            def _(to_right=to_right):
+                ag_own(i, slot, to_right).start()
+
+    def ag_first_done(i, slot):
+        own_copy(i, slot).wait()
+        for to_right in (True, False):
+            far = z if to_right else last - z
+
+            @pl.when(far < last)
+            def _(to_right=to_right):
+                ag_own(i, slot, to_right).wait_send()
+
+    def partial_norm(cur):
+        for c in range(0, d_model, chunk):
+            cols = slice(c, c + chunk)
+            part[cur, :, cols] = (
+                dot_nt(dq_in[cur], wq_ref[cols, :]) + dot_nt(dkv_in[cur, 0], wk_ref[cols, :]) + dot_nt(dkv_in[cur, 1], wv_ref[cols, :])
+            )
+
+    def project_out(cur, lo, hi):
+        for c in range(lo, hi, chunk):
+            cols = slice(c, c + chunk)
+            acc = dot_nn(o_in[cur, 0], wo_ref[0, :, cols])
+            for t in range(1, tp):
+                acc += dot_nn(o_in[cur, t], wo_ref[t, :, cols])
+            y_buf[cur, :, cols] = (x_in[cur, :, cols].astype(F32) + acc).astype(BF16)
+
+    def finalize(i, slot):
+        mine = pl.ds(pl.multiple_of(z * rows, rows), rows)
+        tot[...] = part[slot, mine, :]
+
+        @pl.when(z > 0)
+        def _():
+            rs_copy(i, slots - 1, True).wait_recv()
+            tot[...] += rs_r[i, slots - 1].astype(F32)
+
+        @pl.when(z < last)
+        def _():
+            rs_copy(i, slots - 1, False).wait_recv()
+            tot[...] += rs_l[i, slots - 1].astype(F32)
+
+        @pl.when(i > 1)
+        def _():
+            ag_first_done(i - 2, slot)
+
+        x = x_in[slot, mine, :].astype(F32)
+        centred = x - jnp.mean(x, axis=-1, keepdims=True)
+        inv_std = lax.rsqrt(jnp.mean(centred * centred, axis=-1, keepdims=True) + LN_EPS)
+        x_hat = centred * inv_std
+        dn = tot[...]
+        gg_ref[...] += jnp.sum(dn * x_hat, axis=0, keepdims=True)
+        d_hat = dn * gain_ref[...]
+        dx = inv_std * (d_hat - jnp.mean(d_hat, axis=-1, keepdims=True) - x_hat * jnp.mean(d_hat * x_hat, axis=-1, keepdims=True))
+        gx_buf[slot] = (dy_in[slot].astype(F32) + dx).astype(BF16)
+
+    gg_ref[...] = jnp.zeros_like(gg_ref)
+    for copy in inputs(0, 0):
+        copy.start()
+
+    me = z * cp + r
+
+    def gain_copy(dt, dc):
+        to = {"tp": lax.rem(z + dt, tp), "cp": lax.rem(r + dc, cp)}
+        return remote(gain_all.at[me], gain_all.at[me], gs_sem.at[dt * cp + dc], gr_sem.at[me], to)
+
+    def gain_wait(dt, dc):
+        sender = lax.rem(z + dt, tp) * cp + lax.rem(r + dc, cp)
+        remote(gain_all.at[sender], gain_all.at[sender], gs_sem.at[0], gr_sem.at[sender], right).wait_recv()
+
+    def step(i, carry):
+        cur = lax.rem(i, 2)
+        prv = 1 - cur
+
+        @pl.when(i < groups)
+        def _():
+            for copy in inputs(i, cur):
+                copy.wait()
+            partial_norm(cur)
+
+        rs_send(i, cur, 0)
+        ag_step(i - 2, 1)
+
+        @pl.when(jnp.logical_and(i >= 1, i <= groups))
+        def _():
+            finalize(i - 1, prv)
+
+        @pl.when(i + 1 < groups)
+        def _():
+            for copy in inputs(i + 1, prv):
+                copy.start()
+
+        @pl.when(jnp.logical_and(i >= 2, i < groups))
+        def _():
+            y_copy(i - 2, cur).wait()
+
+        @pl.when(i < groups)
+        def _():
+            project_out(cur, 0, d_model // 2)
+
+        rs_send(i, cur, 1)
+        ag_step(i - 2, 2)
+
+        @pl.when(i < groups)
+        def _():
+            project_out(cur, d_model // 2, d_model)
+            y_copy(i, cur).start()
+
+        rs_send(i, cur, 2)
+
+        @pl.when(jnp.logical_and(i >= 1, i <= groups))
+        def _():
+            ag_first(i - 1, prv)
+
+        @pl.when(i == groups)
+        def _():
+            gain_all[me] = gg_ref[...]
+            for dt, dc in peers:
+                gain_copy(dt, dc).start()
+
+        ag_step(i - 2, 3)
+        return carry
+
+    lax.fori_loop(0, groups + 2, step, 0)
+
+    for i in (groups - 2, groups - 1):
+        y_copy(i, i % 2).wait()
+        ag_first_done(i, i % 2)
+    for to_right in (True, False):
+        far = z if to_right else last - z
+        for s in range(slots):
+            @pl.when(jnp.logical_and(far <= s, far < last))
+            def _(s=s, to_right=to_right):
+                rs_copy(groups - 1, s, to_right).wait_send()
+        for a in range(1, slots):
+            @pl.when(jnp.logical_and(far >= a, far < last))
+            def _(a=a, to_right=to_right):
+                ag_forward(groups - 1, a, to_right).wait_send()
+    for dt, dc in peers:
+        gain_wait(dt, dc)
+        gain_copy(dt, dc).wait_send()
+    total = gain_all[0]
+    for j in range(1, tp * cp):
+        total += gain_all[j]
+    gg_ref[...] = total
+
+
+def backward_norm(dq, dkv, x, dy, o_all, wq, wk, wv, wo_all, gain, rows, tp, cp):
+    tokens, hidden = dq.shape
+    d_model = x.shape[1]
+    span = tp * rows
+    groups = tokens // span
+    slots = tp - 1
+    hbm = pl.BlockSpec(memory_space=pl.ANY)
+    vmem = pl.BlockSpec(memory_space=pltpu.VMEM)
+    dma = pltpu.SemaphoreType.DMA
     return pl.pallas_call(
-        out_kernel,
-        grid=(tokens // rows,),
-        in_specs=[pl.BlockSpec((rows, d_model), lambda i: (i, 0)), pl.BlockSpec((tp, rows, hidden), lambda i: (0, i, 0)), pl.BlockSpec(memory_space=pltpu.VMEM)],
-        out_specs=pl.BlockSpec((rows, d_model), lambda i: (i, 0)),
-        out_shape=jax.ShapeDtypeStruct((tokens, d_model), BF16),
-        compiler_params=pltpu.CompilerParams(dimension_semantics=("arbitrary",), vmem_limit_bytes=48 << 20),
-        cost_estimate=pl.CostEstimate(flops=2 * tokens * tp * hidden * d_model, bytes_accessed=8 * tokens * d_model, transcendentals=0),
-        name="out_project",
-    )(x, o_all, w_all)
-
-
-def dn_kernel(dq_ref, dkv_ref, wq_ref, wk_ref, wv_ref, dn_ref):
-    dn = dot_nt(dq_ref[...], wq_ref[...]) + dot_nt(dkv_ref[0], wk_ref[...]) + dot_nt(dkv_ref[1], wv_ref[...])
-    dn_ref[...] = dn.astype(BF16)
-
-
-def norm_partial(dq, dkv, wq, wk, wv, rows):
-    tokens, hidden = dq.shape
-    d_model = wq.shape[0]
-    whole = pl.BlockSpec(memory_space=pltpu.VMEM)
-    return pl.pallas_call(
-        dn_kernel,
-        grid=(tokens // rows,),
-        in_specs=[pl.BlockSpec((rows, hidden), lambda i: (i, 0)), pl.BlockSpec((2, rows, hidden), lambda i: (0, i, 0)), whole, whole, whole],
-        out_specs=pl.BlockSpec((rows, d_model), lambda i: (i, 0)),
-        out_shape=jax.ShapeDtypeStruct((tokens, d_model), BF16),
-        compiler_params=pltpu.CompilerParams(dimension_semantics=("arbitrary",), vmem_limit_bytes=48 << 20),
-        cost_estimate=pl.CostEstimate(flops=6 * tokens * hidden * d_model, bytes_accessed=2 * tokens * (d_model + 3 * hidden), transcendentals=0),
-        name="norm_partial",
-    )(dq, dkv, wq, wk, wv)
+        functools.partial(back_kernel, groups, rows, tp, cp),
+        in_specs=[hbm] * 5 + [vmem] * 5,
+        out_specs=[hbm, hbm, vmem],
+        out_shape=[
+            jax.ShapeDtypeStruct((tokens, d_model), BF16),
+            jax.ShapeDtypeStruct((tokens, d_model), BF16),
+            jax.ShapeDtypeStruct((1, d_model), F32),
+        ],
+        scratch_shapes=[
+            pltpu.VMEM((2, span, d_model), F32),
+            pltpu.VMEM((groups, slots, rows, d_model), BF16),
+            pltpu.VMEM((groups, slots, rows, d_model), BF16),
+            pltpu.VMEM((slots, rows, d_model), BF16),
+            pltpu.VMEM((slots, rows, d_model), BF16),
+            pltpu.VMEM((rows, d_model), F32),
+            pltpu.VMEM((2, rows, d_model), BF16),
+            pltpu.VMEM((2, span, hidden), BF16),
+            pltpu.VMEM((2, 2, span, hidden), BF16),
+            pltpu.VMEM((2, tp, span, hidden), BF16),
+            pltpu.VMEM((2, span, d_model), BF16),
+            pltpu.VMEM((2, rows, d_model), BF16),
+            pltpu.VMEM((2, span, d_model), BF16),
+            pltpu.VMEM((tp * cp, 1, d_model), F32),
+            dma((2, 5)),
+            dma((2,)),
+            dma((2,)),
+            dma((slots,)),
+            dma((slots,)),
+            dma((groups, slots)),
+            dma((groups, slots)),
+            dma((2,)),
+            dma((2,)),
+            dma((slots,)),
+            dma((slots,)),
+            dma((groups, slots)),
+            dma((groups, slots)),
+            dma((tp * cp,)),
+            dma((tp * cp,)),
+        ],
+        compiler_params=pltpu.CompilerParams(collective_id=0, has_side_effects=True, vmem_limit_bytes=60 << 20),
+        cost_estimate=pl.CostEstimate(flops=14 * tokens * hidden * d_model, bytes_accessed=16 * tokens * d_model, transcendentals=0),
+        name="backward_norm",
+    )(dq, dkv, x, dy, o_all, wq, wk, wv, wo_all, gain)
 
 
 def solution(mesh):
@@ -292,20 +573,8 @@
         dk = (dk_f32 * wide(cos_t) + swapped * wide(sin_t)).astype(BF16)
         dkv = jnp.stack([dk, dkv_sum[1]])
 
-        dn_part = norm_partial(dq, dkv, w_query, w_key, w_value, rows)
-        dn = lax.psum_scatter(dn_part, "tp", scatter_dimension=0, tiled=True).astype(F32)
-        quarter = tokens // tp_size
-        here = lax.axis_index("tp") * quarter
-        x_q = lax.dynamic_slice(x, (here, 0), (quarter, d_model)).astype(F32)
-        dy_q = lax.dynamic_slice(dy, (here, 0), (quarter, d_model)).astype(F32)
-        centred = x_q - jnp.mean(x_q, axis=-1, keepdims=True)
-        inv_std = lax.rsqrt(jnp.mean(centred * centred, axis=-1, keepdims=True) + LN_EPS)
-        x_hat = centred * inv_std
-        d_hat = dn * norm_gain
-        dx = inv_std * (d_hat - jnp.mean(d_hat, axis=-1, keepdims=True) - x_hat * jnp.mean(d_hat * x_hat, axis=-1, keepdims=True))
-        grad_x_q = (dy_q + dx).astype(BF16)
-        grad_x = lax.all_gather(grad_x_q, "tp", axis=0, tiled=True)
-        grad_gain = lax.psum(jnp.sum(dn * x_hat, axis=0), ("tp", "cp"))
+        grad_x, y_out, grad_gain = backward_norm(dq, dkv, x, dy, o_all, w_query, w_key, w_value, w_all, norm_gain.reshape(1, d_model), ROWS, tp_size, cp_size)
+        grad_gain = grad_gain.reshape(d_model)
 
         def tn(a, b):
             return lax.dot_general(a, b, (((0,), (0,)), ((), ())), preferred_element_type=F32)
@@ -324,7 +593,6 @@
         grad_wq = reduce_cp(tn(normed, dq))
         grad_wk = reduce_cp(tn(normed, dkv[0]))
         grad_wv = reduce_cp(tn(normed, dkv[1]))
-        y_out = out_project(x, o_all, w_all, rows)
         return y_out.reshape(x_in.shape), grad_x.reshape(x_in.shape), grad_gain, grad_wq, grad_wk, grad_wv, grad_wo
 
     in_specs = (P("dp", "cp", None), P("dp", "cp"), P("dp", "cp"), P(None, "tp"), P(None, "tp"), P(None, "tp"), P("tp", None), P(None), P("dp", "cp", None))

time: 1130 us -> 900 us (0.80)
  waiting for transfers between devices: 737 us -> 242 us
  Pallas kernels: 119 us -> 332 us
  starting transfers between devices: 18.1 us -> 114 us
  blocking collectives: 33.1 us -> 0 us
    pallas_call x2 -> x1, Pallas kernels: 45.6 us -> 258 us  [backward_norm(): pl.pallas_call(functools.partial(back_kernel, groups, rows, tp, cp), in_s...]
    all_gather x1, waiting for transfers between devices: 167 us -> 0.01 us  [device_step(): o_all = lax.all_gather(o, 'tp', axis=0)]
    reduce_scatter x1 -> x0, waiting for transfers between devices: 143 us -> none  [device_step(): lax.psum_scatter(dn_part, 'tp', scatter_dimension=0, tiled=True).astype(F32)]
    ppermute x18, starting transfers between devices: 17.7 us -> 114 us  [perm(): return lax.ppermute(value, 'cp', pairs)]
    all_gather x1 -> x0, waiting for transfers between devices: 95.9 us -> none  [device_step(): grad_x = lax.all_gather(grad_x_q, 'tp', axis=0, tiled=True)]
    ppermute x18, waiting for transfers between devices: 306 us -> 242 us  [perm(): return lax.ppermute(value, 'cp', pairs)]
    psum x1 -> x0, blocking collectives: 33.1 us -> none  [device_step(): grad_gain = lax.psum(jnp.sum(dn * x_hat, axis=0), ('tp', 'cp'))]
    all_gather x1, waiting for transfers between devices: 23.2 us -> 0.01 us  [device_step(): w_all = lax.all_gather(w_out, 'tp', axis=0)]
  transfers between devices with their start and end apart: 22 -> 20, of which waited for: 10 -> 5; matrix products, arithmetic and copies ran while one was open for 11% -> 16% of each run, Pallas kernels for 2% -> 34%
where the time goes in v2:
time: 900 us; the launch traced here: 894 us
  Pallas kernels  332 us (37%)
  waiting for transfers between devices  242 us (27%)
  starting transfers between devices  114 us (13%)
  other arithmetic  81.1 us (9%)
  local copies, waits for them, and re-layouts  70.6 us (8%)
  matrix products  38.9 us (4%)
  between operations  14.9 us (2%)
    pallas_call x1, Pallas kernels, backward_norm(): pl.pallas_call(functools.partial(back_kernel, groups, rows, tp, cp), in_s...  258 us
    ppermute x18, waiting for transfers between devices, perm(): return lax.ppermute(value, 'cp', pairs)  242 us
    ppermute x18, starting transfers between devices, perm(): return lax.ppermute(value, 'cp', pairs)  114 us
    pallas_call x1, Pallas kernels, attend(): pl.pallas_call(attn_kernel, grid_spec=pltpu.PrefetchScalarGridSpec(num_sc...  42.2 us
    dot_general x4, matrix products, tn(): lax.dot_general(a, b, (((0,), (0,)), ((), ())), preferred_element_type=F32)  38.9 us
    pallas_call x1, Pallas kernels, project(): pl.pallas_call(proj_kernel, grid=(tokens // rows,), in_specs=[tile(d_mode...  31.9 us
    unnamed x55, local copies, waits for them, and re-layouts  30.9 us
    select_n x4, other arithmetic, reduce_cp(): jnp.where(core == 0, jnp.concatenate([total, rest]), jnp.concatenate([res...  25.9 us
  transfers between devices with their start and end apart: 20, of which 5 were waited for; matrix products, arithmetic and copies ran while one was open for 16% of the time, Pallas kernels for 34%

profile of v2, /device:TPU:0, one launch (start us, length us, event | category | flops | bytes accessed | tf_op | source)
XLA Modules:
  0.0 894.1 jit_solution(7277910203180778901)
XLA Ops:
  8.3 6.2 multiply_sine_fusion
  14.5 31.9 %project.1 = (bf16[2304,2048]{1,0:T(8,128)(2,1)}, bf16[2304,512]{1,0:T(8,128)(2,1)}, bf16[2,2304,512]{2,1,0:T(8,128)(2,1)}, bf16[2304,512]{1,0:T(8,128)(2,1)}) custom-call(bf16[2304,2048]{1,0:T(8,128)(2,1)} %bitcast.58, bf16[2304,2048]{1,0:T(8,128)(2,1)} %bitcast.60, f32[2304,128]{1,0:T(8,128)} %get-tuple-element.44.cos_ref, ...), custom_call_target="tpu_custom_call" | custom-call | flops 19327352832 | bytes 46137344 | tf_op jit(solution)/shard_map/project/pallas_call | solution.py:71
  46.4 7.1 collective-permute-start.1
  53.5 3.6 collective-permute-start
  57.1 95.3 %collective-permute-done.1.kv2_ref = bf16[2,2304,512]{2,1,0:T(8,128)(2,1)} collective-permute-done((bf16[2,2304,512]{2,1,0:T(8,128)(2,1)}, bf16[2,2304,512]{2,1,0:T(8,128)(2,1)}, u32[]{:S(2)}, u32[]{:S(2)}) %collective-permute-start.1) | collective-permute-done | bytes 4718624 | tf_op jit(solution)/shard_map/ppermute | solution.py:556
  152.4 2.8 collective-permute-start.2
  155.5 42.2 %attend.1 = (bf16[2304,512]{1,0:T(8,128)(2,1)S(1)}, bf16[2304,512]{1,0:T(8,128)(2,1)}, bf16[2,2304,512]{2,1,0:T(8,128)(2,1)}, bf16[2,2304,512]{2,1,0:T(8,128)(2,...) custom-call(s32[7]{0:T(128)S(1)} %pad_add_fusion.info_ref, s32[6,1,384]{2,1,0:T(1,128)S(1)} %reshape.261.start_ref, ...), custom_call_target="tpu_custom_call" | custom-call | flops 21743271936 | bytes 42467328 | tf_op jit(solution)/shard_map/attend/pallas_call | solution.py:184
  199.1 2.8 collective-permute-start.4
  201.9 8.5 fusion.24
  214.0 24.3 %collective-permute-start.15 = (f32[256,2048]{1,0:T(8,128)}, f32[256,2048]{1,0:T(8,128)}, u32[]{:S(2)}, u32[]{:S(2)}) collective-permute-start(f32[256,2048]{1,0:T(8,128)} %constant_dynamic-slice_fusion), channel_id=1, source_target_pairs={{0,1},{1,0},{2,3},{3,2},{4,5},{5,4},{6,7},{7,6},{8,9},{9,8},{10,11... | collective-permute-start | bytes 6291464 | tf_op jit(solution)/shard_map/ppermute | solution.py:556
  240.0 6.0 add_convert_fusion.1
  247.4 5.3 fusion.23
  256.2 3.2 collective-permute-start.6
  259.5 2.5 add_convert_fusion.2
  262.0 55.7 %collective-permute-start.16 = (bf16[256,2048]{1,0:T(8,128)(2,1)S(1)}, bf16[256,2048]{1,0:T(8,128)(2,1)}, u32[]{:S(2)}, u32[]{:S(2)}) collective-permute-start(bf16[256,2048]{1,0:T(8,128)(2,1)S(1)} %add_convert_fusion.2), channel_id=1, source_target_pairs={{0,2},{2,0},{1,3},{3,1},{4,6},{6,4},{5,7},{7,5},{8,10},{10,8},{9,1... | collective-permute-start | bytes 3145736 | tf_op jit(solution)/shard_map/ppermute | solution.py:556
  317.7 3.5 add_convert_fusion.5
  322.5 101.0 %collective-permute-done.16 = bf16[256,2048]{1,0:T(8,128)(2,1)} collective-permute-done((bf16[256,2048]{1,0:T(8,128)(2,1)S(1)}, bf16[256,2048]{1,0:T(8,128)(2,1)}, u32[]{:S(2)}, u32[]{:S(2)}) %collective-permute-start.16) | collective-permute-done | bytes 1048608 | tf_op jit(solution)/shard_map/ppermute | solution.py:556
  423.5 2.9 convert_add_fusion
  426.4 5.3 collective-permute-start.17
  431.7 14.3 %collective-permute-done.7 = bf16[1024,512]{1,0:T(8,128)(2,1)} collective-permute-done((bf16[1024,512]{1,0:T(8,128)(2,1)}, bf16[1024,512]{1,0:T(8,128)(2,1)}, u32[]{:S(2)}, u32[]{:S(2)}) %collective-permute-start.7) | collective-permute-done | bytes 1048608 | tf_op jit(solution)/shard_map/ppermute | solution.py:556
  446.0 3.1 convert_add_fusion.3
  449.1 2.8 collective-permute-start.8
  451.9 7.1 add_convert_fusion
  459.0 9.4 %fusion.7 = f32[2048,512]{1,0:T(8,128)S(1)} fusion(bf16[2304,2048]{1,0:T(8,128)(2,1)} %get-tuple-element.32, bf16[2,2304,512]{2,1,0:T(8,128)(2,1)S(1)} %add_convert_fusion), kind=kOutput, calls=%fused_computation.23 | convolution fusion | flops 4831838208 | bytes 15990784 | tf_op jit(solution)/shard_map/dot_general | solution.py:580
  471.0 2.2 convert_bitcast_fusion
  473.2 2.2 copy-done.3
  475.4 2.3 fusion.20
  477.7 12.2 %fusion.21 = (f32[2304,511]{1,0:T(8,128)}, f32[1,2304,511]{2,1,0:T(8,128)}, f32[1,2304,511]{2,1,0:T(8,128)}, f32[2304,511]{1,0:T(8,128)}) fusion(f32[2304,512]{1,0:T(8,128)} %copy-done.3), kind=kLoop, calls=%fused_computation.61 | loop fusion | bytes 28256256 | tf_op jit(solution)/shard_map/jit(_roll_static)/slice | solution.py:571
  490.7 2.9 tile.24
  493.6 2.7 copy-done.5
  496.6 15.7 %fusion.5 = f32[2048,512]{1,0:T(8,128)} fusion(bf16[2304,2048]{1,0:T(8,128)(2,1)} %get-tuple-element.32, f32[288,8,4,128]{3,2,1,0:T(4,128)} %bitcast.52, f32[288,8,4,128]{3,2,1,0:T(4,128)S(1)} %bitcast.51, f32[2304,1]{1,0:T(8,128)} %get-tuple-element.36, f32[2304,511]{1,0:T(8,128)} %get-tuple-element.40, f32[2304,511]{1,0:T(8,128)} %get-tuple-element.37, ...), kind=kOutput, calls=%fused_computation.22 | convolution fusion | flops 4844814336 | bytes 36040192 | tf_op jit(solution)/shard_map/dot_general | solution.py:580
  512.4 3.2 constant_dynamic-slice_fusion.2
  516.1 6.7 tile.23
  522.8 6.5 tile.25
  529.3 6.8 maximum_select_fusion.5
  536.2 7.3 maximum_select_fusion.2
  543.5 3.8 add_convert_fusion.3
  547.2 3.4 add_convert_fusion.4
  552.3 4.3 fusion.1
  556.6 4.3 pad_maximum_fusion.dkv_hbm
  560.9 12.4 %collective-permute-done.13 = bf16[1024,512]{1,0:T(8,128)(2,1)} collective-permute-done((bf16[1024,512]{1,0:T(8,128)(2,1)}, bf16[1024,512]{1,0:T(8,128)(2,1)}, u32[]{:S(2)}, u32[]{:S(2)}) %collective-permute-start.13) | collective-permute-done | bytes 1048608 | tf_op jit(solution)/shard_map/ppermute | solution.py:556
  575.2 19.6 %collective-permute-done.10 = bf16[1024,512]{1,0:T(8,128)(2,1)} collective-permute-done((bf16[1024,512]{1,0:T(8,128)(2,1)}, bf16[1024,512]{1,0:T(8,128)(2,1)}, u32[]{:S(2)}, u32[]{:S(2)}) %collective-permute-start.10) | collective-permute-done | bytes 1048608 | tf_op jit(solution)/shard_map/ppermute | solution.py:556
  594.8 3.2 convert_add_fusion.2
  597.9 257.8 %backward_norm.1 = (bf16[2304,2048]{1,0:T(8,128)(2,1)}, bf16[2304,2048]{1,0:T(8,128)(2,1)}, f32[1,2048]{1,0:T(1,128)}) custom-call(bf16[2304,512]{1,0:T(8,128)(2,1)} %get-tuple-element.23.dq_hbm, bf16[2,2304,512]{2,1,0:T(8,128)(2,1)} %pad_maximum_fusion.dkv_hbm, bf16[2304,2048]{1,0:T(8,128)(2,1)} %bitcast.59, bf16[2304,2048]{1,0:T(8,128)(2,1)} %bitcast.62, ...), custom_call_target="tpu_custom_call" | custom-call | flops 33822867456 | bytes 75497472 | tf_op jit(solution)/shard_map/backward_norm/pallas_call | solution.py:486
  855.7 5.3 maximum_select_fusion.4
  861.0 6.5 maximum_select_fusion.3
  867.5 9.4 %copy.24 = bf16[6,384,2048]{2,1,0:T(8,128)(2,1)} copy(bf16[6,384,2048]{2,1,0:T(8,128)(2,1)} %bitcast.56) | data formatting | bytes 18874368
  876.9 9.4 %copy.25 = bf16[6,384,2048]{2,1,0:T(8,128)(2,1)} copy(bf16[6,384,2048]{2,1,0:T(8,128)(2,1)} %bitcast.55) | data formatting | bytes 18874368
  (100 shorter events, 22.6 us)
Async XLA Ops:
  7.2 590.8 %all-gather.7.cloned.1.call-start = ((), (), s32[]{:S(2)}) async-start(), calls=%async_computation.1 | async-start | bytes 10485760 | tf_op jit(solution)/shard_map/all_gather | solution.py:551
  14.5 141.0 %copy-start = (f32[2304,128]{1,0:T(8,128)S(1)}, f32[2304,128]{1,0:T(8,128)}, u32[]{:S(2)}) copy-start(f32[2304,128]{1,0:T(8,128)} %get-tuple-element.43.sin_ref) | copy-start | bytes 3538948
  14.5 141.0 %copy-start.1 = (f32[2304,128]{1,0:T(8,128)S(1)}, f32[2304,128]{1,0:T(8,128)}, u32[]{:S(2)}) copy-start(f32[2304,128]{1,0:T(8,128)} %get-tuple-element.44.cos_ref) | copy-start | bytes 3538948
  46.4 106.0 %collective-permute-start.1 = (bf16[2,2304,512]{2,1,0:T(8,128)(2,1)}, bf16[2,2304,512]{2,1,0:T(8,128)(2,1)}, u32[]{:S(2)}, u32[]{:S(2)}) collective-permute-start(bf16[2,2304,512]{2,1,0:T(8,128)(2,1)} %get-tuple-element.22.kv0_ref), channel_id=1, source_target_pairs={{0,2},{1,3},{4,6},{5,7},{8,10},{9,11},{12,14},{13,15},{16,18},{17,... | collective-permute-start | bytes 14155784 | tf_op jit(solution)/shard_map/ppermute | solution.py:556
  53.5 102.0 %collective-permute-start = (bf16[2,2304,512]{2,1,0:T(8,128)(2,1)}, bf16[2,2304,512]{2,1,0:T(8,128)(2,1)}, u32[]{:S(2)}, u32[]{:S(2)}) collective-permute-start(bf16[2,2304,512]{2,1,0:T(8,128)(2,1)} %get-tuple-element.22.kv0_ref), channel_id=1, source_target_pairs={{0,1},{2,3},{4,5},{6,7},{8,9},{10,11},{12,13},{14,15},{16,17},{18,... | collective-permute-start | bytes 14155784 | tf_op jit(solution)/shard_map/ppermute | solution.py:556
  152.4 3.1 collective-permute-start.2
  155.2 442.7 %all-gather.5.cloned.1.call-start = ((), (), s32[]{:S(2)}) async-start(), calls=%async_computation | async-start | bytes 11796480 | tf_op jit(solution)/shard_map/all_gather | solution.py:562
  197.7 1.4 copy-start.2
  199.1 40.9 %collective-permute-start.4 = (bf16[2,2304,512]{2,1,0:T(8,128)(2,1)}, bf16[2,2304,512]{2,1,0:T(8,128)(2,1)}, u32[]{:S(2)}, u32[]{:S(2)}) collective-permute-start(bf16[2,2304,512]{2,1,0:T(8,128)(2,1)} %get-tuple-element.27), channel_id=1, source_target_pairs={{2,3},{3,2},{6,7},{7,6},{10,11},{11,10},{14,15},{15,14},{18,19},{1... | collective-permute-start | bytes 14155784 | tf_op jit(solution)/shard_map/ppermute | solution.py:556
  201.9 38.1 %copy-start.8 = (bf16[2,2304,512]{2,1,0:T(8,128)(2,1)S(1)}, bf16[2,2304,512]{2,1,0:T(8,128)(2,1)}, u32[]{:S(2)}) copy-start(bf16[2,2304,512]{2,1,0:T(8,128)(2,1)} %get-tuple-element.26) | copy-start | bytes 14155780
  201.9 45.5 %slice-start.8 = ((s8[9437184]{0:T(1024)(128)(4,1)}), s8[4194304]{0:T(1024)(128)(4,1)S(1)}, s32[]{:S(2)}) async-start(s8[9437184]{0:T(1024)(128)(4,1)} %bitcast.67), calls=%async_computation.10 | async-start | bytes 8388608
  201.9 45.5 %slice-start.9 = ((s8[9437184]{0:T(1024)(128)(4,1)}), s8[4194304]{0:T(1024)(128)(4,1)S(1)}, s32[]{:S(2)}) async-start(s8[9437184]{0:T(1024)(128)(4,1)} %bitcast.67), calls=%async_computation.11 | async-start | bytes 8388608
  210.4 2.0 copy-start.10
  214.0 45.5 %collective-permute-start.15 = (f32[256,2048]{1,0:T(8,128)}, f32[256,2048]{1,0:T(8,128)}, u32[]{:S(2)}, u32[]{:S(2)}) collective-permute-start(f32[256,2048]{1,0:T(8,128)} %constant_dynamic-slice_fusion), channel_id=1, source_target_pairs={{0,1},{1,0},{2,3},{3,2},{4,5},{5,4},{6,7},{7,6},{8,9},{9,8},{10,11... | collective-permute-start | bytes 6291464 | tf_op jit(solution)/shard_map/ppermute | solution.py:556
  238.2 213.7 %collective-permute-start.3 = (bf16[2,2304,512]{2,1,0:T(8,128)(2,1)}, bf16[2,2304,512]{2,1,0:T(8,128)(2,1)}, u32[]{:S(2)}, u32[]{:S(2)}) collective-permute-start(bf16[2,2304,512]{2,1,0:T(8,128)(2,1)} %get-tuple-element.25), channel_id=1, source_target_pairs={{1,0},{3,2},{5,4},{7,6},{9,8},{11,10},{13,12},{15,14},{17,16},{19,... | collective-permute-start | bytes 14155784 | tf_op jit(solution)/shard_map/ppermute | solution.py:556
  240.0 7.4 slice-start.10
  240.0 7.4 copy-start.14
  246.1 205.8 %collective-permute-start.5 = (bf16[2,2304,512]{2,1,0:T(8,128)(2,1)}, bf16[2,2304,512]{2,1,0:T(8,128)(2,1)}, u32[]{:S(2)}, u32[]{:S(2)}) collective-permute-start(bf16[2,2304,512]{2,1,0:T(8,128)(2,1)} %add_convert_fusion.1), channel_id=1, source_target_pairs={{2,0},{3,1},{6,4},{7,5},{10,8},{11,9},{14,12},{15,13},{18,16},{19,... | collective-permute-start | bytes 14155784 | tf_op jit(solution)/shard_map/ppermute | solution.py:556
  252.7 2.0 copy-start.11
  256.2 61.5 %collective-permute-start.6 = (f32[1024,512]{1,0:T(8,128)}, f32[1024,512]{1,0:T(8,128)}, u32[]{:S(2)}, u32[]{:S(2)}) collective-permute-start(f32[1024,512]{1,0:T(8,128)} %constant_dynamic-slice_fusion.3), channel_id=1, source_target_pairs={{0,1},{1,0},{2,3},{3,2},{4,5},{5,4},{6,7},{7,6},{8,9},{9,8},{10,11... | collective-permute-start | bytes 6291464 | tf_op jit(solution)/shard_map/ppermute | solution.py:556
  262.0 161.5 %collective-permute-start.16 = (bf16[256,2048]{1,0:T(8,128)(2,1)S(1)}, bf16[256,2048]{1,0:T(8,128)(2,1)}, u32[]{:S(2)}, u32[]{:S(2)}) collective-permute-start(bf16[256,2048]{1,0:T(8,128)(2,1)S(1)} %add_convert_fusion.2), channel_id=1, source_target_pairs={{0,2},{2,0},{1,3},{3,1},{4,6},{6,4},{5,7},{7,5},{8,10},{10,8},{9,1... | collective-permute-start | bytes 3145736 | tf_op jit(solution)/shard_map/ppermute | solution.py:556
  321.3 124.7 %collective-permute-start.7 = (bf16[1024,512]{1,0:T(8,128)(2,1)}, bf16[1024,512]{1,0:T(8,128)(2,1)}, u32[]{:S(2)}, u32[]{:S(2)}) collective-permute-start(bf16[1024,512]{1,0:T(8,128)(2,1)} %add_convert_fusion.5), channel_id=1, source_target_pairs={{0,2},{2,0},{1,3},{3,1},{4,6},{6,4},{5,7},{7,5},{8,10},{10,8},{9,1... | collective-permute-start | bytes 3145736 | tf_op jit(solution)/shard_map/ppermute | solution.py:556
  426.4 102.9 %collective-permute-start.17 = (f32[256,2048]{1,0:T(8,128)}, f32[256,2048]{1,0:T(8,128)}, u32[]{:S(2)}, u32[]{:S(2)}) collective-permute-start(f32[256,2048]{1,0:T(8,128)} %convert_add_fusion), channel_id=1, source_target_pairs={{0,1},{1,0},{2,3},{3,2},{4,5},{5,4},{6,7},{7,6},{8,9},{9,8},{10,11... | collective-permute-start | bytes 6291464 | tf_op jit(solution)/shard_map/ppermute | solution.py:556
  449.1 87.1 %collective-permute-start.8 = (f32[1024,512]{1,0:T(8,128)}, f32[1024,512]{1,0:T(8,128)}, u32[]{:S(2)}, u32[]{:S(2)}) collective-permute-start(f32[1024,512]{1,0:T(8,128)} %convert_add_fusion.3), channel_id=1, source_target_pairs={{0,1},{1,0},{2,3},{3,2},{4,5},{5,4},{6,7},{7,6},{8,9},{9,8},{10,11... | collective-permute-start | bytes 6291464 | tf_op jit(solution)/shard_map/ppermute | solution.py:556
  459.0 12.0 %copy-start.4 = (bf16[2,2304,512]{2,1,0:T(8,128)(2,1)}, bf16[2,2304,512]{2,1,0:T(8,128)(2,1)S(1)}, u32[]{:S(2)}) copy-start(bf16[2,2304,512]{2,1,0:T(8,128)(2,1)S(1)} %add_convert_fusion) | copy-start | bytes 14155780
  468.3 2.6 copy-start.9
  471.0 72.5 %collective-permute-start.12 = (f32[1024,512]{1,0:T(8,128)}, f32[1024,512]{1,0:T(8,128)}, u32[]{:S(2)}, u32[]{:S(2)}) collective-permute-start(f32[1024,512]{1,0:T(8,128)} %constant_dynamic-slice_fusion.1), channel_id=1, source_target_pairs={{0,1},{1,0},{2,3},{3,2},{4,5},{5,4},{6,7},{7,6},{8,9},{9,8},{10,11... | collective-permute-start | bytes 6291464 | tf_op jit(solution)/shard_map/ppermute | solution.py:556
  473.2 2.2 copy-start.3
  490.7 21.7 %copy-start.6 = (f32[2304,4,128]{2,1,0:T(4,128)}, f32[2304,4,128]{2,1,0:T(4,128)S(1)}, u32[]{:S(2)}) copy-start(f32[2304,4,128]{2,1,0:T(4,128)S(1)} %tile.22) | copy-start | bytes 14155780
  490.7 5.6 copy-start.5
  490.7 6.0 copy-start.12
  515.6 31.7 %collective-permute-start.9 = (f32[1024,512]{1,0:T(8,128)}, f32[1024,512]{1,0:T(8,128)S(1)}, u32[]{:S(2)}, u32[]{:S(2)}) collective-permute-start(f32[1024,512]{1,0:T(8,128)} %constant_dynamic-slice_fusion.2), channel_id=1, source_target_pairs={{0,1},{1,0},{2,3},{3,2},{4,5},{5,4},{6,7},{7,6},{8,9},{9,8},{10,11... | collective-permute-start | bytes 6291464 | tf_op jit(solution)/shard_map/ppermute | solution.py:556
  529.3 22.9 %slice-start.2 = ((s8[4718592]{0:T(1024)(128)(4,1)}), s8[4194304]{0:T(1024)(128)(4,1)S(1)}, s32[]{:S(2)}) async-start(s8[4718592]{0:T(1024)(128)(4,1)} %bitcast.47), calls=%async_computation.4 | async-start | bytes 8388608
  529.3 22.9 %slice-start.4 = ((s8[4718592]{0:T(1024)(128)(4,1)}), s8[4194304]{0:T(1024)(128)(4,1)S(1)}, s32[]{:S(2)}) async-start(s8[4718592]{0:T(1024)(128)(4,1)} %bitcast.49), calls=%async_computation.6 | async-start | bytes 8388608
  529.3 22.9 %slice-start.6 = ((s8[4718592]{0:T(1024)(128)(4,1)}), s8[4194304]{0:T(1024)(128)(4,1)S(1)}, s32[]{:S(2)}) async-start(s8[4718592]{0:T(1024)(128)(4,1)} %bitcast.53), calls=%async_computation.8 | async-start | bytes 8388608
  536.2 16.0 %slice-start.3 = ((s8[4718592]{0:T(1024)(128)(4,1)}), s8[524288]{0:T(1024)(128)(4,1)S(1)}, s32[]{:S(2)}) async-start(s8[4718592]{0:T(1024)(128)(4,1)} %bitcast.47), calls=%async_computation.5 | async-start | bytes 1048576
  536.2 16.0 %slice-start.5 = ((s8[4718592]{0:T(1024)(128)(4,1)}), s8[524288]{0:T(1024)(128)(4,1)S(1)}, s32[]{:S(2)}) async-start(s8[4718592]{0:T(1024)(128)(4,1)} %bitcast.49), calls=%async_computation.7 | async-start | bytes 1048576
  536.2 16.0 %slice-start.7 = ((s8[4718592]{0:T(1024)(128)(4,1)}), s8[524288]{0:T(1024)(128)(4,1)S(1)}, s32[]{:S(2)}) async-start(s8[4718592]{0:T(1024)(128)(4,1)} %bitcast.53), calls=%async_computation.9 | async-start | bytes 1048576
  536.2 16.0 %slice-start = ((s8[4718592]{0:T(1024)(128)(4,1)}), s8[524288]{0:T(1024)(128)(4,1)S(1)}, s32[]{:S(2)}) async-start(s8[4718592]{0:T(1024)(128)(4,1)} %bitcast.45), calls=%async_computation.2 | async-start | bytes 1048576
  543.5 8.7 slice-start.1
  543.5 8.8 copy-start.7
  547.2 26.0 %collective-permute-start.13 = (bf16[1024,512]{1,0:T(8,128)(2,1)}, bf16[1024,512]{1,0:T(8,128)(2,1)}, u32[]{:S(2)}, u32[]{:S(2)}) collective-permute-start(bf16[1024,512]{1,0:T(8,128)(2,1)} %add_convert_fusion.3), channel_id=1, source_target_pairs={{0,2},{2,0},{1,3},{3,1},{4,6},{6,4},{5,7},{7,5},{8,10},{10,8},{9,1... | collective-permute-start | bytes 3145736 | tf_op jit(solution)/shard_map/ppermute | solution.py:556
  550.6 44.1 %collective-permute-start.10 = (bf16[1024,512]{1,0:T(8,128)(2,1)}, bf16[1024,512]{1,0:T(8,128)(2,1)}, u32[]{:S(2)}, u32[]{:S(2)}) collective-permute-start(bf16[1024,512]{1,0:T(8,128)(2,1)} %add_convert_fusion.4), channel_id=1, source_target_pairs={{0,2},{2,0},{1,3},{3,1},{4,6},{6,4},{5,7},{7,5},{8,10},{10,8},{9,1... | collective-permute-start | bytes 3145736 | tf_op jit(solution)/shard_map/ppermute | solution.py:556
  575.1 280.6 %collective-permute-start.14 = (f32[1024,512]{1,0:T(8,128)S(1)}, f32[1024,512]{1,0:T(8,128)}, u32[]{:S(2)}, u32[]{:S(2)}) collective-permute-start(f32[1024,512]{1,0:T(8,128)S(1)} %convert_add_fusion.1), channel_id=1, source_target_pairs={{0,1},{1,0},{2,3},{3,2},{4,5},{5,4},{6,7},{7,6},{8,9},{9,8},{10,11... | collective-permute-start | bytes 6291464 | tf_op jit(solution)/shard_map/ppermute | solution.py:556
  597.9 263.1 %collective-permute-start.11 = (f32[1024,512]{1,0:T(8,128)}, f32[1024,512]{1,0:T(8,128)}, u32[]{:S(2)}, u32[]{:S(2)}) collective-permute-start(f32[1024,512]{1,0:T(8,128)} %convert_add_fusion.2), channel_id=1, source_target_pairs={{0,1},{1,0},{2,3},{3,2},{4,5},{5,4},{6,7},{7,6},{8,9},{9,8},{10,11... | collective-permute-start | bytes 6291464 | tf_op jit(solution)/shard_map/ppermute | solution.py:556
  876.8 9.4 %copy-start.13 = (f32[1,2048]{1,0:T(1,128)S(1)}, f32[1,2048]{1,0:T(1,128)}, u32[]{:S(2)}) copy-start(f32[1,2048]{1,0:T(1,128)} %get-tuple-element.31) | copy-start | bytes 24580
Sparse Core Ops, SparseCore 0:
  155.4 150.9 all-gather.6
  322.6 166.3 all-gather.4

commit v3 on v2

--- a/solution.py
+++ b/solution.py
@@ -43,169 +43,439 @@
     return t * cos_t + swap_pairs(t, sign) * sin_t
 
 
-def proj_kernel(x_ref, dy_ref, cos_ref, sin_ref, gain_ref, wq_ref, wk_ref, wv_ref, wo_ref, n_ref, q_ref, kv_ref, do_ref):
+def put_rope(dst, raw, cos_t, sin_t):
+    for h in range(raw.shape[1] // HEAD_DIM):
+        cols = slice(h * HEAD_DIM, (h + 1) * HEAD_DIM)
+        dst[:, cols] = rope(raw[:, cols], cos_t, sin_t, 1.0).astype(BF16)
+
+
+def keys_kernel(x_ref, cos_ref, sin_ref, gain_ref, wk_ref, wv_ref, n_ref, kv_ref):
     x = x_ref[...].astype(F32)
     centred = x - jnp.mean(x, axis=-1, keepdims=True)
     inv_std = lax.rsqrt(jnp.mean(centred * centred, axis=-1, keepdims=True) + LN_EPS)
     normed = ((centred * inv_std) * gain_ref[...]).astype(BF16)
     n_ref[...] = normed
-    cos_t = cos_ref[...]
-    sin_t = sin_ref[...]
-
-    def put_rope(dst, raw):
-        for h in range(raw.shape[1] // HEAD_DIM):
-            cols = slice(h * HEAD_DIM, (h + 1) * HEAD_DIM)
-            dst[:, cols] = rope(raw[:, cols], cos_t, sin_t, 1.0).astype(BF16)
-
-    put_rope(kv_ref.at[0], dot_nn(normed, wk_ref[...]))
+    put_rope(kv_ref.at[0], dot_nn(normed, wk_ref[...]), cos_ref[...], sin_ref[...])
     kv_ref[1] = dot_nn(normed, wv_ref[...]).astype(BF16)
-    put_rope(q_ref, dot_nn(normed, wq_ref[...]))
-    do_ref[...] = dot_nt(dy_ref[...], wo_ref[...]).astype(BF16)
-
-
-def project(x, dy, cos_t, sin_t, gain, wq, wk, wv, wo, rows):
+
+
+def project_keys(x, cos_t, sin_t, gain, wk, wv, rows):
     tokens, d_model = x.shape
-    hidden = wq.shape[1]
+    hidden = wk.shape[1]
     whole = pl.BlockSpec(memory_space=pltpu.VMEM)
     tile = lambda width: pl.BlockSpec((rows, width), lambda i: (i, 0))
     return pl.pallas_call(
-        proj_kernel,
+        keys_kernel,
         grid=(tokens // rows,),
-        in_specs=[tile(d_model), tile(d_model), tile(HEAD_DIM), tile(HEAD_DIM), whole, whole, whole, whole, whole],
-        out_specs=[tile(d_model), tile(hidden), pl.BlockSpec((2, rows, hidden), lambda i: (0, i, 0)), tile(hidden)],
+        in_specs=[tile(d_model), tile(HEAD_DIM), tile(HEAD_DIM), whole, whole, whole],
+        out_specs=[tile(d_model), pl.BlockSpec((2, rows, hidden), lambda i: (0, i, 0))],
+        out_shape=[jax.ShapeDtypeStruct((tokens, d_model), BF16), jax.ShapeDtypeStruct((2, tokens, hidden), BF16)],
+        compiler_params=pltpu.CompilerParams(dimension_semantics=("arbitrary",), vmem_limit_bytes=48 << 20),
+        cost_estimate=pl.CostEstimate(flops=4 * tokens * d_model * hidden, bytes_accessed=4 * tokens * (d_model + hidden), transcendentals=0),
+        name="project_keys",
+    )(x, cos_t, sin_t, gain, wk, wv)
+
+
+MESH = pl.DeviceIdType.MESH
+SUB = 128
+ROWS = 48
+RELAY_LAG = 2
+CHIP_BUFS = 3
+
+
+def front_kernel(batch, seq, tp, cp, kv_hbm, n_hbm, dy_hbm, cos_ref, sin_ref, start_ref, wq_ref, wo_ref,
+                 o_all, dq_hbm, dkv_hbm,
+                 q_all, do_all, n_in, dy_in, kv_own, kvr, s_scr, dp_scr, m_scr, l_scr, d_scr, ot_scr, dqt_scr,
+                 o_buf, dq_buf, g_own, g_part, g_chip, g_far, xin, part_in, dkv_out,
+                 tile_sem, own_sem, kvs_part, kvs_chip, kvs_far, kv_recv, o_local, o_send, o_recv, relay_send, dq_sem,
+                 far_send, part_send, chip_send, x_recv, part_recv, dkv_sem):
+    z = lax.axis_index("tp")
+    r = lax.axis_index("cp")
+    core = lax.rem(r, 2)
+    chip = lax.div(r, 2)
+    hidden = q_all.shape[1]
+    heads = hidden // HEAD_DIM
+    first_chip, second_chip = chip == 0, chip == 1
+    first_core, second_core = core == 0, core == 1
+    partner = {"cp": r + 1 - 2 * core}
+    peer = {"cp": r + 2 - 4 * chip}
+
+    barrier = pltpu.get_barrier_semaphore()
+    for dev in [partner, peer] + [{"tp": lax.rem(z + dt, tp)} for dt in range(1, tp)]:
+        pl.semaphore_signal(barrier, inc=1, device_id=dev, device_id_type=MESH)
+    pl.semaphore_wait(barrier, tp + 1)
+
+    def remote(src, dst, ssem, rsem, dev):
+        return pltpu.make_async_remote_copy(src_ref=src, dst_ref=dst, send_sem=ssem, recv_sem=rsem, device_id=dev, device_id_type=MESH)
+
+    def row(b):
+        return pl.ds(pl.multiple_of(b * seq, seq), seq)
+
+    def kv_to_partner(b):
+        return remote(kv_hbm.at[:, row(b), :], kvr.at[0, b], kvs_part.at[b], kv_recv.at[0, b], partner)
+
+    def kv_to_chip(b):
+        return remote(kv_hbm.at[:, row(b), :], kvr.at[1, b], kvs_chip.at[b], kv_recv.at[1, b], peer)
+
+    def kv_forward(b):
+        return remote(kvr.at[1, b], kvr.at[2, b], kvs_far.at[b], kv_recv.at[2, b], partner)
+
+    for b in range(batch):
+        @pl.when(first_chip)
+        def _(b=b):
+            kv_to_chip(b).start()
+
+        @pl.when(first_core)
+        def _(b=b):
+            kv_to_partner(b).start()
+
+    def own_load(b, par):
+        return pltpu.make_async_copy(kv_hbm.at[:, row(b), :], kv_own.at[par], own_sem.at[par])
+
+    own_load(0, 0).start()
+
+    tile = n_in.shape[1]
+    tiles = batch * seq // tile
+
+    def tile_rows(t):
+        return pl.ds(pl.multiple_of(t * tile, tile), tile)
+
+    def tile_loads(t, par):
+        return [
+            pltpu.make_async_copy(n_hbm.at[tile_rows(t), :], n_in.at[par], tile_sem.at[par, 0]),
+            pltpu.make_async_copy(dy_hbm.at[tile_rows(t), :], dy_in.at[par], tile_sem.at[par, 1]),
+        ]
+
+    for copy in tile_loads(0, 0):
+        copy.start()
+
+    def project(t, carry):
+        par = lax.rem(t, 2)
+        for copy in tile_loads(t, par):
+            copy.wait()
+
+        @pl.when(t + 1 < tiles)
+        def _():
+            for copy in tile_loads(t + 1, 1 - par):
+                copy.start()
+
+        rows = tile_rows(t)
+        put_rope(q_all.at[rows, :], dot_nn(n_in[par], wq_ref[...]), cos_ref[rows, :], sin_ref[rows, :])
+        do_all[rows, :] = dot_nt(dy_in[par], wo_ref[...]).astype(BF16)
+        return carry
+
+    lax.fori_loop(0, tiles, project, 0)
+
+    def o_local_copy(b):
+        return pltpu.make_async_copy(o_buf.at[b], o_all.at[z, row(b), :], o_local.at[b])
+
+    def o_copy(b, k, step):
+        return remote(o_buf.at[b], o_all.at[z, row(b), :], o_send.at[k, b], o_recv.at[z, b], {"tp": jnp.clip(z + step, 0, tp - 1)})
+
+    hops = [(k, step, jnp.logical_and(z + step >= 0, z + step < tp)) for k, step in enumerate((1, -1, 2, -2))]
+
+    def o_start(b):
+        o_local_copy(b).start()
+        for k, step, ok in hops:
+            @pl.when(ok)
+            def _(k=k, step=step):
+                o_copy(b, k, step).start()
+
+    def o_arrived(src, b):
+        remote(o_all.at[src, row(b), :], o_all.at[src, row(b), :], relay_send.at[b], o_recv.at[src, b], partner).wait_recv()
+
+    def relay_copy(b, src, dst):
+        return remote(o_all.at[src, row(b), :], o_all.at[src, row(b), :], relay_send.at[b], o_recv.at[src, b], {"tp": dst})
+
+    def relay(b):
+        @pl.when(z == tp - 2)
+        def _():
+            o_arrived(0, b)
+            relay_copy(b, 0, tp - 1).start()
+
+        @pl.when(z == 1)
+        def _():
+            o_arrived(tp - 1, b)
+            relay_copy(b, tp - 1, 0).start()
+
+    def far_copy(b, par):
+        return remote(g_far.at[par], xin.at[b], far_send.at[par], x_recv.at[b], partner)
+
+    def part_copy(b, par):
+        return remote(g_part.at[par], part_in.at[b], part_send.at[par], part_recv.at[b], partner)
+
+    def chip_copy(b):
+        par = lax.rem(b, CHIP_BUFS)
+        return remote(g_chip.at[par], xin.at[b], chip_send.at[par], x_recv.at[b], peer)
+
+    def chip_sum(b):
+        @pl.when(second_chip)
+        def _():
+            par = lax.rem(b, CHIP_BUFS)
+            far_copy(b, 0).wait_recv()
+            g_chip[par] = (g_chip[par].astype(F32) + xin[b].astype(F32)).astype(BF16)
+            chip_copy(b).start()
+
+    def dkv_store(b, par):
+        return pltpu.make_async_copy(dkv_out.at[par], dkv_hbm.at[:, row(b), :], dkv_sem.at[par])
+
+    def key_grads(b):
+        par = lax.rem(b, 2)
+
+        @pl.when(first_core)
+        def _():
+            part_copy(b, 0).wait_recv()
+
+        @pl.when(first_chip)
+        def _():
+            chip_copy(b).wait_recv()
+
+        @pl.when(b >= 2)
+        def _():
+            dkv_store(b - 2, par).wait()
+
+        rows = row(b)
+        for which in range(2):
+            for h in range(heads):
+                cols = slice(h * HEAD_DIM, (h + 1) * HEAD_DIM)
+                acc = g_own[b, which, :, cols].astype(F32)
+                acc = acc + jnp.where(first_core, part_in[b, which, :, cols].astype(F32), 0.0)
+                acc = (acc + jnp.where(first_chip, xin[b, which, :, cols].astype(F32), 0.0)).astype(BF16)
+                if which == 0:
+                    acc = rope(acc.astype(F32), cos_ref[rows, :], sin_ref[rows, :], -1.0).astype(BF16)
+                dkv_out[par, which, :, cols] = acc
+        dkv_store(b, par).start()
+
+    def dq_store(b, par):
+        return pltpu.make_async_copy(dq_buf.at[par], dq_hbm.at[row(b), :], dq_sem.at[par])
+
+    subs = range(0, seq, SUB)
+
+    def attend_row(i, par):
+        rows = row(i)
+        start = start_ref[i]
+        chip_par = lax.rem(i, CHIP_BUFS)
+        keys_of = [kv_own.at[par]] + [kvr.at[s, i] for s in range(3)]
+        grads = [g_own.at[i], g_part.at[par], g_chip.at[chip_par], g_far.at[par]]
+        live = [None, second_core, second_chip, second_chip]
+        piece = [r, r + 1 - 2 * core, r + 2 - 4 * chip, r + 3 - 2 * core - 4 * chip]
+
+        def each(body):
+            body(0)
+            for slot in (1, 2, 3):
+                pl.when(live[slot])(functools.partial(body, slot))
+
+        def one_head(h, carry):
+            cols = pl.ds(pl.multiple_of(h * HEAD_DIM, HEAD_DIM), HEAD_DIM)
+            q = q_all[rows, cols]
+            do = do_all[rows, cols]
+            m_scr[...] = jnp.full(m_scr.shape, NEG_BIG, F32)
+            l_scr[...] = jnp.zeros_like(l_scr)
+            d_scr[...] = jnp.zeros_like(d_scr)
+            ot_scr[...] = jnp.zeros_like(ot_scr)
+            dqt_scr[...] = jnp.zeros_like(dqt_scr)
+
+            def scores(slot):
+                base = piece[slot] * seq
+                for s in subs:
+                    raw = dot_nt(keys_of[slot][0, s:s + SUB, cols], q)
+                    local = lax.broadcasted_iota(jnp.int32, raw.shape, 0) + s
+                    allowed = (local + base) >= start
+                    if slot == 0:
+                        allowed = jnp.logical_and(allowed, local <= lax.broadcasted_iota(jnp.int32, raw.shape, 1))
+                    raw = jnp.where(allowed, raw, NEG_BIG)
+                    s_scr[slot, s:s + SUB, :] = raw
+                    m_scr[...] = jnp.maximum(m_scr[...], jnp.max(raw, axis=0, keepdims=True))
+
+            def exps(slot):
+                for s in subs:
+                    e = jnp.exp2((s_scr[slot, s:s + SUB, :] - m_scr[...]) * EXP2_SCALE)
+                    s_scr[slot, s:s + SUB, :] = e
+                    l_scr[...] += jnp.sum(e, axis=0, keepdims=True)
+
+            def values(slot):
+                for s in subs:
+                    v = keys_of[slot][1, s:s + SUB, cols]
+                    prob = s_scr[slot, s:s + SUB, :] * l_scr[...]
+                    low = prob.astype(BF16)
+                    dp = dot_nt(v, do)
+                    s_scr[slot, s:s + SUB, :] = prob
+                    dp_scr[slot, s:s + SUB, :] = dp
+                    d_scr[...] += jnp.sum(prob * dp, axis=0, keepdims=True)
+                    grads[slot][1, s:s + SUB, cols] = dot_nn(low, do).astype(BF16)
+                    ot_scr[...] += dot_nn(v.T, low)
+
+            def keys(slot):
+                for s in subs:
+                    k = keys_of[slot][0, s:s + SUB, cols]
+                    ds = (s_scr[slot, s:s + SUB, :] * (dp_scr[slot, s:s + SUB, :] - d_scr[...])).astype(BF16)
+                    grads[slot][0, s:s + SUB, cols] = (dot_nn(ds, q) * SCALE).astype(BF16)
+                    dqt_scr[...] += dot_nn(k.T, ds)
+
+            each(scores)
+            each(exps)
+            l_scr[...] = 1.0 / l_scr[...]
+            each(values)
+            each(keys)
+            o_buf[i, :, cols] = ot_scr[...].T.astype(BF16)
+            dq_buf[par, :, cols] = rope(dqt_scr[...].T * SCALE, cos_ref[rows, :], sin_ref[rows, :], -1.0).astype(BF16)
+            return carry
+
+        lax.fori_loop(0, heads, one_head, 0)
+
+    def step(i, carry):
+        par = lax.rem(i, 2)
+        own_load(i, par).wait()
+
+        @pl.when(i + 1 < batch)
+        def _():
+            own_load(i + 1, 1 - par).start()
+
+        @pl.when(second_chip)
+        def _():
+            kv_to_chip(i).wait_recv()
+            kv_forward(i).start()
+
+        @pl.when(second_core)
+        def _():
+            kv_to_partner(i).wait_recv()
+
+        @pl.when(second_chip)
+        def _():
+            kv_forward(i).wait_recv()
+
+        @pl.when(i >= 2)
+        def _():
+            dq_store(i - 2, par).wait()
+
+            @pl.when(second_core)
+            def _():
+                part_copy(i - 2, par).wait_send()
+
+            @pl.when(second_chip)
+            def _():
+                far_copy(i - 2, par).wait_send()
+
+        @pl.when(jnp.logical_and(second_chip, i >= CHIP_BUFS))
+        def _():
+            chip_copy(i - CHIP_BUFS).wait_send()
+
+        attend_row(i, par)
+        o_start(i)
+        dq_store(i, par).start()
+
+        @pl.when(second_chip)
+        def _():
+            far_copy(i, par).start()
+
+        @pl.when(second_core)
+        def _():
+            part_copy(i, par).start()
+
+        @pl.when(i >= 1)
+        def _():
+            chip_sum(i - 1)
+
+        @pl.when(i >= RELAY_LAG)
+        def _():
+            relay(i - RELAY_LAG)
+
+        return carry
+
+    lax.fori_loop(0, batch, step, 0)
+    chip_sum(batch - 1)
+    lag = min(RELAY_LAG, batch)
+    for k in range(lag):
+        relay(batch - lag + k)
+
+    def finish(b, carry):
+        key_grads(b)
+        return carry
+
+    lax.fori_loop(0, batch, finish, 0)
+
+    for b in range(batch):
+        @pl.when(first_chip)
+        def _(b=b):
+            kv_to_chip(b).wait_send()
+
+        @pl.when(first_core)
+        def _(b=b):
+            kv_to_partner(b).wait_send()
+
+        @pl.when(second_chip)
+        def _(b=b):
+            kv_forward(b).wait_send()
+
+        o_local_copy(b).wait()
+        for k, step_, ok in hops:
+            @pl.when(ok)
+            def _(b=b, k=k, step_=step_):
+                o_copy(b, k, step_).wait_send()
+
+        @pl.when(jnp.logical_or(z == 1, z == tp - 2))
+        def _(b=b):
+            relay_copy(b, 0, tp - 1).wait_send()
+
+        for src in range(tp):
+            taken = jnp.logical_or(jnp.logical_and(z == tp - 2, src == 0), jnp.logical_and(z == 1, src == tp - 1))
+
+            @pl.when(jnp.logical_and(z != src, jnp.logical_not(taken)))
+            def _(b=b, src=src):
+                o_arrived(src, b)
+
+    for b in range(max(0, batch - 2), batch):
+        dq_store(b, b % 2).wait()
+        dkv_store(b, b % 2).wait()
+
+        @pl.when(second_core)
+        def _(b=b):
+            part_copy(b, b % 2).wait_send()
+
+        @pl.when(second_chip)
+        def _(b=b):
+            far_copy(b, b % 2).wait_send()
+
+    for b in range(max(0, batch - CHIP_BUFS), batch):
+        @pl.when(second_chip)
+        def _(b=b):
+            chip_copy(b).wait_send()
+
+
+def front(kv, normed, dy, cos_t, sin_t, start, wq, wo, seq, tp, cp):
+    _, tokens, hidden = kv.shape
+    d_model = normed.shape[1]
+    batch = tokens // seq
+    tile = seq // 2
+    hbm = pl.BlockSpec(memory_space=pl.ANY)
+    vmem = pl.BlockSpec(memory_space=pltpu.VMEM)
+    dma = pltpu.SemaphoreType.DMA
+    bf = lambda *shape: pltpu.VMEM(shape, BF16)
+    f32 = lambda *shape: pltpu.VMEM(shape, F32)
+    return pl.pallas_call(
+        functools.partial(front_kernel, batch, seq, tp, cp),
+        in_specs=[hbm] * 3 + [vmem] * 5,
+        out_specs=[hbm] * 3,
         out_shape=[
-            jax.ShapeDtypeStruct((tokens, d_model), BF16),
+            jax.ShapeDtypeStruct((tp, tokens, hidden), BF16),
             jax.ShapeDtypeStruct((tokens, hidden), BF16),
             jax.ShapeDtypeStruct((2, tokens, hidden), BF16),
-            jax.ShapeDtypeStruct((tokens, hidden), BF16),
         ],
-        compiler_params=pltpu.CompilerParams(dimension_semantics=("arbitrary",), vmem_limit_bytes=60 << 20),
-        cost_estimate=pl.CostEstimate(flops=8 * tokens * d_model * hidden, bytes_accessed=8 * tokens * d_model + 8 * d_model * hidden, transcendentals=0),
-        name="project",
-    )(x, dy, cos_t, sin_t, gain, wq, wk, wv, wo)
-
-
-SUB = 128
-ROWS = 48
-
-
-def attn_kernel(info_ref, start_ref, cos_ref, sin_ref, q_ref, do_ref, kv0_ref, kv1_ref, kv2_ref, kv3_ref,
-                o_ref, dq_ref, g0_ref, g1_ref, g2_ref, g3_ref, s_scr, dp_scr, m_scr, l_scr, d_scr, ot_scr, dqt_scr):
-    b = pl.program_id(0)
-    rank = info_ref[0]
-    first = info_ref[1 + b]
-    seq = q_ref.shape[0]
-    kvs = (kv0_ref, kv1_ref, kv2_ref, kv3_ref)
-    grads = (g0_ref, g1_ref, g2_ref, g3_ref)
-    q = q_ref[...]
-    do = do_ref[...]
-    start = start_ref[0]
-    subs = range(0, seq, SUB)
-
-    def piece_of(slot):
-        return rank ^ slot if slot else rank
-
-    def live(slot):
-        piece = piece_of(slot)
-        return jnp.logical_and(piece < rank, first < (piece + 1) * seq)
-
-    def each(body):
-        body(0)
-        for slot in (1, 2, 3):
-            pl.when(live(slot))(functools.partial(body, slot))
-
-    m_scr[...] = jnp.full(m_scr.shape, NEG_BIG, F32)
-    l_scr[...] = jnp.zeros_like(l_scr)
-    d_scr[...] = jnp.zeros_like(d_scr)
-    ot_scr[...] = jnp.zeros_like(ot_scr)
-    dqt_scr[...] = jnp.zeros_like(dqt_scr)
-
-    def scores(slot):
-        base = piece_of(slot) * seq
-        for s in subs:
-            raw = dot_nt(kvs[slot][0, s:s + SUB, :], q)
-            local = lax.broadcasted_iota(jnp.int32, raw.shape, 0) + s
-            allowed = (local + base) >= start
-            if slot == 0:
-                allowed = jnp.logical_and(allowed, local <= lax.broadcasted_iota(jnp.int32, raw.shape, 1))
-            raw = jnp.where(allowed, raw, NEG_BIG)
-            s_scr[slot, s:s + SUB, :] = raw
-            m_scr[...] = jnp.maximum(m_scr[...], jnp.max(raw, axis=0, keepdims=True))
-
-    each(scores)
-
-    def exps(slot):
-        for s in subs:
-            e = jnp.exp2((s_scr[slot, s:s + SUB, :] - m_scr[...]) * EXP2_SCALE)
-            s_scr[slot, s:s + SUB, :] = e
-            l_scr[...] += jnp.sum(e, axis=0, keepdims=True)
-
-    each(exps)
-    l_scr[...] = 1.0 / l_scr[...]
-
-    def values(slot):
-        for s in subs:
-            v = kvs[slot][1, s:s + SUB, :]
-            prob = s_scr[slot, s:s + SUB, :] * l_scr[...]
-            low = prob.astype(BF16)
-            dp = dot_nt(v, do)
-            s_scr[slot, s:s + SUB, :] = prob
-            dp_scr[slot, s:s + SUB, :] = dp
-            d_scr[...] += jnp.sum(prob * dp, axis=0, keepdims=True)
-            grads[slot][1, s:s + SUB, :] = dot_nn(low, do).astype(BF16)
-            ot_scr[...] += dot_nn(v.T, low)
-
-    each(values)
-
-    def keys(slot):
-        for s in subs:
-            k = kvs[slot][0, s:s + SUB, :]
-            ds = (s_scr[slot, s:s + SUB, :] * (dp_scr[slot, s:s + SUB, :] - d_scr[...])).astype(BF16)
-            grads[slot][0, s:s + SUB, :] = (dot_nn(ds, q) * SCALE).astype(BF16)
-            dqt_scr[...] += dot_nn(k.T, ds)
-
-    each(keys)
-    for slot in (1, 2, 3):
-        @pl.when(jnp.logical_not(live(slot)))
-        def _(slot=slot):
-            grads[slot][...] = jnp.zeros_like(grads[slot])
-
-    o_ref[...] = ot_scr[...].T.astype(BF16)
-    dq = dqt_scr[...].T * SCALE
-    dq_ref[...] = rope(dq, cos_ref[...], sin_ref[...], -1.0).astype(BF16)
-
-
-def attend(info, start, cos_t, sin_t, q, do, kvs, seq):
-    tokens, hidden = q.shape
-    batch, heads = tokens // seq, hidden // HEAD_DIM
-    tile = pl.BlockSpec((seq, HEAD_DIM), lambda b, h, _: (b, h))
-    table = pl.BlockSpec((seq, HEAD_DIM), lambda b, h, _: (b, 0))
-    pair = pl.BlockSpec((2, seq, HEAD_DIM), lambda b, h, _: (0, b, h))
-    return pl.pallas_call(
-        attn_kernel,
-        grid_spec=pltpu.PrefetchScalarGridSpec(
-            num_scalar_prefetch=1,
-            grid=(batch, heads),
-            in_specs=[pl.BlockSpec((1, 1, seq), lambda b, h, _: (b, 0, 0)), table, table, tile, tile, pair, pair, pair, pair],
-            out_specs=[tile, tile, pair, pair, pair, pair],
-            scratch_shapes=[
-                pltpu.VMEM((4, seq, seq), F32),
-                pltpu.VMEM((4, seq, seq), F32),
-                pltpu.VMEM((1, seq), F32),
-                pltpu.VMEM((1, seq), F32),
-                pltpu.VMEM((1, seq), F32),
-                pltpu.VMEM((HEAD_DIM, seq), F32),
-                pltpu.VMEM((HEAD_DIM, seq), F32),
-            ],
-        ),
-        out_shape=[jax.ShapeDtypeStruct((tokens, hidden), BF16)] * 2 + [jax.ShapeDtypeStruct((2, tokens, hidden), BF16)] * 4,
-        compiler_params=pltpu.CompilerParams(dimension_semantics=("arbitrary", "arbitrary"), vmem_limit_bytes=48 << 20),
-        cost_estimate=pl.CostEstimate(flops=48 * tokens * seq * hidden, bytes_accessed=36 * tokens * hidden, transcendentals=4 * tokens * seq * heads),
-        name="attend",
-    )(info, start, cos_t, sin_t, q, do, *kvs)
-
-
-MESH = pl.DeviceIdType.MESH
+        scratch_shapes=[
+            bf(tokens, hidden), bf(tokens, hidden), bf(2, tile, d_model), bf(2, tile, d_model),
+            bf(2, 2, seq, hidden), bf(3, batch, 2, seq, hidden),
+            f32(4, seq, seq), f32(4, seq, seq), f32(1, seq), f32(1, seq), f32(1, seq), f32(HEAD_DIM, seq), f32(HEAD_DIM, seq),
+            bf(batch, seq, hidden), bf(2, seq, hidden),
+            bf(batch, 2, seq, hidden), bf(2, 2, seq, hidden), bf(CHIP_BUFS, 2, seq, hidden), bf(2, 2, seq, hidden),
+            bf(batch, 2, seq, hidden), bf(batch, 2, seq, hidden), bf(2, 2, seq, hidden),
+            dma((2, 2)), dma((2,)), dma((batch,)), dma((batch,)), dma((batch,)), dma((3, batch)),
+            dma((batch,)), dma((4, batch)), dma((tp, batch)), dma((batch,)), dma((2,)),
+            dma((2,)), dma((2,)), dma((CHIP_BUFS,)), dma((batch,)), dma((batch,)), dma((2,)),
+        ],
+        compiler_params=pltpu.CompilerParams(collective_id=1, has_side_effects=True, vmem_limit_bytes=63 << 20),
+        cost_estimate=pl.CostEstimate(flops=48 * tokens * seq * hidden, bytes_accessed=16 * tokens * d_model, transcendentals=4 * tokens * seq * (hidden // HEAD_DIM)),
+        name="front",
+    )(kv, normed, dy, cos_t, sin_t, start, wq, wo)
 
 
 def back_kernel(groups, rows, tp, cp, dq_hbm, dkv_hbm, x_hbm, dy_hbm, o_hbm, wq_ref, wk_ref, wv_ref, wo_ref, gain_ref,
@@ -350,10 +620,12 @@
     def project_out(cur, lo, hi):
         for c in range(lo, hi, chunk):
             cols = slice(c, c + chunk)
-            acc = dot_nn(o_in[cur, 0], wo_ref[0, :, cols])
-            for t in range(1, tp):
-                acc += dot_nn(o_in[cur, t], wo_ref[t, :, cols])
-            y_buf[cur, :, cols] = (x_in[cur, :, cols].astype(F32) + acc).astype(BF16)
+            shares, share = wo_ref.shape[0], wo_ref.shape[2]
+            acc = x_in[cur, :, cols].astype(F32)
+            for t in range(tp):
+                for g in range(shares):
+                    acc += dot_nn(o_in[cur, t, :, g * share:(g + 1) * share], wo_ref[g, t, :, cols])
+            y_buf[cur, :, cols] = acc.astype(BF16)
 
     def finalize(i, slot):
         mine = pl.ds(pl.multiple_of(z * rows, rows), rows)
@@ -528,10 +800,10 @@
         name="backward_norm",
     )(dq, dkv, x, dy, o_all, wq, wk, wv, wo_all, gain)
 
-
 def solution(mesh):
     cp_size = mesh.shape["cp"]
     tp_size = mesh.shape["tp"]
+    dp_size = mesh.shape["dp"]
 
     def device_step(x_in, segment_ids, positions, w_query, w_key, w_value, w_out, norm_gain, grad_out):
         batch, seq, d_model = x_in.shape
@@ -546,35 +818,20 @@
         angles = positions.reshape(tokens, 1).astype(F32) * jnp.repeat(inv_freq, 2)[None, :]
         cos_t, sin_t = jnp.cos(angles), jnp.sin(angles)
         start = (rank * seq + jnp.arange(seq, dtype=jnp.int32))[None, :] - positions
-        info = jnp.concatenate([jnp.full((1,), rank, jnp.int32), start[:, 0]])
-
-        w_all = lax.all_gather(w_out, "tp", axis=0)
+
+        share = w_out.shape[0] // (cp_size * dp_size)
+        mine = (lax.axis_index("dp") * cp_size + rank) * share
+        w_all = lax.all_gather(lax.dynamic_slice(w_out, (mine, 0), (share, d_model)), ("dp", "tp", "cp"), axis=0)
+        w_all = w_all.reshape(dp_size, tp_size, cp_size * share, d_model)
+
         rows = min(384, tokens)
-        normed, q, kv, do = project(x, dy, cos_t, sin_t, norm_gain.reshape(1, d_model), w_query, w_key, w_value, w_out, rows)
+        normed, kv = project_keys(x, cos_t, sin_t, norm_gain.reshape(1, d_model), w_key, w_value, rows)
+        o_all, dq, dkv = front(kv, normed, dy, cos_t, sin_t, start.reshape(batch, 1, seq), w_query, w_out, seq, tp_size, cp_size)
+        grad_x, y_out, grad_gain = backward_norm(dq, dkv, x, dy, o_all, w_query, w_key, w_value, w_all, norm_gain.reshape(1, d_model), ROWS, tp_size, cp_size)
+        grad_gain = grad_gain.reshape(d_model)
 
         def perm(value, pairs):
             return lax.ppermute(value, "cp", pairs)
-
-        from_chip = perm(kv, [(0, 2), (1, 3)])
-        from_partner = perm(kv, [(0, 1), (2, 3)])
-        from_far = perm(from_chip, [(2, 3), (3, 2)])
-        o, dq, g_own, g_partner, g_chip, g_far = attend(info, start.reshape(batch, 1, seq), cos_t, sin_t, q, do, (kv, from_partner, from_chip, from_far), seq)
-        o_all = lax.all_gather(o, "tp", axis=0)
-
-        far_sum = perm(g_far, [(2, 3), (3, 2)])
-        chip_sum = (g_chip.astype(F32) + far_sum.astype(F32)).astype(BF16)
-        partner_in = perm(g_partner, [(1, 0), (3, 2)])
-        chip_in = perm(chip_sum, [(2, 0), (3, 1)])
-        dkv_sum = (g_own.astype(F32) + partner_in.astype(F32) + chip_in.astype(F32)).astype(BF16)
-        dk_f32 = dkv_sum[0].astype(F32)
-        lane = lax.broadcasted_iota(jnp.int32, (tokens, hidden), 1)
-        swapped = jnp.where(lane % 2 == 0, jnp.roll(dk_f32, -1, 1), -jnp.roll(dk_f32, 1, 1))
-        wide = lambda t: jnp.tile(t, (1, hidden // HEAD_DIM))
-        dk = (dk_f32 * wide(cos_t) + swapped * wide(sin_t)).astype(BF16)
-        dkv = jnp.stack([dk, dkv_sum[1]])
-
-        grad_x, y_out, grad_gain = backward_norm(dq, dkv, x, dy, o_all, w_query, w_key, w_value, w_all, norm_gain.reshape(1, d_model), ROWS, tp_size, cp_size)
-        grad_gain = grad_gain.reshape(d_model)
 
         def tn(a, b):
             return lax.dot_general(a, b, (((0,), (0,)), ((), ())), preferred_element_type=F32)
@@ -589,6 +846,7 @@
             rest = perm(total, [(0, 1), (1, 0), (2, 3), (3, 2)])
             return jnp.where(core == 0, jnp.concatenate([total, rest]), jnp.concatenate([rest, total]))
 
+        o = lax.dynamic_index_in_dim(o_all, lax.axis_index("tp"), 0, keepdims=False)
         grad_wo = reduce_cp(tn(o, dy))
         grad_wq = reduce_cp(tn(normed, dq))
         grad_wk = reduce_cp(tn(normed, dkv[0]))

time: 900 us -> 718 us (0.80)
  waiting for transfers between devices: 242 us -> 80.2 us
  Pallas kernels: 332 us -> 479 us
  starting transfers between devices: 114 us -> 26.8 us
  other arithmetic: 81.1 us -> 42.6 us
  local copies, waits for them, and re-layouts: 70.6 us -> 37.3 us
  matrix products: 38.9 us -> 28.4 us
    ppermute x18 -> x12, waiting for transfers between devices: 242 us -> 80.2 us  [perm(): return lax.ppermute(value, 'cp', pairs)]
    pallas_call x2, Pallas kernels: 74.1 us -> 220 us  [the longest x1 202 us: front(): pl.pallas_call(functools.partial(front_kernel, batch, seq, tp, cp), in_sp...]
    ppermute x18 -> x12, starting transfers between devices: 114 us -> 26.8 us  [perm(): return lax.ppermute(value, 'cp', pairs)]
    convert_element_type x5 -> x0, other arithmetic: 20.5 us -> none  [the longest x1 7.07 us: device_step(): (g_own.astype(F32) + partner_in.astype(F32) + chip_in.astype(F32)).astype...]
    another operation x4 -> x0, local copies, waits for them, and re-layouts: 17 us -> none  [device_step(): wide = lambda t: jnp.tile(t, (1, hidden // HEAD_DIM))]
    slice x3 -> x0, local copies, waits for them, and re-layouts: 14.5 us -> none  [the longest x2 14.4 us: device_step(): jnp.roll(dk_f32, 1, 1)]
    dot_general x4, matrix products: 38.9 us -> 28.4 us  [tn(): lax.dot_general(a, b, (((0,), (0,)), ((), ())), preferred_element_type=F32)]
    unnamed x55 -> x27, local copies, waits for them, and re-layouts: 30.9 us -> 27 us
  transfers between devices with their start and end apart: 20 -> 13, of which waited for: 5 -> 4; matrix products, arithmetic and copies ran while one was open for 16% -> 11% of each run, Pallas kernels for 34% -> 31%
where the time goes in v3:
time: 718 us; the launch traced here: 709 us
  Pallas kernels  479 us (67%)
  waiting for transfers between devices  80.2 us (11%)
  other arithmetic  42.6 us (6%)
  local copies, waits for them, and re-layouts  37.3 us (5%)
  matrix products  28.4 us (4%)
  starting transfers between devices  26.8 us (4%)
  between operations  14.7 us (2%)
    pallas_call x1, Pallas kernels, backward_norm(): pl.pallas_call(functools.partial(back_kernel, groups, rows, tp, cp), in_s...  259 us
    pallas_call x1, Pallas kernels, front(): pl.pallas_call(functools.partial(front_kernel, batch, seq, tp, cp), in_sp...  202 us
    ppermute x12, waiting for transfers between devices, perm(): return lax.ppermute(value, 'cp', pairs)  80.2 us
    dot_general x4, matrix products, tn(): lax.dot_general(a, b, (((0,), (0,)), ((), ())), preferred_element_type=F32)  28.4 us
    unnamed x27, local copies, waits for them, and re-layouts  27 us
    ppermute x12, starting transfers between devices, perm(): return lax.ppermute(value, 'cp', pairs)  26.8 us
    select_n x4, other arithmetic, reduce_cp(): jnp.where(core == 0, jnp.concatenate([total, rest]), jnp.concatenate([res...  24.9 us
    pallas_call x1, Pallas kernels, project_keys(): pl.pallas_call(keys_kernel, grid=(tokens // rows,), in_specs=[tile(d_mode...  18.6 us
  transfers between devices with their start and end apart: 13, of which 4 were waited for; matrix products, arithmetic and copies ran while one was open for 11% of the time, Pallas kernels for 31%

profile of v3, /device:TPU:0, one launch (start us, length us, event | category | flops | bytes accessed | tf_op | source)
XLA Modules:
  0.0 709.0 jit_solution(964559611234920412)
XLA Ops:
  7.2 1.7 constant_dynamic-slice_fusion.4
  9.2 0.8 broadcast_subtract_fusion
  10.0 4.1 multiply_sine_fusion
  14.1 1.6 copy-done.2
  15.7 0.7 copy-done.3
  16.4 18.6 %project_keys.1 = (bf16[2304,2048]{1,0:T(8,128)(2,1)}, bf16[2,2304,512]{2,1,0:T(8,128)(2,1)}) custom-call(bf16[2304,2048]{1,0:T(8,128)(2,1)} %bitcast.26, f32[2304,128]{1,0:T(8,128)S(1)} %get-tuple-element.24.cos_ref, f32[2304,128]{1,0:T(8,128)S(1)} %get-tuple-element.23.sin_ref, f32[1,2048]{1,0:T(1,128)S(1)} %bitcast.22, bf16[2048,512]{1,0:T(8,128)(2,1)S(1)} %copy-done.2, ...), custom_call_target="tpu_custom_call" | custom-call | flops 9663676416 | bytes 23592960 | tf_op jit(solution)/shard_map/project_keys/pallas_call | solution.py:67
  35.0 1.0 copy-done
  36.0 1.0 copy-done.1
  37.0 0.6 reshape.56.start_ref
  37.6 201.6 %front.1 = (bf16[4,2304,512]{2,1,0:T(8,128)(2,1)}, bf16[2304,512]{1,0:T(8,128)(2,1)}, bf16[2,2304,512]{2,1,0:T(8,128)(2,1)}) custom-call(bf16[2,2304,512]{2,1,0:T(8,128)(2,1)} %get-tuple-element.15.kv_hbm, bf16[2304,2048]{1,0:T(8,128)(2,1)} %get-tuple-element.16.n_hbm, bf16[2304,2048]{1,0:T(8,128)(2,1)} %bitcast.28, f32[2304,128]{1,0:T(8,128)} %copy-done.1, ...), custom_call_target="tpu_custom_call" | custom-call | flops 21743271936 | bytes 75497472 | tf_op jit(solution)/shard_map/front/pallas_call | solution.py:455
  239.2 8.5 %fusion.10 = f32[2048,512]{1,0:T(8,128)S(1)} fusion(bf16[2304,2048]{1,0:T(8,128)(2,1)} %get-tuple-element.16.n_hbm, bf16[2304,512]{1,0:T(8,128)(2,1)} %get-tuple-element.17.dq_hbm), kind=kOutput, calls=%fused_computation.32 | convolution fusion | flops 4831838208 | bytes 15990784 | tf_op jit(solution)/shard_map/dot_general | solution.py:837
  247.8 1.6 constant_dynamic-slice_fusion.3
  249.4 0.7 collective-permute-start
  250.1 0.3 copy-done.7
  250.4 5.1 fusion.4
  255.5 1.6 constant_dynamic-slice_fusion.2
  257.2 1.0 copy-done.6
  258.2 0.7 collective-permute-start.3
  258.9 5.1 fusion.2
  264.0 2.0 copy-done.4
  266.0 1.5 constant_dynamic-slice_fusion.1
  267.5 9.7 %fusion = f32[512,2048]{1,0:T(8,128)} fusion(bf16[2304,2048]{1,0:T(8,128)(2,1)} %bitcast.29, bf16[4,2304,512]{2,1,0:T(8,128)(2,1)} %get-tuple-element.19.o_hbm, s32[]{:T(128)S(6)} %select_n.63), kind=kOutput, calls=%fused_computation.4 | convolution fusion | flops 4831838208 | bytes 15990788 | tf_op jit(solution)/shard_map/dot_general | solution.py:837
  277.2 3.1 constant_dynamic-slice_fusion
  280.3 0.5 collective-permute-start.9
  280.8 2.7 add_convert_fusion.3
  283.6 22.3 %collective-permute-start.1 = (bf16[1024,512]{1,0:T(8,128)(2,1)S(1)}, bf16[1024,512]{1,0:T(8,128)(2,1)S(1)}, u32[]{:S(2)}, u32[]{:S(2)}) collective-permute-start(bf16[1024,512]{1,0:T(8,128)(2,1)S(1)} %add_convert_fusion.3), channel_id=1, source_target_pairs={{0,2},{2,0},{1,3},{3,1},{4,6},{6,4},{5,7},{7,5},{8,10},{10,8},{9,1... | collective-permute-start | bytes 3145736 | tf_op jit(solution)/shard_map/ppermute | solution.py:834
  305.9 2.6 add_convert_fusion.2
  308.5 0.3 collective-permute-start.4
  308.8 0.4 add_convert_fusion.1
  309.1 1.9 collective-permute-start.7
  311.0 1.9 add_convert_fusion
  312.9 0.3 collective-permute-start.10
  313.2 16.8 %collective-permute-done.1 = bf16[1024,512]{1,0:T(8,128)(2,1)S(1)} collective-permute-done((bf16[1024,512]{1,0:T(8,128)(2,1)S(1)}, bf16[1024,512]{1,0:T(8,128)(2,1)S(1)}, u32[]{:S(2)}, u32[]{:S(2)}) %collective-permute-start.1) | collective-permute-done | bytes 1048608 | tf_op jit(solution)/shard_map/ppermute | solution.py:834
  329.9 0.3 convert_add_fusion.3
  330.3 22.1 %collective-permute-done.4 = bf16[1024,512]{1,0:T(8,128)(2,1)S(1)} collective-permute-done((bf16[1024,512]{1,0:T(8,128)(2,1)S(1)}, bf16[1024,512]{1,0:T(8,128)(2,1)S(1)}, u32[]{:S(2)}, u32[]{:S(2)}) %collective-permute-start.4) | collective-permute-done | bytes 1048608 | tf_op jit(solution)/shard_map/ppermute | solution.py:834
  352.4 1.6 convert_add_fusion.2
  354.0 20.8 %collective-permute-done.7 = bf16[1024,512]{1,0:T(8,128)(2,1)S(1)} collective-permute-done((bf16[1024,512]{1,0:T(8,128)(2,1)S(1)}, bf16[1024,512]{1,0:T(8,128)(2,1)S(1)}, u32[]{:S(2)}, u32[]{:S(2)}) %collective-permute-start.7) | collective-permute-done | bytes 1048608 | tf_op jit(solution)/shard_map/ppermute | solution.py:834
  374.9 1.6 convert_add_fusion.1
  376.5 20.5 %collective-permute-done.10 = bf16[256,2048]{1,0:T(8,128)(2,1)S(1)} collective-permute-done((bf16[256,2048]{1,0:T(8,128)(2,1)S(1)}, bf16[256,2048]{1,0:T(8,128)(2,1)S(1)}, u32[]{:S(2)}, u32[]{:S(2)}) %collective-permute-start.10) | collective-permute-done | bytes 1048608 | tf_op jit(solution)/shard_map/ppermute | solution.py:834
  397.0 1.7 convert_add_fusion
  398.7 5.3 maximum_select_fusion
  403.9 6.5 maximum_select_fusion.1
  410.5 6.5 maximum_select_fusion.2
  417.0 6.6 maximum_select_fusion.3
  423.5 258.8 %backward_norm.1 = (bf16[2304,2048]{1,0:T(8,128)(2,1)}, bf16[2304,2048]{1,0:T(8,128)(2,1)}, f32[1,2048]{1,0:T(1,128)}) custom-call(bf16[2304,512]{1,0:T(8,128)(2,1)} %get-tuple-element.17.dq_hbm, bf16[2,2304,512]{2,1,0:T(8,128)(2,1)} %get-tuple-element.18.dkv_hbm, bf16[2304,2048]{1,0:T(8,128)(2,1)} %bitcast.27, bf16[2304,2048]{1,0:T(8,128)(2,1)} %bitcast.30, ...), custom_call_target="tpu_custom_call" | custom-call | flops 33822867456 | bytes 75497472 | tf_op jit(solution)/shard_map/backward_norm/pallas_call | solution.py:758
  682.4 9.4 %copy.18 = bf16[6,384,2048]{2,1,0:T(8,128)(2,1)} copy(bf16[6,384,2048]{2,1,0:T(8,128)(2,1)} %bitcast.24) | data formatting | bytes 18874368
  691.7 9.4 %copy.19 = bf16[6,384,2048]{2,1,0:T(8,128)(2,1)} copy(bf16[6,384,2048]{2,1,0:T(8,128)(2,1)} %bitcast.23) | data formatting | bytes 18874368
  701.1 0.6 copy.20
  (38 shorter events, 0.4 us)
Async XLA Ops:
  7.2 416.4 %all-gather.3.cloned.1.call-start = ((), (), s32[]{:S(2)}) async-start(), calls=%async_computation | async-start | bytes 8650752 | tf_op jit(solution)/shard_map/all_gather | solution.py:824
  14.1 1.6 copy-start.2
  15.7 0.7 copy-start.3
  35.0 1.0 copy-start
  36.0 1.0 copy-start.1
  239.2 11.2 %copy-start.10 = (bf16[2304,2048]{1,0:T(8,128)(2,1)S(1)}, bf16[2304,2048]{1,0:T(8,128)(2,1)}, u32[]{:S(2)}) copy-start(bf16[2304,2048]{1,0:T(8,128)(2,1)} %get-tuple-element.16.n_hbm) | copy-start | bytes 28311556
  239.2 11.2 %copy-start.11 = (bf16[2,2304,512]{2,1,0:T(8,128)(2,1)S(1)}, bf16[2,2304,512]{2,1,0:T(8,128)(2,1)}, u32[]{:S(2)}) copy-start(bf16[2,2304,512]{2,1,0:T(8,128)(2,1)} %get-tuple-element.18.dkv_hbm) | copy-start | bytes 14155780
  247.8 2.6 copy-start.7
  249.4 31.4 %collective-permute-start = (f32[1024,512]{1,0:T(8,128)}, f32[1024,512]{1,0:T(8,128)}, u32[]{:S(2)}, u32[]{:S(2)}) collective-permute-start(f32[1024,512]{1,0:T(8,128)} %constant_dynamic-slice_fusion.3), channel_id=1, source_target_pairs={{0,1},{1,0},{2,3},{3,2},{4,5},{5,4},{6,7},{7,6},{8,9},{9,8},{10,11... | collective-permute-start | bytes 6291464 | tf_op jit(solution)/shard_map/ppermute | solution.py:834
  255.5 2.6 copy-start.6
  258.2 47.7 %collective-permute-start.3 = (f32[1024,512]{1,0:T(8,128)}, f32[1024,512]{1,0:T(8,128)}, u32[]{:S(2)}, u32[]{:S(2)}) collective-permute-start(f32[1024,512]{1,0:T(8,128)} %constant_dynamic-slice_fusion.2), channel_id=1, source_target_pairs={{0,1},{1,0},{2,3},{3,2},{4,5},{5,4},{6,7},{7,6},{8,9},{9,8},{10,11... | collective-permute-start | bytes 6291464 | tf_op jit(solution)/shard_map/ppermute | solution.py:834
  264.0 2.0 copy-start.4
  267.5 41.2 %collective-permute-start.6 = (f32[1024,512]{1,0:T(8,128)}, f32[1024,512]{1,0:T(8,128)S(1)}, u32[]{:S(2)}, u32[]{:S(2)}) collective-permute-start(f32[1024,512]{1,0:T(8,128)} %constant_dynamic-slice_fusion.1), channel_id=1, source_target_pairs={{0,1},{1,0},{2,3},{3,2},{4,5},{5,4},{6,7},{7,6},{8,9},{9,8},{10,11... | collective-permute-start | bytes 6291464 | tf_op jit(solution)/shard_map/ppermute | solution.py:834
  280.3 30.7 %collective-permute-start.9 = (f32[256,2048]{1,0:T(8,128)}, f32[256,2048]{1,0:T(8,128)}, u32[]{:S(2)}, u32[]{:S(2)}) collective-permute-start(f32[256,2048]{1,0:T(8,128)} %constant_dynamic-slice_fusion), channel_id=1, source_target_pairs={{0,1},{1,0},{2,3},{3,2},{4,5},{5,4},{6,7},{7,6},{8,9},{9,8},{10,11... | collective-permute-start | bytes 6291464 | tf_op jit(solution)/shard_map/ppermute | solution.py:834
  280.8 27.9 %copy-start.5 = (f32[2048,512]{1,0:T(8,128)S(1)}, f32[2048,512]{1,0:T(8,128)}, u32[]{:S(2)}) copy-start(f32[2048,512]{1,0:T(8,128)} %copy-done.4) | copy-start | bytes 12582916
  283.6 27.4 %copy-start.8 = (f32[512,2048]{1,0:T(8,128)S(1)}, f32[512,2048]{1,0:T(8,128)}, u32[]{:S(2)}) copy-start(f32[512,2048]{1,0:T(8,128)} %fusion) | copy-start | bytes 12582916
  283.6 46.3 %collective-permute-start.1 = (bf16[1024,512]{1,0:T(8,128)(2,1)S(1)}, bf16[1024,512]{1,0:T(8,128)(2,1)S(1)}, u32[]{:S(2)}, u32[]{:S(2)}) collective-permute-start(bf16[1024,512]{1,0:T(8,128)(2,1)S(1)} %add_convert_fusion.3), channel_id=1, source_target_pairs={{0,2},{2,0},{1,3},{3,1},{4,6},{6,4},{5,7},{7,5},{8,10},{10,8},{9,1... | collective-permute-start | bytes 3145736 | tf_op jit(solution)/shard_map/ppermute | solution.py:834
  308.5 43.9 %collective-permute-start.4 = (bf16[1024,512]{1,0:T(8,128)(2,1)S(1)}, bf16[1024,512]{1,0:T(8,128)(2,1)S(1)}, u32[]{:S(2)}, u32[]{:S(2)}) collective-permute-start(bf16[1024,512]{1,0:T(8,128)(2,1)S(1)} %add_convert_fusion.2), channel_id=1, source_target_pairs={{0,2},{2,0},{1,3},{3,1},{4,6},{6,4},{5,7},{7,5},{8,10},{10,8},{9,1... | collective-permute-start | bytes 3145736 | tf_op jit(solution)/shard_map/ppermute | solution.py:834
  309.1 65.8 %collective-permute-start.7 = (bf16[1024,512]{1,0:T(8,128)(2,1)S(1)}, bf16[1024,512]{1,0:T(8,128)(2,1)S(1)}, u32[]{:S(2)}, u32[]{:S(2)}) collective-permute-start(bf16[1024,512]{1,0:T(8,128)(2,1)S(1)} %add_convert_fusion.1), channel_id=1, source_target_pairs={{0,2},{2,0},{1,3},{3,1},{4,6},{6,4},{5,7},{7,5},{8,10},{10,8},{9,1... | collective-permute-start | bytes 3145736 | tf_op jit(solution)/shard_map/ppermute | solution.py:834
  312.9 84.1 %collective-permute-start.10 = (bf16[256,2048]{1,0:T(8,128)(2,1)S(1)}, bf16[256,2048]{1,0:T(8,128)(2,1)S(1)}, u32[]{:S(2)}, u32[]{:S(2)}) collective-permute-start(bf16[256,2048]{1,0:T(8,128)(2,1)S(1)} %add_convert_fusion), channel_id=1, source_target_pairs={{0,2},{2,0},{1,3},{3,1},{4,6},{6,4},{5,7},{7,5},{8,10},{10,8},{9,1... | collective-permute-start | bytes 3145736 | tf_op jit(solution)/shard_map/ppermute | solution.py:834
  330.2 68.4 %collective-permute-start.2 = (f32[1024,512]{1,0:T(8,128)S(1)}, f32[1024,512]{1,0:T(8,128)}, u32[]{:S(2)}, u32[]{:S(2)}) collective-permute-start(f32[1024,512]{1,0:T(8,128)S(1)} %convert_add_fusion.3), channel_id=1, source_target_pairs={{0,1},{1,0},{2,3},{3,2},{4,5},{5,4},{6,7},{7,6},{8,9},{9,8},{10,11... | collective-permute-start | bytes 6291464 | tf_op jit(solution)/shard_map/ppermute | solution.py:834
  354.0 49.9 %collective-permute-start.5 = (f32[1024,512]{1,0:T(8,128)}, f32[1024,512]{1,0:T(8,128)}, u32[]{:S(2)}, u32[]{:S(2)}) collective-permute-start(f32[1024,512]{1,0:T(8,128)} %convert_add_fusion.2), channel_id=1, source_target_pairs={{0,1},{1,0},{2,3},{3,2},{4,5},{5,4},{6,7},{7,6},{8,9},{9,8},{10,11... | collective-permute-start | bytes 6291464 | tf_op jit(solution)/shard_map/ppermute | solution.py:834
  376.5 34.0 %collective-permute-start.8 = (f32[1024,512]{1,0:T(8,128)}, f32[1024,512]{1,0:T(8,128)}, u32[]{:S(2)}, u32[]{:S(2)}) collective-permute-start(f32[1024,512]{1,0:T(8,128)} %convert_add_fusion.1), channel_id=1, source_target_pairs={{0,1},{1,0},{2,3},{3,2},{4,5},{5,4},{6,7},{7,6},{8,9},{9,8},{10,11... | collective-permute-start | bytes 6291464 | tf_op jit(solution)/shard_map/ppermute | solution.py:834
  398.7 18.3 %collective-permute-start.11 = (f32[256,2048]{1,0:T(8,128)}, f32[256,2048]{1,0:T(8,128)}, u32[]{:S(2)}, u32[]{:S(2)}) collective-permute-start(f32[256,2048]{1,0:T(8,128)} %convert_add_fusion), channel_id=1, source_target_pairs={{0,1},{1,0},{2,3},{3,2},{4,5},{5,4},{6,7},{7,6},{8,9},{9,8},{10,11... | collective-permute-start | bytes 6291464 | tf_op jit(solution)/shard_map/ppermute | solution.py:834
  691.7 9.4 %copy-start.9 = (f32[1,2048]{1,0:T(1,128)S(1)}, f32[1,2048]{1,0:T(1,128)}, u32[]{:S(2)}) copy-start(f32[1,2048]{1,0:T(1,128)} %get-tuple-element.22) | copy-start | bytes 24580
Sparse Core Ops, SparseCore 0:
  10.8 86.9 all-gather.2

commit v4 on v3

--- a/solution.py
+++ b/solution.py
@@ -79,6 +79,7 @@
 MESH = pl.DeviceIdType.MESH
 SUB = 128
 ROWS = 48
+WIDTH = 256
 RELAY_LAG = 2
 CHIP_BUFS = 3
 
@@ -478,16 +479,40 @@
     )(kv, normed, dy, cos_t, sin_t, start, wq, wo)
 
 
-def back_kernel(groups, rows, tp, cp, dq_hbm, dkv_hbm, x_hbm, dy_hbm, o_hbm, wq_ref, wk_ref, wv_ref, wo_ref, gain_ref,
-                gx_hbm, y_hbm, gg_ref, part, rs_r, rs_l, send_r, send_l, tot, gx_buf, dq_in, dkv_in, o_in, x_in, dy_in, y_buf, gain_all,
-                in_sem, y_sem, own_sem, rss_r, rss_l, rsr_r, rsr_l, ag0_r, ag0_l, agf_r, agf_l, agr_r, agr_l, gs_sem, gr_sem):
+PART_RING = 4
+RS_RING = 5
+
+
+def back_kernel(groups, rows, tp, cp, dq_hbm, dkv_hbm, x_hbm, dy_hbm, o_hbm, n_hbm, wq_hbm, wk_hbm, wv_hbm, wo_hbm, gain_ref,
+                gx_hbm, y_hbm, ga_hbm, gb_hbm, gg_ref,
+                wq_ref, wk_ref, wv_ref, wo_ref, dq_all, dkv_all, o_t, part, rs_r, rs_l, send_r, send_l, tot, gx_buf,
+                o_in, x_in, xo_in, dyo_in, y_buf, n_in, dy_in, away, part_in, mine, gain_all,
+                w_sem, in_sem, fin_sem, job_sem, y_sem, own_sem, rss_r, rss_l, rsr_r, rsr_l, ag0_r, ag0_l, agf_r, agf_l, agr_r, agr_l,
+                away_send, away_recv, mine_own, mine_part, mine_chip, ga_recv, chip_recv, gb_send, gb_recv, gs_sem, gr_sem):
     z = lax.axis_index("tp")
     r = lax.axis_index("cp")
+    core = lax.rem(r, 2)
+    chip = lax.div(r, 2)
     last = tp - 1
     slots = tp - 1
     span = tp * rows
-    d_model = x_hbm.shape[1]
+    tokens, d_model = x_hbm.shape
+    hidden = dq_hbm.shape[1]
     chunk = min(512, d_model)
+    blocks = ga_hbm.shape[0]
+    width = ga_hbm.shape[1]
+    pairs = blocks // 2
+    partner = {"cp": r + 1 - 2 * core}
+    peer = {"cp": r + 2 - 4 * chip}
+
+    shares, share = wo_hbm.shape[0], wo_hbm.shape[2]
+    weight_loads = [pltpu.make_async_copy(src, dst, w_sem.at[k]) for k, (src, dst) in enumerate(((wq_hbm, wq_ref), (wk_hbm, wk_ref), (wv_hbm, wv_ref), (dq_hbm, dq_all), (dkv_hbm, dkv_all)))]
+    out_loads = [
+        pltpu.make_async_copy(wo_hbm.at[g, t], wo_ref.at[t, g * share:(g + 1) * share, :], w_sem.at[5 + g * tp + t])
+        for g in range(shares) for t in range(tp)
+    ]
+    for copy in weight_loads:
+        copy.start()
 
     barrier = pltpu.get_barrier_semaphore()
     peers = [(dt, dc) for dt in range(tp) for dc in range(cp) if dt or dc]
@@ -498,10 +523,8 @@
     def remote(src, dst, ssem, rsem, dev):
         return pltpu.make_async_remote_copy(src_ref=src, dst_ref=dst, send_sem=ssem, recv_sem=rsem, device_id=dev, device_id_type=MESH)
 
-    def move(dir_right):
-        return {"tp": jnp.where(z < last, z + 1, z)} if dir_right else {"tp": jnp.where(z > 0, z - 1, z)}
-
-    right, left = move(True), move(False)
+    right = {"tp": jnp.where(z < last, z + 1, z)}
+    left = {"tp": jnp.where(z > 0, z - 1, z)}
 
     def group_rows(i):
         return pl.ds(pl.multiple_of(i * span, span), span)
@@ -512,45 +535,51 @@
     def inputs(i, slot):
         g = group_rows(i)
         return [
-            pltpu.make_async_copy(dq_hbm.at[g, :], dq_in.at[slot], in_sem.at[slot, 0]),
-            pltpu.make_async_copy(dkv_hbm.at[:, g, :], dkv_in.at[slot], in_sem.at[slot, 1]),
-            pltpu.make_async_copy(o_hbm.at[:, g, :], o_in.at[slot], in_sem.at[slot, 2]),
-            pltpu.make_async_copy(x_hbm.at[g, :], x_in.at[slot], in_sem.at[slot, 3]),
-            pltpu.make_async_copy(dy_hbm.at[tile_rows(i, z), :], dy_in.at[slot], in_sem.at[slot, 4]),
+            pltpu.make_async_copy(o_hbm.at[:, g, :], o_in.at[slot], in_sem.at[slot, 0]),
+            pltpu.make_async_copy(x_hbm.at[g, :], x_in.at[slot], in_sem.at[slot, 1]),
+        ]
+
+    def final_inputs(i, slot):
+        g = tile_rows(i, z)
+        return [
+            pltpu.make_async_copy(x_hbm.at[g, :], xo_in.at[slot], fin_sem.at[slot, 0]),
+            pltpu.make_async_copy(dy_hbm.at[g, :], dyo_in.at[slot], fin_sem.at[slot, 1]),
         ]
 
     def y_copy(i, slot):
         return pltpu.make_async_copy(y_buf.at[slot], y_hbm.at[group_rows(i), :], y_sem.at[slot])
 
     def rs_copy(i, s, to_right):
+        ring = lax.rem(i, RS_RING)
         if to_right:
-            return remote(send_r.at[s], rs_r.at[i, s], rss_r.at[s], rsr_r.at[i, s], right)
-        return remote(send_l.at[s], rs_l.at[i, s], rss_l.at[s], rsr_l.at[i, s], left)
-
-    def rs_send(i, cur, s):
+            return remote(send_r.at[s], rs_r.at[ring, s], rss_r.at[s], rsr_r.at[ring, s], right)
+        return remote(send_l.at[s], rs_l.at[ring, s], rss_l.at[s], rsr_l.at[ring, s], left)
+
+    def rs_send(i, s):
         for to_right in (True, False):
             far = z if to_right else last - z
             owner = (z + slots - s) if to_right else (z - slots + s)
             buf, held = (send_r, rs_r) if to_right else (send_l, rs_l)
 
-            @pl.when(jnp.logical_and(i < groups, jnp.logical_and(far <= s, far < last)))
+            @pl.when(jnp.logical_and(jnp.logical_and(i >= 0, i < groups), jnp.logical_and(far <= s, far < last)))
             def _(to_right=to_right, far=far, owner=owner, buf=buf, held=held):
                 @pl.when(i > 0)
                 def _():
                     rs_copy(i - 1, s, to_right).wait_send()
 
-                mine = pl.ds(pl.multiple_of(owner * rows, rows), rows)
+                cur = lax.rem(i, PART_RING)
+                own = pl.ds(pl.multiple_of(owner * rows, rows), rows)
                 if s == 0:
-                    buf[s] = part[cur, mine, :].astype(BF16)
+                    buf[s] = part[cur, own, :].astype(BF16)
                 else:
                     @pl.when(far == 0)
                     def _():
-                        buf[s] = part[cur, mine, :].astype(BF16)
+                        buf[s] = part[cur, own, :].astype(BF16)
 
                     @pl.when(far > 0)
                     def _():
                         rs_copy(i, s - 1, to_right).wait_recv()
-                        buf[s] = (part[cur, mine, :] + held[i, s - 1].astype(F32)).astype(BF16)
+                        buf[s] = (part[cur, own, :] + held[lax.rem(i, RS_RING), s - 1].astype(F32)).astype(BF16)
 
                 rs_copy(i, s, to_right).start()
 
@@ -610,42 +639,45 @@
             def _(to_right=to_right):
                 ag_own(i, slot, to_right).wait_send()
 
-    def partial_norm(cur):
+    def partial_norm(i):
+        cur = lax.rem(i, PART_RING)
+        g = group_rows(i)
         for c in range(0, d_model, chunk):
             cols = slice(c, c + chunk)
             part[cur, :, cols] = (
-                dot_nt(dq_in[cur], wq_ref[cols, :]) + dot_nt(dkv_in[cur, 0], wk_ref[cols, :]) + dot_nt(dkv_in[cur, 1], wv_ref[cols, :])
+                dot_nt(dq_all[g, :], wq_ref[cols, :]) + dot_nt(dkv_all[0, g, :], wk_ref[cols, :]) + dot_nt(dkv_all[1, g, :], wv_ref[cols, :])
             )
 
-    def project_out(cur, lo, hi):
-        for c in range(lo, hi, chunk):
+    def project_out(cur):
+        for c in range(0, d_model, chunk):
             cols = slice(c, c + chunk)
-            shares, share = wo_ref.shape[0], wo_ref.shape[2]
             acc = x_in[cur, :, cols].astype(F32)
             for t in range(tp):
-                for g in range(shares):
-                    acc += dot_nn(o_in[cur, t, :, g * share:(g + 1) * share], wo_ref[g, t, :, cols])
+                acc += dot_nn(o_in[cur, t], wo_ref[t, :, cols])
             y_buf[cur, :, cols] = acc.astype(BF16)
 
-    def finalize(i, slot):
-        mine = pl.ds(pl.multiple_of(z * rows, rows), rows)
-        tot[...] = part[slot, mine, :]
+    def finalize(i):
+        slot = lax.rem(i, 2)
+        own = pl.ds(pl.multiple_of(z * rows, rows), rows)
+        tot[...] = part[lax.rem(i, PART_RING), own, :]
 
         @pl.when(z > 0)
         def _():
             rs_copy(i, slots - 1, True).wait_recv()
-            tot[...] += rs_r[i, slots - 1].astype(F32)
+            tot[...] += rs_r[lax.rem(i, RS_RING), slots - 1].astype(F32)
 
         @pl.when(z < last)
         def _():
             rs_copy(i, slots - 1, False).wait_recv()
-            tot[...] += rs_l[i, slots - 1].astype(F32)
+            tot[...] += rs_l[lax.rem(i, RS_RING), slots - 1].astype(F32)
 
         @pl.when(i > 1)
         def _():
             ag_first_done(i - 2, slot)
 
-        x = x_in[slot, mine, :].astype(F32)
+        for copy in final_inputs(i, slot):
+            copy.wait()
+        x = xo_in[slot].astype(F32)
         centred = x - jnp.mean(x, axis=-1, keepdims=True)
         inv_std = lax.rsqrt(jnp.mean(centred * centred, axis=-1, keepdims=True) + LN_EPS)
         x_hat = centred * inv_std
@@ -653,12 +685,97 @@
         gg_ref[...] += jnp.sum(dn * x_hat, axis=0, keepdims=True)
         d_hat = dn * gain_ref[...]
         dx = inv_std * (d_hat - jnp.mean(d_hat, axis=-1, keepdims=True) - x_hat * jnp.mean(d_hat * x_hat, axis=-1, keepdims=True))
-        gx_buf[slot] = (dy_in[slot].astype(F32) + dx).astype(BF16)
+        gx_buf[slot] = (dyo_in[slot].astype(F32) + dx).astype(BF16)
+        ag_first(i, slot)
+
+    def block_of(t):
+        return 2 * lax.div(t, 2) + jnp.where(lax.rem(t, 2) == 0, 1 - core, core)
+
+    def job_loads(t, slot):
+        cols = pl.ds(pl.multiple_of(block_of(t) * width, width), width)
+        return [
+            pltpu.make_async_copy(n_hbm.at[:, cols], n_in.at[slot], job_sem.at[slot, 0]),
+            pltpu.make_async_copy(dy_hbm.at[:, cols], dy_in.at[slot], job_sem.at[slot, 1]),
+        ]
+
+    def away_copy(p):
+        ring = lax.rem(p, 2)
+        return remote(away, part_in.at[ring], away_send.at[0], away_recv.at[ring], partner)
+
+    def job_block(t, put):
+        slot = lax.rem(t, 2)
+        n_t = n_in[slot].T
+        put(0, hidden, dot_nn(n_t, dq_all[...]))
+        put(hidden, hidden, dot_nn(n_t, dkv_all[0]))
+        put(2 * hidden, hidden, dot_nn(n_t, dkv_all[1]))
+        for k in range(hidden // width):
+            put(3 * hidden + k * width, width, dot_nn(o_t[k * width:(k + 1) * width, :], dy_in[slot]))
+
+    def mine_to_own(p, slot):
+        return pltpu.make_async_copy(mine.at[slot], ga_hbm.at[2 * p + core], mine_own.at[slot])
+
+    def mine_to_part(p, slot):
+        return remote(mine.at[slot], ga_hbm.at[2 * p + core], mine_part.at[slot], ga_recv.at[p], partner)
+
+    def mine_to_chip(p, slot):
+        return remote(mine.at[slot], gb_hbm.at[2 * p + core], mine_chip.at[slot], chip_recv.at[p], peer)
+
+    def mine_done(p, slot):
+        mine_to_own(p, slot).wait()
+        mine_to_part(p, slot).wait_send()
+        mine_to_chip(p, slot).wait_send()
+
+    def chip_forward(p):
+        b = 2 * p + core
+        return remote(gb_hbm.at[b], gb_hbm.at[b], gb_send.at[p], gb_recv.at[p], partner)
+
+    def job(t):
+        p = lax.div(t, 2)
+        for copy in job_loads(t, lax.rem(t, 2)):
+            copy.wait()
+
+        @pl.when(t + 1 < blocks)
+        def _():
+            for copy in job_loads(t + 1, 1 - lax.rem(t, 2)):
+                copy.start()
+
+        @pl.when(lax.rem(t, 2) == 0)
+        def _():
+            @pl.when(p > 0)
+            def _():
+                away_copy(p - 1).wait_send()
+
+            def put(at, size, value):
+                away[:, at:at + size] = value
+
+            job_block(t, put)
+            away_copy(p).start()
+
+        @pl.when(lax.rem(t, 2) == 1)
+        def _():
+            slot = lax.rem(p, 2)
+            away_copy(p).wait_recv()
+
+            @pl.when(p > 1)
+            def _():
+                mine_done(p - 2, slot)
+
+            def put(at, size, value):
+                mine[slot, :, at:at + size] = (value + part_in[slot, :, at:at + size]).astype(BF16)
+
+            job_block(t, put)
+            mine_to_chip(p, slot).start()
+            mine_to_part(p, slot).start()
+            mine_to_own(p, slot).start()
 
     gg_ref[...] = jnp.zeros_like(gg_ref)
+    o_loads = [pltpu.make_async_copy(o_hbm.at[z, :, k * width:(k + 1) * width], n_in.at[k], job_sem.at[k, 0]) for k in range(hidden // width)]
+    for copy in o_loads:
+        copy.start()
     for copy in inputs(0, 0):
         copy.start()
-
+    for copy in out_loads:
+        copy.start()
     me = z * cp + r
 
     def gain_copy(dt, dc):
@@ -669,60 +786,76 @@
         sender = lax.rem(z + dt, tp) * cp + lax.rem(r + dc, cp)
         remote(gain_all.at[sender], gain_all.at[sender], gs_sem.at[0], gr_sem.at[sender], right).wait_recv()
 
+    for copy in weight_loads:
+        copy.wait()
+
     def step(i, carry):
         cur = lax.rem(i, 2)
-        prv = 1 - cur
 
         @pl.when(i < groups)
         def _():
-            for copy in inputs(i, cur):
-                copy.wait()
-            partial_norm(cur)
-
-        rs_send(i, cur, 0)
-        ag_step(i - 2, 1)
-
-        @pl.when(jnp.logical_and(i >= 1, i <= groups))
-        def _():
-            finalize(i - 1, prv)
-
-        @pl.when(i + 1 < groups)
-        def _():
-            for copy in inputs(i + 1, prv):
-                copy.start()
-
-        @pl.when(jnp.logical_and(i >= 2, i < groups))
-        def _():
-            y_copy(i - 2, cur).wait()
-
-        @pl.when(i < groups)
-        def _():
-            project_out(cur, 0, d_model // 2)
-
-        rs_send(i, cur, 1)
-        ag_step(i - 2, 2)
-
-        @pl.when(i < groups)
-        def _():
-            project_out(cur, d_model // 2, d_model)
-            y_copy(i, cur).start()
-
-        rs_send(i, cur, 2)
-
-        @pl.when(jnp.logical_and(i >= 1, i <= groups))
-        def _():
-            ag_first(i - 1, prv)
-
-        @pl.when(i == groups)
+            partial_norm(i)
+
+        for a in range(1, slots + 1):
+            ag_step(i - slots - a, a)
+        for s in reversed(range(slots)):
+            rs_send(i - s, s)
+
+        @pl.when(jnp.logical_and(i >= slots, i < groups + slots))
+        def _():
+            finalize(i - slots)
+
+        @pl.when(i == groups + slots - 1)
         def _():
             gain_all[me] = gg_ref[...]
             for dt, dc in peers:
                 gain_copy(dt, dc).start()
 
-        ag_step(i - 2, 3)
+        @pl.when(jnp.logical_and(i >= slots - 1, i < groups + slots - 1))
+        def _():
+            for copy in final_inputs(i - slots + 1, lax.rem(i - slots + 1, 2)):
+                copy.start()
+
+        @pl.when(i == 0)
+        def _():
+            for copy in out_loads:
+                copy.wait()
+            for k, copy in enumerate(o_loads):
+                copy.wait()
+                o_t[k * width:(k + 1) * width, :] = n_in[k].T
+            for copy in job_loads(0, 0):
+                copy.start()
+
+        @pl.when(i < groups)
+        def _():
+            for copy in inputs(i, cur):
+                copy.wait()
+
+            @pl.when(i + 1 < groups)
+            def _():
+                for copy in inputs(i + 1, 1 - cur):
+                    copy.start()
+
+            @pl.when(i >= 2)
+            def _():
+                y_copy(i - 2, cur).wait()
+
+            project_out(cur)
+            y_copy(i, cur).start()
+
+        @pl.when(jnp.logical_and(i >= 1, i <= blocks))
+        def _():
+            job(i - 1)
+
+        @pl.when(jnp.logical_and(lax.rem(i, 2) == 1, jnp.logical_and(i >= 5, i < 5 + 2 * pairs)))
+        def _():
+            p = lax.div(i - 5, 2)
+            mine_to_chip(p, 0).wait_recv()
+            chip_forward(p).start()
+
         return carry
 
-    lax.fori_loop(0, groups + 2, step, 0)
+    lax.fori_loop(0, max(groups + 2 * slots, 2 * pairs + 4), step, 0)
 
     for i in (groups - 2, groups - 1):
         y_copy(i, i % 2).wait()
@@ -737,6 +870,13 @@
             @pl.when(jnp.logical_and(far >= a, far < last))
             def _(a=a, to_right=to_right):
                 ag_forward(groups - 1, a, to_right).wait_send()
+    away_copy(pairs - 1).wait_send()
+    for p in range(max(0, pairs - 2), pairs):
+        mine_done(p, p % 2)
+    for p in range(pairs):
+        chip_forward(p).wait_send()
+        chip_forward(p).wait_recv()
+        mine_to_part(p, 0).wait_recv()
     for dt, dc in peers:
         gain_wait(dt, dc)
         gain_copy(dt, dc).wait_send()
@@ -746,59 +886,83 @@
     gg_ref[...] = total
 
 
-def backward_norm(dq, dkv, x, dy, o_all, wq, wk, wv, wo_all, gain, rows, tp, cp):
+def backward_norm(dq, dkv, x, dy, o_all, normed, wq, wk, wv, wo_all, gain, rows, tp, cp):
     tokens, hidden = dq.shape
     d_model = x.shape[1]
     span = tp * rows
     groups = tokens // span
     slots = tp - 1
+    width = WIDTH
+    blocks = d_model // width
+    pairs = blocks // 2
     hbm = pl.BlockSpec(memory_space=pl.ANY)
     vmem = pl.BlockSpec(memory_space=pltpu.VMEM)
     dma = pltpu.SemaphoreType.DMA
+    bf = lambda *shape: pltpu.VMEM(shape, BF16)
+    f32 = lambda *shape: pltpu.VMEM(shape, F32)
     return pl.pallas_call(
         functools.partial(back_kernel, groups, rows, tp, cp),
-        in_specs=[hbm] * 5 + [vmem] * 5,
-        out_specs=[hbm, hbm, vmem],
+        in_specs=[hbm] * 10 + [vmem],
+        out_specs=[hbm, hbm, hbm, hbm, vmem],
         out_shape=[
             jax.ShapeDtypeStruct((tokens, d_model), BF16),
             jax.ShapeDtypeStruct((tokens, d_model), BF16),
+            jax.ShapeDtypeStruct((blocks, width, 4 * hidden), BF16),
+            jax.ShapeDtypeStruct((blocks, width, 4 * hidden), BF16),
             jax.ShapeDtypeStruct((1, d_model), F32),
         ],
         scratch_shapes=[
-            pltpu.VMEM((2, span, d_model), F32),
-            pltpu.VMEM((groups, slots, rows, d_model), BF16),
-            pltpu.VMEM((groups, slots, rows, d_model), BF16),
-            pltpu.VMEM((slots, rows, d_model), BF16),
-            pltpu.VMEM((slots, rows, d_model), BF16),
-            pltpu.VMEM((rows, d_model), F32),
-            pltpu.VMEM((2, rows, d_model), BF16),
-            pltpu.VMEM((2, span, hidden), BF16),
-            pltpu.VMEM((2, 2, span, hidden), BF16),
-            pltpu.VMEM((2, tp, span, hidden), BF16),
-            pltpu.VMEM((2, span, d_model), BF16),
-            pltpu.VMEM((2, rows, d_model), BF16),
-            pltpu.VMEM((2, span, d_model), BF16),
-            pltpu.VMEM((tp * cp, 1, d_model), F32),
-            dma((2, 5)),
-            dma((2,)),
-            dma((2,)),
-            dma((slots,)),
-            dma((slots,)),
-            dma((groups, slots)),
-            dma((groups, slots)),
-            dma((2,)),
-            dma((2,)),
-            dma((slots,)),
-            dma((slots,)),
-            dma((groups, slots)),
-            dma((groups, slots)),
-            dma((tp * cp,)),
-            dma((tp * cp,)),
+            bf(d_model, hidden), bf(d_model, hidden), bf(d_model, hidden), bf(tp, hidden, d_model),
+            bf(tokens, hidden), bf(2, tokens, hidden), bf(hidden, tokens),
+            f32(PART_RING, span, d_model), bf(RS_RING, slots, rows, d_model), bf(RS_RING, slots, rows, d_model),
+            bf(slots, rows, d_model), bf(slots, rows, d_model), f32(rows, d_model), bf(2, rows, d_model),
+            bf(2, tp, span, hidden), bf(2, span, d_model), bf(2, rows, d_model), bf(2, rows, d_model), bf(2, span, d_model),
+            bf(2, tokens, width), bf(2, tokens, width),
+            f32(width, 4 * hidden), f32(2, width, 4 * hidden), bf(2, width, 4 * hidden), f32(tp * cp, 1, d_model),
+            dma((5 + tp * wo_all.shape[0],)), dma((2, 2)), dma((2, 2)), dma((2, 2)), dma((2,)), dma((2,)),
+            dma((slots,)), dma((slots,)), dma((RS_RING, slots)), dma((RS_RING, slots)),
+            dma((2,)), dma((2,)), dma((slots,)), dma((slots,)), dma((groups, slots)), dma((groups, slots)),
+            dma((1,)), dma((2,)), dma((2,)), dma((2,)), dma((2,)), dma((pairs,)), dma((pairs,)), dma((pairs,)), dma((pairs,)),
+            dma((tp * cp,)), dma((tp * cp,)),
         ],
-        compiler_params=pltpu.CompilerParams(collective_id=0, has_side_effects=True, vmem_limit_bytes=60 << 20),
-        cost_estimate=pl.CostEstimate(flops=14 * tokens * hidden * d_model, bytes_accessed=16 * tokens * d_model, transcendentals=0),
+        compiler_params=pltpu.CompilerParams(collective_id=0, has_side_effects=True, vmem_limit_bytes=63 << 20),
+        cost_estimate=pl.CostEstimate(flops=22 * tokens * hidden * d_model, bytes_accessed=16 * tokens * d_model, transcendentals=0),
         name="backward_norm",
-    )(dq, dkv, x, dy, o_all, wq, wk, wv, wo_all, gain)
+    )(dq, dkv, x, dy, o_all, normed, wq, wk, wv, wo_all, gain)
+
+
+def finish_kernel(y_ref, gx_ref, ga_ref, gb_ref, yo_ref, gxo_ref, wq_ref, wk_ref, wv_ref, wo_ref):
+    yo_ref[...] = y_ref[...]
+    gxo_ref[...] = gx_ref[...]
+    width = ga_ref.shape[1]
+    hidden = wq_ref.shape[1]
+    for k, ref in enumerate((wq_ref, wk_ref, wv_ref)):
+        cols = slice(k * hidden, (k + 1) * hidden)
+        ref[...] = ga_ref[0, :, cols].astype(F32) + gb_ref[0, :, cols].astype(F32)
+    for k in range(hidden // width):
+        cols = slice(3 * hidden + k * width, 3 * hidden + (k + 1) * width)
+        wo_ref[k * width:(k + 1) * width, :] = ga_ref[0, :, cols].astype(F32) + gb_ref[0, :, cols].astype(F32)
+
+
+def finish(y, gx, ga, gb):
+    tokens, d_model = y.shape
+    blocks, width, packed = ga.shape
+    hidden = packed // 4
+    rows = tokens // blocks
+    tile = pl.BlockSpec((rows, d_model), lambda j: (j, 0))
+    block = pl.BlockSpec((1, width, packed), lambda j: (j, 0, 0))
+    wide = pl.BlockSpec((width, hidden), lambda j: (j, 0))
+    return pl.pallas_call(
+        finish_kernel,
+        grid=(blocks,),
+        in_specs=[tile, tile, block, block],
+        out_specs=[tile, tile, wide, wide, wide, pl.BlockSpec((hidden, width), lambda j: (0, j))],
+        out_shape=[jax.ShapeDtypeStruct((tokens, d_model), BF16)] * 2 + [jax.ShapeDtypeStruct((d_model, hidden), F32)] * 3 + [jax.ShapeDtypeStruct((hidden, d_model), F32)],
+        compiler_params=pltpu.CompilerParams(dimension_semantics=("arbitrary",), vmem_limit_bytes=48 << 20),
+        cost_estimate=pl.CostEstimate(flops=8 * d_model * hidden, bytes_accessed=8 * tokens * d_model + 32 * d_model * hidden, transcendentals=0),
+        name="finish",
+    )(y, gx, ga, gb)
+
 
 def solution(mesh):
     cp_size = mesh.shape["cp"]
@@ -807,10 +971,8 @@
 
     def device_step(x_in, segment_ids, positions, w_query, w_key, w_value, w_out, norm_gain, grad_out):
         batch, seq, d_model = x_in.shape
-        hidden = w_query.shape[1]
         tokens = batch * seq
         rank = lax.axis_index("cp")
-        core = rank % 2
         x = x_in.reshape(tokens, d_model)
         dy = grad_out.reshape(tokens, d_model)
 
@@ -827,30 +989,9 @@
         rows = min(384, tokens)
         normed, kv = project_keys(x, cos_t, sin_t, norm_gain.reshape(1, d_model), w_key, w_value, rows)
         o_all, dq, dkv = front(kv, normed, dy, cos_t, sin_t, start.reshape(batch, 1, seq), w_query, w_out, seq, tp_size, cp_size)
-        grad_x, y_out, grad_gain = backward_norm(dq, dkv, x, dy, o_all, w_query, w_key, w_value, w_all, norm_gain.reshape(1, d_model), ROWS, tp_size, cp_size)
+        grad_x, y_out, sum_a, sum_b, grad_gain = backward_norm(dq, dkv, x, dy, o_all, normed, w_query, w_key, w_value, w_all, norm_gain.reshape(1, d_model), ROWS, tp_size, cp_size)
         grad_gain = grad_gain.reshape(d_model)
-
-        def perm(value, pairs):
-            return lax.ppermute(value, "cp", pairs)
-
-        def tn(a, b):
-            return lax.dot_general(a, b, (((0,), (0,)), ((), ())), preferred_element_type=F32)
-
-        def reduce_cp(part):
-            half = part.shape[0] // 2
-            away = lax.dynamic_slice(part, ((1 - core) * half, 0), (half, part.shape[1]))
-            mine = lax.dynamic_slice(part, (core * half, 0), (half, part.shape[1]))
-            mine = (mine + perm(away, [(0, 1), (1, 0), (2, 3), (3, 2)])).astype(BF16)
-            other = perm(mine, [(0, 2), (2, 0), (1, 3), (3, 1)])
-            total = mine.astype(F32) + other.astype(F32)
-            rest = perm(total, [(0, 1), (1, 0), (2, 3), (3, 2)])
-            return jnp.where(core == 0, jnp.concatenate([total, rest]), jnp.concatenate([rest, total]))
-
-        o = lax.dynamic_index_in_dim(o_all, lax.axis_index("tp"), 0, keepdims=False)
-        grad_wo = reduce_cp(tn(o, dy))
-        grad_wq = reduce_cp(tn(normed, dq))
-        grad_wk = reduce_cp(tn(normed, dkv[0]))
-        grad_wv = reduce_cp(tn(normed, dkv[1]))
+        y_out, grad_x, grad_wq, grad_wk, grad_wv, grad_wo = finish(y_out, grad_x, sum_a, sum_b)
         return y_out.reshape(x_in.shape), grad_x.reshape(x_in.shape), grad_gain, grad_wq, grad_wk, grad_wv, grad_wo
 
     in_specs = (P("dp", "cp", None), P("dp", "cp"), P("dp", "cp"), P(None, "tp"), P(None, "tp"), P(None, "tp"), P("tp", None), P(None), P("dp", "cp", None))

time: 718 us -> 547 us (0.76); the launches traced: 709 us -> 546 us
  waiting for transfers between devices: 80.2 us -> 0.04 us
  Pallas kernels: 479 us -> 521 us
  other arithmetic: 42.6 us -> 4.94 us
  local copies, waits for them, and re-layouts: 37.3 us -> 6.25 us
  matrix products: 28.4 us -> 0 us
  starting transfers between devices: 26.8 us -> 0.04 us
    ppermute x12 -> x0, waiting for transfers between devices: 80.2 us -> none  [perm(): return lax.ppermute(value, 'cp', pairs)]
    dot_general x4 -> x0, matrix products: 28.4 us -> none  [tn(): lax.dot_general(a, b, (((0,), (0,)), ((), ())), preferred_element_type=F32)]
    ppermute x12 -> x0, starting transfers between devices: 26.8 us -> none  [perm(): return lax.ppermute(value, 'cp', pairs)]
    select_n x4 -> x0, other arithmetic: 24.9 us -> none  [reduce_cp(): jnp.where(core == 0, jnp.concatenate([total, rest]), jnp.concatenate([res...]
    pallas_call x0 -> x1, Pallas kernels: none -> 23.4 us  [finish(): pl.pallas_call(finish_kernel, grid=(blocks,), in_specs=[tile, tile, block...]
    unnamed x27 -> x11, local copies, waits for them, and re-layouts: 27 us -> 3.75 us
    pallas_call x1, Pallas kernels: 259 us -> 276 us  [backward_norm(): pl.pallas_call(functools.partial(back_kernel, groups, rows, tp, cp), in_s...]
    dynamic_slice x4 -> x0, local copies, waits for them, and re-layouts: 7.89 us -> none  [reduce_cp(): lax.dynamic_slice(part, ((1 - core) * half, 0), (half, part.shape[1]))]
  transfers between devices with their start and end apart: 13 -> 1, of which waited for: 4 -> 0; matrix products, arithmetic and copies ran while one was open for 11% -> 1% of each run, Pallas kernels for 31% -> 41%
where the time goes in v4:
time: 547 us; the launch traced here: 546 us
  Pallas kernels  521 us (95%)
  between operations  14.1 us (3%)
  local copies, waits for them, and re-layouts  6.25 us (1%)
    pallas_call x1, Pallas kernels, backward_norm(): pl.pallas_call(functools.partial(back_kernel, groups, rows, tp, cp), in_s...  276 us
    pallas_call x1, Pallas kernels, front(): pl.pallas_call(functools.partial(front_kernel, batch, seq, tp, cp), in_sp...  203 us
    pallas_call x1, Pallas kernels, finish(): pl.pallas_call(finish_kernel, grid=(blocks,), in_specs=[tile, tile, block...  23.4 us
    pallas_call x1, Pallas kernels, project_keys(): pl.pallas_call(keys_kernel, grid=(tokens // rows,), in_specs=[tile(d_mode...  18.6 us
  transfers between devices with their start and end apart: 1, of which 0 were waited for; matrix products, arithmetic and copies ran while one was open for 1% of the time, Pallas kernels for 41%

profile of v4, /device:TPU:0, one launch (start us, length us, event | category | flops | bytes accessed | tf_op | source)
XLA Modules:
  0.0 546.4 jit_solution(2208783244340731224)
XLA Ops:
  7.2 0.0 all-gather.3.cloned.1.call-start
  7.2 1.7 constant_dynamic-slice_fusion
  8.9 0.0 all-gather.3.cloned.1.call-update
  8.9 0.8 broadcast_subtract_fusion
  9.7 0.6 reshape.56.start_ref
  10.3 0.1 broadcast_in_dim.4
  10.4 0.1 mul.33
  10.6 4.1 multiply_sine_fusion
  14.7 0.0 copy-start
  14.7 0.0 copy-start.1
  14.7 0.0 copy-start.2
  14.7 2.4 copy-done.2
  17.2 0.0 copy-start.3
  17.2 0.7 copy-done.3
  17.9 18.6 %project_keys.1 = (bf16[2304,2048]{1,0:T(8,128)(2,1)}, bf16[2,2304,512]{2,1,0:T(8,128)(2,1)}) custom-call(bf16[2304,2048]{1,0:T(8,128)(2,1)} %bitcast.10, f32[2304,128]{1,0:T(8,128)S(1)} %get-tuple-element.40.cos_ref, f32[2304,128]{1,0:T(8,128)S(1)} %get-tuple-element.39.sin_ref, f32[1,2048]{1,0:T(1,128)S(1)} %bitcast.8, bf16[2048,512]{1,0:T(8,128)(2,1)S(1)} %copy-done.2, ...), custom_call_target="tpu_custom_call" | custom-call | flops 9663676416 | bytes 23592960 | tf_op jit(solution)/shard_map/project_keys/pallas_call | solution.py:67
  36.5 0.0 copy-done
  36.5 0.0 copy-done.1
  36.5 203.4 %front.1 = (bf16[4,2304,512]{2,1,0:T(8,128)(2,1)}, bf16[2304,512]{1,0:T(8,128)(2,1)}, bf16[2,2304,512]{2,1,0:T(8,128)(2,1)}) custom-call(bf16[2,2304,512]{2,1,0:T(8,128)(2,1)} %get-tuple-element.23.kv_hbm, bf16[2304,2048]{1,0:T(8,128)(2,1)} %get-tuple-element.24.n_hbm, bf16[2304,2048]{1,0:T(8,128)(2,1)} %bitcast.12, f32[2304,128]{1,0:T(8,128)} %copy-done.1, ...), custom_call_target="tpu_custom_call" | custom-call | flops 21743271936 | bytes 75497472 | tf_op jit(solution)/shard_map/front/pallas_call | solution.py:456
  239.9 0.0 all-gather.3.cloned.1.call-done
  239.9 275.6 %backward_norm.1 = (bf16[2304,2048]{1,0:T(8,128)(2,1)}, bf16[2304,2048]{1,0:T(8,128)(2,1)}, bf16[8,256,2048]{2,1,0:T(8,128)(2,1)}, bf16[8,256,2048]{2,1,0:T(8,128)(2,1)}, f32[1,2048]{1,0:T(1,128)}) custom-call(bf16[2304,512]{1,0:T(8,128)(2,1)} %get-tuple-element.25.dq_hbm, bf16[2,2304,512]{2,1,0:T(8,128)(2,1)} %get-tuple-element.26.dkv_hbm, ...), custom_call_target="tpu_custom_call" | custom-call | flops 53150220288 | bytes 75497472 | tf_op jit(solution)/shard_map/backward_norm/pallas_call | solution.py:903
  515.5 0.0 copy-start.4
  515.5 23.4 %finish.1 = (bf16[2304,2048]{1,0:T(8,128)(2,1)}, bf16[2304,2048]{1,0:T(8,128)(2,1)}, f32[2048,512]{1,0:T(8,128)}, f32[2048,512]{1,0:T(8,128)}, f32[2048,512]{1,0:T(8,128)}, /*index=5*/f32[512,2048]{1,0:T(8,128)}) custom-call(bf16[2304,2048]{1,0:T(8,128)(2,1)} %get-tuple-element.28.y_ref, bf16[2304,2048]{1,0:T(8,128)(2,1)} %get-tuple-element.29.gx_ref, ...), custom_call_target="tpu_custom_call" | custom-call | flops 8388608 | bytes 71303168 | tf_op jit(solution)/shard_map/finish/pallas_call | solution.py:955
  539.0 0.0 copy-done.4
  539.0 0.6 copy.16
  (3 shorter events, 0.0 us)
Async XLA Ops:
  7.2 232.7 %all-gather.3.cloned.1.call-start = ((), (), s32[]{:S(2)}) async-start(), calls=%async_computation | async-start | bytes 8650752 | tf_op jit(solution)/shard_map/all_gather | solution.py:986
  14.7 21.8 %copy-start = (f32[2304,128]{1,0:T(8,128)}, f32[2304,128]{1,0:T(8,128)S(1)}, u32[]{:S(2)}) copy-start(f32[2304,128]{1,0:T(8,128)S(1)} %get-tuple-element.39.sin_ref) | copy-start | bytes 3538948
  14.7 21.8 %copy-start.1 = (f32[2304,128]{1,0:T(8,128)}, f32[2304,128]{1,0:T(8,128)S(1)}, u32[]{:S(2)}) copy-start(f32[2304,128]{1,0:T(8,128)S(1)} %get-tuple-element.40.cos_ref) | copy-start | bytes 3538948
  14.7 2.4 copy-start.2
  17.2 0.7 copy-start.3
  515.5 23.5 %copy-start.4 = (f32[1,2048]{1,0:T(1,128)S(1)}, f32[1,2048]{1,0:T(1,128)}, u32[]{:S(2)}) copy-start(f32[1,2048]{1,0:T(1,128)} %get-tuple-element.34) | copy-start | bytes 24580
Sparse Core Ops, SparseCore 0:
  11.4 91.2 all-gather.2

commit v5 on v4

--- a/solution.py
+++ b/solution.py
@@ -49,123 +49,185 @@
         dst[:, cols] = rope(raw[:, cols], cos_t, sin_t, 1.0).astype(BF16)
 
 
-def keys_kernel(x_ref, cos_ref, sin_ref, gain_ref, wk_ref, wv_ref, n_ref, kv_ref):
-    x = x_ref[...].astype(F32)
-    centred = x - jnp.mean(x, axis=-1, keepdims=True)
-    inv_std = lax.rsqrt(jnp.mean(centred * centred, axis=-1, keepdims=True) + LN_EPS)
-    normed = ((centred * inv_std) * gain_ref[...]).astype(BF16)
-    n_ref[...] = normed
-    put_rope(kv_ref.at[0], dot_nn(normed, wk_ref[...]), cos_ref[...], sin_ref[...])
-    kv_ref[1] = dot_nn(normed, wv_ref[...]).astype(BF16)
-
-
-def project_keys(x, cos_t, sin_t, gain, wk, wv, rows):
-    tokens, d_model = x.shape
-    hidden = wk.shape[1]
-    whole = pl.BlockSpec(memory_space=pltpu.VMEM)
-    tile = lambda width: pl.BlockSpec((rows, width), lambda i: (i, 0))
-    return pl.pallas_call(
-        keys_kernel,
-        grid=(tokens // rows,),
-        in_specs=[tile(d_model), tile(HEAD_DIM), tile(HEAD_DIM), whole, whole, whole],
-        out_specs=[tile(d_model), pl.BlockSpec((2, rows, hidden), lambda i: (0, i, 0))],
-        out_shape=[jax.ShapeDtypeStruct((tokens, d_model), BF16), jax.ShapeDtypeStruct((2, tokens, hidden), BF16)],
-        compiler_params=pltpu.CompilerParams(dimension_semantics=("arbitrary",), vmem_limit_bytes=48 << 20),
-        cost_estimate=pl.CostEstimate(flops=4 * tokens * d_model * hidden, bytes_accessed=4 * tokens * (d_model + hidden), transcendentals=0),
-        name="project_keys",
-    )(x, cos_t, sin_t, gain, wk, wv)
-
-
 MESH = pl.DeviceIdType.MESH
 SUB = 128
-ROWS = 48
+ROWS = 32
 WIDTH = 256
 RELAY_LAG = 2
 CHIP_BUFS = 3
-
-
-def front_kernel(batch, seq, tp, cp, kv_hbm, n_hbm, dy_hbm, cos_ref, sin_ref, start_ref, wq_ref, wo_ref,
-                 o_all, dq_hbm, dkv_hbm,
-                 q_all, do_all, n_in, dy_in, kv_own, kvr, s_scr, dp_scr, m_scr, l_scr, d_scr, ot_scr, dqt_scr,
-                 o_buf, dq_buf, g_own, g_part, g_chip, g_far, xin, part_in, dkv_out,
-                 tile_sem, own_sem, kvs_part, kvs_chip, kvs_far, kv_recv, o_local, o_send, o_recv, relay_send, dq_sem,
+W_TWIN = 1
+W_PARTNER = 4
+
+
+def front_kernel(batch, seq, tp, cp, x_hbm, dy_hbm, wq_hbm, wk_hbm, wv_hbm, wo_hbm, cos_ref, sin_ref, start_ref, gain_ref,
+                 n_hbm, o_all, dq_hbm, dkv_hbm, w_all,
+                 big, wo_ref, q_row, do_row, a_in, b_in, kv_own, kvr, s_scr, dp_scr, m_scr, l_scr, d_scr, ot_scr, dqt_scr,
+                 o_buf, dq_buf, g_part, g_chip, g_far, xin, part_in,
+                 w_sem, wl_sem, wz_send, wz_recv, wx_send, wx_recv, wp_send, wp_recv, wf_send, wf_recv,
+                 tile_sem, n_sem, kvs_part, kvs_chip, kvs_far, kv_recv, o_local, o_send, o_recv, relay_send, dq_sem,
                  far_send, part_send, chip_send, x_recv, part_recv, dkv_sem):
     z = lax.axis_index("tp")
     r = lax.axis_index("cp")
+    dp = lax.axis_index("dp")
     core = lax.rem(r, 2)
     chip = lax.div(r, 2)
-    hidden = q_all.shape[1]
+    d_model = x_hbm.shape[1]
+    hidden = wq_hbm.shape[1]
     heads = hidden // HEAD_DIM
     first_chip, second_chip = chip == 0, chip == 1
     first_core, second_core = core == 0, core == 1
     partner = {"cp": r + 1 - 2 * core}
     peer = {"cp": r + 2 - 4 * chip}
+    twin = {"dp": 1 - dp}
+
+    weight_loads = [pltpu.make_async_copy(src, dst, w_sem.at[k]) for k, (src, dst) in enumerate(((wk_hbm, big.at[0]), (wv_hbm, big.at[1]), (wq_hbm, big.at[2]), (wo_hbm, wo_ref)))]
+    for copy in weight_loads:
+        copy.start()
+
+    tile = a_in.shape[1]
+    per_row = seq // tile
+    tiles = batch * per_row
+
+    def tile_rows(t):
+        return pl.ds(pl.multiple_of(t * tile, tile), tile)
+
+    def row(b):
+        return pl.ds(pl.multiple_of(b * seq, seq), seq)
+
+    def x_load(t, par):
+        return pltpu.make_async_copy(x_hbm.at[tile_rows(t), :], a_in.at[par], tile_sem.at[par, 0])
+
+    def n_load(t, par):
+        return pltpu.make_async_copy(n_hbm.at[tile_rows(t), :], a_in.at[par], tile_sem.at[par, 0])
+
+    def dy_load(t, par):
+        return pltpu.make_async_copy(dy_hbm.at[tile_rows(t), :], b_in.at[par], tile_sem.at[par, 1])
+
+    def n_store(t, par):
+        return pltpu.make_async_copy(b_in.at[par], n_hbm.at[tile_rows(t), :], n_sem.at[par])
+
+    x_load(0, 0).start()
 
     barrier = pltpu.get_barrier_semaphore()
-    for dev in [partner, peer] + [{"tp": lax.rem(z + dt, tp)} for dt in range(1, tp)]:
+    for dev in [partner, peer, twin] + [{"tp": lax.rem(z + dt, tp)} for dt in range(1, tp)]:
         pl.semaphore_signal(barrier, inc=1, device_id=dev, device_id_type=MESH)
-    pl.semaphore_wait(barrier, tp + 1)
+    pl.semaphore_wait(barrier, tp + 2)
 
     def remote(src, dst, ssem, rsem, dev):
         return pltpu.make_async_remote_copy(src_ref=src, dst_ref=dst, send_sem=ssem, recv_sem=rsem, device_id=dev, device_id_type=MESH)
 
-    def row(b):
-        return pl.ds(pl.multiple_of(b * seq, seq), seq)
+    share = hidden // 4
+
+    def share_rows(c, g):
+        return pl.ds(pl.multiple_of((2 * c + g) * share, share), share)
+
+    mine, twins = share_rows(core, dp), share_rows(core, 1 - dp)
+
+    def wz_copy(d):
+        return remote(wo_hbm.at[mine, :], w_all.at[z, mine, :], wz_send.at[d], wz_recv.at[z], {"tp": lax.rem(z + d, tp)})
+
+    def wz_wait(d):
+        src = lax.rem(z + d, tp)
+        remote(wo_hbm.at[mine, :], w_all.at[src, mine, :], wz_send.at[d], wz_recv.at[src], partner).wait_recv()
+
+    def w_slice(d, rows):
+        return w_all.at[lax.rem(z + d, tp), rows, :]
+
+    def wx_copy(d):
+        return remote(w_slice(d, mine), w_slice(d, mine), wx_send.at[d], wx_recv.at[d], twin)
+
+    def wp_copy(d):
+        return remote(w_slice(d, mine), w_slice(d, mine), wp_send.at[d], wp_recv.at[d], partner)
+
+    def wf_copy(d):
+        return remote(w_slice(d, twins), w_slice(d, twins), wf_send.at[d], wf_recv.at[d], partner)
+
+    for d in range(1, tp):
+        wz_copy(d).start()
 
     def kv_to_partner(b):
-        return remote(kv_hbm.at[:, row(b), :], kvr.at[0, b], kvs_part.at[b], kv_recv.at[0, b], partner)
+        return remote(kv_own.at[b], kvr.at[0, b], kvs_part.at[b], kv_recv.at[0, b], partner)
 
     def kv_to_chip(b):
-        return remote(kv_hbm.at[:, row(b), :], kvr.at[1, b], kvs_chip.at[b], kv_recv.at[1, b], peer)
+        return remote(kv_own.at[b], kvr.at[1, b], kvs_chip.at[b], kv_recv.at[1, b], peer)
 
     def kv_forward(b):
         return remote(kvr.at[1, b], kvr.at[2, b], kvs_far.at[b], kv_recv.at[2, b], partner)
 
-    for b in range(batch):
-        @pl.when(first_chip)
-        def _(b=b):
-            kv_to_chip(b).start()
-
-        @pl.when(first_core)
-        def _(b=b):
-            kv_to_partner(b).start()
-
-    def own_load(b, par):
-        return pltpu.make_async_copy(kv_hbm.at[:, row(b), :], kv_own.at[par], own_sem.at[par])
-
-    own_load(0, 0).start()
-
-    tile = n_in.shape[1]
-    tiles = batch * seq // tile
-
-    def tile_rows(t):
-        return pl.ds(pl.multiple_of(t * tile, tile), tile)
-
-    def tile_loads(t, par):
-        return [
-            pltpu.make_async_copy(n_hbm.at[tile_rows(t), :], n_in.at[par], tile_sem.at[par, 0]),
-            pltpu.make_async_copy(dy_hbm.at[tile_rows(t), :], dy_in.at[par], tile_sem.at[par, 1]),
-        ]
-
-    for copy in tile_loads(0, 0):
+    for copy in weight_loads:
+        copy.wait()
+    w_local = pltpu.make_async_copy(wo_ref, w_all.at[z], wl_sem.at[0])
+    w_local.start()
+
+    def key_tile(t, carry):
+        par = lax.rem(t, 2)
+        x_load(t, par).wait()
+
+        @pl.when(t + 1 < tiles)
+        def _():
+            x_load(t + 1, 1 - par).start()
+
+        @pl.when(t >= 2)
+        def _():
+            n_store(t - 2, par).wait()
+
+        x = a_in[par].astype(F32)
+        centred = x - jnp.mean(x, axis=-1, keepdims=True)
+        inv_std = lax.rsqrt(jnp.mean(centred * centred, axis=-1, keepdims=True) + LN_EPS)
+        normed = ((centred * inv_std) * gain_ref[...]).astype(BF16)
+        b_in[par] = normed
+        n_store(t, par).start()
+        b = lax.div(t, per_row)
+        part = lax.rem(t, per_row)
+        inside = pl.ds(pl.multiple_of(part * tile, tile), tile)
+        rows = tile_rows(t)
+        put_rope(kv_own.at[b, 0, inside, :], dot_nn(normed, big[0]), cos_ref[rows, :], sin_ref[rows, :])
+        kv_own[b, 1, inside, :] = dot_nn(normed, big[1]).astype(BF16)
+
+        @pl.when(part == per_row - 1)
+        def _():
+            @pl.when(first_chip)
+            def _():
+                kv_to_chip(b).start()
+
+            @pl.when(first_core)
+            def _():
+                kv_to_partner(b).start()
+
+        return carry
+
+    lax.fori_loop(0, tiles, key_tile, 0)
+    for t in range(tiles - 2, tiles):
+        n_store(t, t % 2).wait()
+
+    def query_loads(t, par):
+        return [n_load(t, par), dy_load(t, par)]
+
+    for copy in query_loads(0, 0):
         copy.start()
 
-    def project(t, carry):
-        par = lax.rem(t, 2)
-        for copy in tile_loads(t, par):
-            copy.wait()
-
-        @pl.when(t + 1 < tiles)
-        def _():
-            for copy in tile_loads(t + 1, 1 - par):
-                copy.start()
-
-        rows = tile_rows(t)
-        put_rope(q_all.at[rows, :], dot_nn(n_in[par], wq_ref[...]), cos_ref[rows, :], sin_ref[rows, :])
-        do_all[rows, :] = dot_nt(dy_in[par], wo_ref[...]).astype(BF16)
-        return carry
-
-    lax.fori_loop(0, tiles, project, 0)
+    def query_row(i):
+        for k in range(per_row):
+            t = i * per_row + k
+            par = lax.rem(t, 2)
+            for copy in query_loads(t, par):
+                copy.wait()
+
+            @pl.when(t + 1 < tiles)
+            def _(t=t, par=par):
+                for copy in query_loads(t + 1, 1 - par):
+                    copy.start()
+
+            rows = tile_rows(t)
+            inside = slice(k * tile, (k + 1) * tile)
+            put_rope(q_row.at[inside, :], dot_nn(a_in[par], big[2]), cos_ref[rows, :], sin_ref[rows, :])
+            do_row[inside, :] = dot_nt(b_in[par], wo_ref[...]).astype(BF16)
+
+    fit = d_model // seq
+
+    def g_own(b, which):
+        k = 2 * b + which
+        return big.at[lax.div(k, fit), pl.ds(pl.multiple_of(lax.rem(k, fit) * seq, seq), seq), :]
 
     def o_local_copy(b):
         return pltpu.make_async_copy(o_buf.at[b], o_all.at[z, row(b), :], o_local.at[b])
@@ -217,12 +279,10 @@
             g_chip[par] = (g_chip[par].astype(F32) + xin[b].astype(F32)).astype(BF16)
             chip_copy(b).start()
 
-    def dkv_store(b, par):
-        return pltpu.make_async_copy(dkv_out.at[par], dkv_hbm.at[:, row(b), :], dkv_sem.at[par])
+    def dkv_store(b, which):
+        return pltpu.make_async_copy(g_own(b, which), dkv_hbm.at[which, row(b), :], dkv_sem.at[b, which])
 
     def key_grads(b):
-        par = lax.rem(b, 2)
-
         @pl.when(first_core)
         def _():
             part_copy(b, 0).wait_recv()
@@ -230,22 +290,19 @@
         @pl.when(first_chip)
         def _():
             chip_copy(b).wait_recv()
-
-        @pl.when(b >= 2)
-        def _():
-            dkv_store(b - 2, par).wait()
 
         rows = row(b)
         for which in range(2):
+            own = g_own(b, which)
             for h in range(heads):
                 cols = slice(h * HEAD_DIM, (h + 1) * HEAD_DIM)
-                acc = g_own[b, which, :, cols].astype(F32)
+                acc = own[:, cols].astype(F32)
                 acc = acc + jnp.where(first_core, part_in[b, which, :, cols].astype(F32), 0.0)
                 acc = (acc + jnp.where(first_chip, xin[b, which, :, cols].astype(F32), 0.0)).astype(BF16)
                 if which == 0:
                     acc = rope(acc.astype(F32), cos_ref[rows, :], sin_ref[rows, :], -1.0).astype(BF16)
-                dkv_out[par, which, :, cols] = acc
-        dkv_store(b, par).start()
+                own[:, cols] = acc
+            dkv_store(b, which).start()
 
     def dq_store(b, par):
         return pltpu.make_async_copy(dq_buf.at[par], dq_hbm.at[row(b), :], dq_sem.at[par])
@@ -256,8 +313,12 @@
         rows = row(i)
         start = start_ref[i]
         chip_par = lax.rem(i, CHIP_BUFS)
-        keys_of = [kv_own.at[par]] + [kvr.at[s, i] for s in range(3)]
-        grads = [g_own.at[i], g_part.at[par], g_chip.at[chip_par], g_far.at[par]]
+        keys_of = [kv_own.at[i]] + [kvr.at[s, i] for s in range(3)]
+        places = [g_part.at[par], g_chip.at[chip_par], g_far.at[par]]
+
+        def grad(slot, which):
+            return places[slot - 1].at[which] if slot else g_own(i, which)
+
         live = [None, second_core, second_chip, second_chip]
         piece = [r, r + 1 - 2 * core, r + 2 - 4 * chip, r + 3 - 2 * core - 4 * chip]
 
@@ -268,8 +329,8 @@
 
         def one_head(h, carry):
             cols = pl.ds(pl.multiple_of(h * HEAD_DIM, HEAD_DIM), HEAD_DIM)
-            q = q_all[rows, cols]
-            do = do_all[rows, cols]
+            q = q_row[:, cols]
+            do = do_row[:, cols]
             m_scr[...] = jnp.full(m_scr.shape, NEG_BIG, F32)
             l_scr[...] = jnp.zeros_like(l_scr)
             d_scr[...] = jnp.zeros_like(d_scr)
@@ -303,14 +364,14 @@
                     s_scr[slot, s:s + SUB, :] = prob
                     dp_scr[slot, s:s + SUB, :] = dp
                     d_scr[...] += jnp.sum(prob * dp, axis=0, keepdims=True)
-                    grads[slot][1, s:s + SUB, cols] = dot_nn(low, do).astype(BF16)
+                    grad(slot, 1)[s:s + SUB, cols] = dot_nn(low, do).astype(BF16)
                     ot_scr[...] += dot_nn(v.T, low)
 
             def keys(slot):
                 for s in subs:
                     k = keys_of[slot][0, s:s + SUB, cols]
                     ds = (s_scr[slot, s:s + SUB, :] * (dp_scr[slot, s:s + SUB, :] - d_scr[...])).astype(BF16)
-                    grads[slot][0, s:s + SUB, cols] = (dot_nn(ds, q) * SCALE).astype(BF16)
+                    grad(slot, 0)[s:s + SUB, cols] = (dot_nn(ds, q) * SCALE).astype(BF16)
                     dqt_scr[...] += dot_nn(k.T, ds)
 
             each(scores)
@@ -326,11 +387,7 @@
 
     def step(i, carry):
         par = lax.rem(i, 2)
-        own_load(i, par).wait()
-
-        @pl.when(i + 1 < batch)
-        def _():
-            own_load(i + 1, 1 - par).start()
+        query_row(i)
 
         @pl.when(second_chip)
         def _():
@@ -380,6 +437,19 @@
         @pl.when(i >= RELAY_LAG)
         def _():
             relay(i - RELAY_LAG)
+
+        @pl.when(i == min(W_TWIN, batch - 1))
+        def _():
+            for d in range(1, tp):
+                wz_wait(d)
+                wx_copy(d).start()
+                wp_copy(d).start()
+
+        @pl.when(i == min(W_PARTNER, batch - 1))
+        def _():
+            for d in range(1, tp):
+                wx_copy(d).wait_recv()
+                wf_copy(d).start()
 
         return carry
 
@@ -395,7 +465,17 @@
 
     lax.fori_loop(0, batch, finish, 0)
 
+    w_local.wait()
+    for d in range(1, tp):
+        wz_copy(d).wait_send()
+        wx_copy(d).wait_send()
+        for copy in (wp_copy(d), wf_copy(d)):
+            copy.wait_send()
+            copy.wait_recv()
     for b in range(batch):
+        for which in range(2):
+            dkv_store(b, which).wait()
+
         @pl.when(first_chip)
         def _(b=b):
             kv_to_chip(b).wait_send()
@@ -427,7 +507,6 @@
 
     for b in range(max(0, batch - 2), batch):
         dq_store(b, b % 2).wait()
-        dkv_store(b, b % 2).wait()
 
         @pl.when(second_core)
         def _(b=b):
@@ -443,9 +522,9 @@
             chip_copy(b).wait_send()
 
 
-def front(kv, normed, dy, cos_t, sin_t, start, wq, wo, seq, tp, cp):
-    _, tokens, hidden = kv.shape
-    d_model = normed.shape[1]
+def front(x, dy, wq, wk, wv, wo, cos_t, sin_t, start, gain, seq, tp, cp):
+    tokens, d_model = x.shape
+    hidden = wq.shape[1]
     batch = tokens // seq
     tile = seq // 2
     hbm = pl.BlockSpec(memory_space=pl.ANY)
@@ -455,32 +534,36 @@
     f32 = lambda *shape: pltpu.VMEM(shape, F32)
     return pl.pallas_call(
         functools.partial(front_kernel, batch, seq, tp, cp),
-        in_specs=[hbm] * 3 + [vmem] * 5,
-        out_specs=[hbm] * 3,
+        in_specs=[hbm] * 6 + [vmem] * 4,
+        out_specs=[hbm] * 5,
         out_shape=[
+            jax.ShapeDtypeStruct((tokens, d_model), BF16),
             jax.ShapeDtypeStruct((tp, tokens, hidden), BF16),
             jax.ShapeDtypeStruct((tokens, hidden), BF16),
             jax.ShapeDtypeStruct((2, tokens, hidden), BF16),
+            jax.ShapeDtypeStruct((tp, hidden, d_model), BF16),
         ],
         scratch_shapes=[
-            bf(tokens, hidden), bf(tokens, hidden), bf(2, tile, d_model), bf(2, tile, d_model),
-            bf(2, 2, seq, hidden), bf(3, batch, 2, seq, hidden),
+            bf(3, d_model, hidden), bf(hidden, d_model), bf(seq, hidden), bf(seq, hidden), bf(2, tile, d_model), bf(2, tile, d_model),
+            bf(batch, 2, seq, hidden), bf(3, batch, 2, seq, hidden),
             f32(4, seq, seq), f32(4, seq, seq), f32(1, seq), f32(1, seq), f32(1, seq), f32(HEAD_DIM, seq), f32(HEAD_DIM, seq),
             bf(batch, seq, hidden), bf(2, seq, hidden),
-            bf(batch, 2, seq, hidden), bf(2, 2, seq, hidden), bf(CHIP_BUFS, 2, seq, hidden), bf(2, 2, seq, hidden),
-            bf(batch, 2, seq, hidden), bf(batch, 2, seq, hidden), bf(2, 2, seq, hidden),
+            bf(2, 2, seq, hidden), bf(CHIP_BUFS, 2, seq, hidden), bf(2, 2, seq, hidden),
+            bf(batch, 2, seq, hidden), bf(batch, 2, seq, hidden),
+            dma((4,)), dma((1,)), dma((tp,)), dma((tp,)), dma((tp,)), dma((tp,)), dma((tp,)), dma((tp,)), dma((tp,)), dma((tp,)),
             dma((2, 2)), dma((2,)), dma((batch,)), dma((batch,)), dma((batch,)), dma((3, batch)),
             dma((batch,)), dma((4, batch)), dma((tp, batch)), dma((batch,)), dma((2,)),
-            dma((2,)), dma((2,)), dma((CHIP_BUFS,)), dma((batch,)), dma((batch,)), dma((2,)),
+            dma((2,)), dma((2,)), dma((CHIP_BUFS,)), dma((batch,)), dma((batch,)), dma((batch, 2)),
         ],
         compiler_params=pltpu.CompilerParams(collective_id=1, has_side_effects=True, vmem_limit_bytes=63 << 20),
-        cost_estimate=pl.CostEstimate(flops=48 * tokens * seq * hidden, bytes_accessed=16 * tokens * d_model, transcendentals=4 * tokens * seq * (hidden // HEAD_DIM)),
+        cost_estimate=pl.CostEstimate(flops=60 * tokens * seq * hidden, bytes_accessed=16 * tokens * d_model, transcendentals=4 * tokens * seq * (hidden // HEAD_DIM)),
         name="front",
-    )(kv, normed, dy, cos_t, sin_t, start, wq, wo)
+    )(x, dy, wq, wk, wv, wo, cos_t, sin_t, start, gain)
 
 
 PART_RING = 4
 RS_RING = 5
+FORWARD_LAG = 7
 
 
 def back_kernel(groups, rows, tp, cp, dq_hbm, dkv_hbm, x_hbm, dy_hbm, o_hbm, n_hbm, wq_hbm, wk_hbm, wv_hbm, wo_hbm, gain_ref,
@@ -505,12 +588,8 @@
     partner = {"cp": r + 1 - 2 * core}
     peer = {"cp": r + 2 - 4 * chip}
 
-    shares, share = wo_hbm.shape[0], wo_hbm.shape[2]
     weight_loads = [pltpu.make_async_copy(src, dst, w_sem.at[k]) for k, (src, dst) in enumerate(((wq_hbm, wq_ref), (wk_hbm, wk_ref), (wv_hbm, wv_ref), (dq_hbm, dq_all), (dkv_hbm, dkv_all)))]
-    out_loads = [
-        pltpu.make_async_copy(wo_hbm.at[g, t], wo_ref.at[t, g * share:(g + 1) * share, :], w_sem.at[5 + g * tp + t])
-        for g in range(shares) for t in range(tp)
-    ]
+    out_loads = [pltpu.make_async_copy(wo_hbm, wo_ref, w_sem.at[5])]
     for copy in weight_loads:
         copy.start()
 
@@ -847,15 +926,15 @@
         def _():
             job(i - 1)
 
-        @pl.when(jnp.logical_and(lax.rem(i, 2) == 1, jnp.logical_and(i >= 5, i < 5 + 2 * pairs)))
-        def _():
-            p = lax.div(i - 5, 2)
+        @pl.when(jnp.logical_and(lax.rem(i, 2) == 1, jnp.logical_and(i >= FORWARD_LAG, i < FORWARD_LAG + 2 * pairs)))
+        def _():
+            p = lax.div(i - FORWARD_LAG, 2)
             mine_to_chip(p, 0).wait_recv()
             chip_forward(p).start()
 
         return carry
 
-    lax.fori_loop(0, max(groups + 2 * slots, 2 * pairs + 4), step, 0)
+    lax.fori_loop(0, max(groups + 2 * slots, 2 * pairs + FORWARD_LAG - 1), step, 0)
 
     for i in (groups - 2, groups - 1):
         y_copy(i, i % 2).wait()
@@ -919,7 +998,7 @@
             bf(2, tp, span, hidden), bf(2, span, d_model), bf(2, rows, d_model), bf(2, rows, d_model), bf(2, span, d_model),
             bf(2, tokens, width), bf(2, tokens, width),
             f32(width, 4 * hidden), f32(2, width, 4 * hidden), bf(2, width, 4 * hidden), f32(tp * cp, 1, d_model),
-            dma((5 + tp * wo_all.shape[0],)), dma((2, 2)), dma((2, 2)), dma((2, 2)), dma((2,)), dma((2,)),
+            dma((6,)), dma((2, 2)), dma((2, 2)), dma((2, 2)), dma((2,)), dma((2,)),
             dma((slots,)), dma((slots,)), dma((RS_RING, slots)), dma((RS_RING, slots)),
             dma((2,)), dma((2,)), dma((slots,)), dma((slots,)), dma((groups, slots)), dma((groups, slots)),
             dma((1,)), dma((2,)), dma((2,)), dma((2,)), dma((2,)), dma((pairs,)), dma((pairs,)), dma((pairs,)), dma((pairs,)),
@@ -967,7 +1046,6 @@
 def solution(mesh):
     cp_size = mesh.shape["cp"]
     tp_size = mesh.shape["tp"]
-    dp_size = mesh.shape["dp"]
 
     def device_step(x_in, segment_ids, positions, w_query, w_key, w_value, w_out, norm_gain, grad_out):
         batch, seq, d_model = x_in.shape
@@ -981,15 +1059,9 @@
         cos_t, sin_t = jnp.cos(angles), jnp.sin(angles)
         start = (rank * seq + jnp.arange(seq, dtype=jnp.int32))[None, :] - positions
 
-        share = w_out.shape[0] // (cp_size * dp_size)
-        mine = (lax.axis_index("dp") * cp_size + rank) * share
-        w_all = lax.all_gather(lax.dynamic_slice(w_out, (mine, 0), (share, d_model)), ("dp", "tp", "cp"), axis=0)
-        w_all = w_all.reshape(dp_size, tp_size, cp_size * share, d_model)
-
-        rows = min(384, tokens)
-        normed, kv = project_keys(x, cos_t, sin_t, norm_gain.reshape(1, d_model), w_key, w_value, rows)
-        o_all, dq, dkv = front(kv, normed, dy, cos_t, sin_t, start.reshape(batch, 1, seq), w_query, w_out, seq, tp_size, cp_size)
-        grad_x, y_out, sum_a, sum_b, grad_gain = backward_norm(dq, dkv, x, dy, o_all, normed, w_query, w_key, w_value, w_all, norm_gain.reshape(1, d_model), ROWS, tp_size, cp_size)
+        gain = norm_gain.reshape(1, d_model)
+        normed, o_all, dq, dkv, w_all = front(x, dy, w_query, w_key, w_value, w_out, cos_t, sin_t, start.reshape(batch, 1, seq), gain, seq, tp_size, cp_size)
+        grad_x, y_out, sum_a, sum_b, grad_gain = backward_norm(dq, dkv, x, dy, o_all, normed, w_query, w_key, w_value, w_all, gain, ROWS, tp_size, cp_size)
         grad_gain = grad_gain.reshape(d_model)
         y_out, grad_x, grad_wq, grad_wk, grad_wv, grad_wo = finish(y_out, grad_x, sum_a, sum_b)
         return y_out.reshape(x_in.shape), grad_x.reshape(x_in.shape), grad_gain, grad_wq, grad_wk, grad_wv, grad_wo

time: 547 us -> 505 us (0.923)
  Pallas kernels: 521 us -> 493 us
  between operations: 14.1 us -> 0.68 us
    pallas_call x1 -> x0, Pallas kernels: 18.6 us -> none  [project_keys(): pl.pallas_call(keys_kernel, grid=(tokens // rows,), in_specs=[tile(d_mode...]
    pallas_call x1, Pallas kernels: 276 us -> 263 us  [backward_norm(): pl.pallas_call(functools.partial(back_kernel, groups, rows, tp, cp), in_s...]
  transfers between devices with their start and end apart: 1 -> 0, of which waited for: 0 -> 0; matrix products, arithmetic and copies ran while one was open for 1% -> 0% of each run, Pallas kernels for 41% -> 0%
where the time goes in v5:
time: 505 us; the launch traced here: 502 us
  Pallas kernels  493 us (98%)
  other arithmetic  7.02 us (1%)
    pallas_call x1, Pallas kernels, backward_norm(): pl.pallas_call(functools.partial(back_kernel, groups, rows, tp, cp), in_s...  263 us
    pallas_call x1, Pallas kernels, front(): pl.pallas_call(functools.partial(front_kernel, batch, seq, tp, cp), in_sp...  206 us
    pallas_call x1, Pallas kernels, finish(): pl.pallas_call(finish_kernel, grid=(blocks,), in_specs=[tile, tile, block...  23.4 us

profile of v5, /device:TPU:0, one launch (start us, length us, event | category | flops | bytes accessed | tf_op | source)
XLA Modules:
  0.0 501.8 jit_solution(15639363726391220095)
XLA Ops:
  0.7 0.8 broadcast_subtract_fusion
  1.5 0.6 reshape.51.start_ref
  2.1 0.1 broadcast_in_dim.4
  2.1 0.1 mul.27
  2.3 6.2 %multiply_sine_fusion = (f32[2304,128]{1,0:T(8,128)}, f32[2304,128]{1,0:T(8,128)}) fusion(f32[128]{0:T(128)S(1)} %mul.27, f32[2304]{0:T(1024)S(1)} %convert_element_type.15), kind=kLoop, calls=%fused_computation | loop fusion | flops 294912 | bytes 2369024 | tf_op jit(solution)/shard_map/sin | solution.py:1059
  8.5 206.4 %front.1 = (bf16[2304,2048]{1,0:T(8,128)(2,1)}, bf16[4,2304,512]{2,1,0:T(8,128)(2,1)}, bf16[2304,512]{1,0:T(8,128)(2,1)}, bf16[2,2304,512]{2,1,0:T(8,128)(2,1)}, bf16[4,512,2048]{2,1,0:T(8,128)(2,1)}) custom-call(bf16[2304,2048]{1,0:T(8,128)(2,1)} %bitcast.7, bf16[2304,2048]{1,0:T(8,128)(2,1)} %bitcast.9, bf16[2048,512]{1,0:T(8,128)(2,1)} %wq_hbm.3, ...), custom_call_target="tpu_custom_call" | custom-call | flops 27179089920 | bytes 75497472 | tf_op jit(solution)/shard_map/front/pallas_call | solution.py:535
  214.9 262.9 %backward_norm.1 = (bf16[2304,2048]{1,0:T(8,128)(2,1)}, bf16[2304,2048]{1,0:T(8,128)(2,1)}, bf16[8,256,2048]{2,1,0:T(8,128)(2,1)}, bf16[8,256,2048]{2,1,0:T(8,128)(2,1)}, f32[1,2048]{1,0:T(1,128)}) custom-call(bf16[2304,512]{1,0:T(8,128)(2,1)} %get-tuple-element.23.dq_hbm, bf16[2,2304,512]{2,1,0:T(8,128)(2,1)} %get-tuple-element.24.dkv_hbm, ...), custom_call_target="tpu_custom_call" | custom-call | flops 53150220288 | bytes 75497472 | tf_op jit(solution)/shard_map/backward_norm/pallas_call | solution.py:982
  477.8 0.0 copy-start
  477.8 23.4 %finish.1 = (bf16[2304,2048]{1,0:T(8,128)(2,1)}, bf16[2304,2048]{1,0:T(8,128)(2,1)}, f32[2048,512]{1,0:T(8,128)}, f32[2048,512]{1,0:T(8,128)}, f32[2048,512]{1,0:T(8,128)}, /*index=5*/f32[512,2048]{1,0:T(8,128)}) custom-call(bf16[2304,2048]{1,0:T(8,128)(2,1)} %get-tuple-element.28.y_ref, bf16[2304,2048]{1,0:T(8,128)(2,1)} %get-tuple-element.29.gx_ref, ...), custom_call_target="tpu_custom_call" | custom-call | flops 8388608 | bytes 71303168 | tf_op jit(solution)/shard_map/finish/pallas_call | solution.py:1034
  501.2 0.0 copy-done
  501.2 0.6 copy.16
  (3 shorter events, 0.0 us)
Async XLA Ops:
  477.8 23.5 %copy-start = (f32[1,2048]{1,0:T(1,128)S(1)}, f32[1,2048]{1,0:T(1,128)}, u32[]{:S(2)}) copy-start(f32[1,2048]{1,0:T(1,128)} %get-tuple-element.34) | copy-start | bytes 24580

commit v6 on v5

--- a/solution.py
+++ b/solution.py
@@ -563,7 +563,10 @@
 
 PART_RING = 4
 RS_RING = 5
-FORWARD_LAG = 7
+FORWARD_LAG = 11
+JOB_LAG = 5
+OUT_LAG = 4
+EARLY = 4
 
 
 def back_kernel(groups, rows, tp, cp, dq_hbm, dkv_hbm, x_hbm, dy_hbm, o_hbm, n_hbm, wq_hbm, wk_hbm, wv_hbm, wo_hbm, gain_ref,
@@ -588,7 +591,13 @@
     partner = {"cp": r + 1 - 2 * core}
     peer = {"cp": r + 2 - 4 * chip}
 
-    weight_loads = [pltpu.make_async_copy(src, dst, w_sem.at[k]) for k, (src, dst) in enumerate(((wq_hbm, wq_ref), (wk_hbm, wk_ref), (wv_hbm, wv_ref), (dq_hbm, dq_all), (dkv_hbm, dkv_all)))]
+    head = min(EARLY, groups) * span
+    weight_loads = [pltpu.make_async_copy(src, dst, w_sem.at[k]) for k, (src, dst) in enumerate((
+        (dq_hbm.at[:head, :], dq_all.at[:head, :]), (dkv_hbm.at[:, :head, :], dkv_all.at[:, :head, :]), (wq_hbm, wq_ref), (wk_hbm, wk_ref), (wv_hbm, wv_ref)))]
+    rest_loads = [] if head == tokens else [
+        pltpu.make_async_copy(dq_hbm.at[head:, :], dq_all.at[head:, :], w_sem.at[6]),
+        pltpu.make_async_copy(dkv_hbm.at[:, head:, :], dkv_all.at[:, head:, :], w_sem.at[7]),
+    ]
     out_loads = [pltpu.make_async_copy(wo_hbm, wo_ref, w_sem.at[5])]
     for copy in weight_loads:
         copy.start()
@@ -853,7 +862,7 @@
         copy.start()
     for copy in inputs(0, 0):
         copy.start()
-    for copy in out_loads:
+    for copy in rest_loads + out_loads:
         copy.start()
     me = z * cp + r
 
@@ -869,7 +878,10 @@
         copy.wait()
 
     def step(i, carry):
-        cur = lax.rem(i, 2)
+        @pl.when(i == EARLY)
+        def _():
+            for copy in rest_loads:
+                copy.wait()
 
         @pl.when(i < groups)
         def _():
@@ -895,36 +907,41 @@
             for copy in final_inputs(i - slots + 1, lax.rem(i - slots + 1, 2)):
                 copy.start()
 
-        @pl.when(i == 0)
-        def _():
-            for copy in out_loads:
-                copy.wait()
+        @pl.when(i == JOB_LAG - 1)
+        def _():
             for k, copy in enumerate(o_loads):
                 copy.wait()
                 o_t[k * width:(k + 1) * width, :] = n_in[k].T
             for copy in job_loads(0, 0):
                 copy.start()
 
-        @pl.when(i < groups)
-        def _():
-            for copy in inputs(i, cur):
+        @pl.when(i == OUT_LAG)
+        def _():
+            for copy in out_loads:
                 copy.wait()
 
-            @pl.when(i + 1 < groups)
+        @pl.when(jnp.logical_and(i >= OUT_LAG, i < groups + OUT_LAG))
+        def _():
+            j = i - OUT_LAG
+            at = lax.rem(j, 2)
+            for copy in inputs(j, at):
+                copy.wait()
+
+            @pl.when(j + 1 < groups)
             def _():
-                for copy in inputs(i + 1, 1 - cur):
+                for copy in inputs(j + 1, 1 - at):
                     copy.start()
 
-            @pl.when(i >= 2)
+            @pl.when(j >= 2)
             def _():
-                y_copy(i - 2, cur).wait()
-
-            project_out(cur)
-            y_copy(i, cur).start()
-
-        @pl.when(jnp.logical_and(i >= 1, i <= blocks))
-        def _():
-            job(i - 1)
+                y_copy(j - 2, at).wait()
+
+            project_out(at)
+            y_copy(j, at).start()
+
+        @pl.when(jnp.logical_and(i >= JOB_LAG, i < JOB_LAG + blocks))
+        def _():
+            job(i - JOB_LAG)
 
         @pl.when(jnp.logical_and(lax.rem(i, 2) == 1, jnp.logical_and(i >= FORWARD_LAG, i < FORWARD_LAG + 2 * pairs)))
         def _():
@@ -934,7 +951,7 @@
 
         return carry
 
-    lax.fori_loop(0, max(groups + 2 * slots, 2 * pairs + FORWARD_LAG - 1), step, 0)
+    lax.fori_loop(0, max(groups + 2 * slots, groups + OUT_LAG, blocks + JOB_LAG, 2 * pairs + FORWARD_LAG - 1), step, 0)
 
     for i in (groups - 2, groups - 1):
         y_copy(i, i % 2).wait()
@@ -998,7 +1015,7 @@
             bf(2, tp, span, hidden), bf(2, span, d_model), bf(2, rows, d_model), bf(2, rows, d_model), bf(2, span, d_model),
             bf(2, tokens, width), bf(2, tokens, width),
             f32(width, 4 * hidden), f32(2, width, 4 * hidden), bf(2, width, 4 * hidden), f32(tp * cp, 1, d_model),
-            dma((6,)), dma((2, 2)), dma((2, 2)), dma((2, 2)), dma((2,)), dma((2,)),
+            dma((8,)), dma((2, 2)), dma((2, 2)), dma((2, 2)), dma((2,)), dma((2,)),
             dma((slots,)), dma((slots,)), dma((RS_RING, slots)), dma((RS_RING, slots)),
             dma((2,)), dma((2,)), dma((slots,)), dma((slots,)), dma((groups, slots)), dma((groups, slots)),
             dma((1,)), dma((2,)), dma((2,)), dma((2,)), dma((2,)), dma((pairs,)), dma((pairs,)), dma((pairs,)), dma((pairs,)),

time: 505 us -> 498 us (0.986)
  no operation moved by 1% of the time
where the time goes in v6:
time: 498 us
  Pallas kernels  489 us (98%)
  other arithmetic  7.02 us (1%)
    pallas_call x1, Pallas kernels, backward_norm(): pl.pallas_call(functools.partial(back_kernel, groups, rows, tp, cp), in_s...  259 us
    pallas_call x1, Pallas kernels, front(): pl.pallas_call(functools.partial(front_kernel, batch, seq, tp, cp), in_sp...  206 us
    pallas_call x1, Pallas kernels, finish(): pl.pallas_call(finish_kernel, grid=(blocks,), in_specs=[tile, tile, block...  23.4 us

profile of v6, /device:TPU:0, one launch (start us, length us, event | category | flops | bytes accessed | tf_op | source)
XLA Modules:
  0.0 497.7 jit_solution(17901310360465502765)
XLA Ops:
  0.7 0.8 broadcast_subtract_fusion
  1.5 0.6 reshape.51.start_ref
  2.1 0.1 broadcast_in_dim.4
  2.1 0.1 mul.27
  2.3 6.2 %multiply_sine_fusion = (f32[2304,128]{1,0:T(8,128)}, f32[2304,128]{1,0:T(8,128)}) fusion(f32[128]{0:T(128)S(1)} %mul.27, f32[2304]{0:T(1024)S(1)} %convert_element_type.15), kind=kLoop, calls=%fused_computation | loop fusion | flops 294912 | bytes 2369024 | tf_op jit(solution)/shard_map/sin | solution.py:1076
  8.5 206.4 %front.1 = (bf16[2304,2048]{1,0:T(8,128)(2,1)}, bf16[4,2304,512]{2,1,0:T(8,128)(2,1)}, bf16[2304,512]{1,0:T(8,128)(2,1)}, bf16[2,2304,512]{2,1,0:T(8,128)(2,1)}, bf16[4,512,2048]{2,1,0:T(8,128)(2,1)}) custom-call(bf16[2304,2048]{1,0:T(8,128)(2,1)} %bitcast.7, bf16[2304,2048]{1,0:T(8,128)(2,1)} %bitcast.9, bf16[2048,512]{1,0:T(8,128)(2,1)} %wq_hbm.3, ...), custom_call_target="tpu_custom_call" | custom-call | flops 27179089920 | bytes 75497472 | tf_op jit(solution)/shard_map/front/pallas_call | solution.py:535
  214.9 258.7 %backward_norm.1 = (bf16[2304,2048]{1,0:T(8,128)(2,1)}, bf16[2304,2048]{1,0:T(8,128)(2,1)}, bf16[8,256,2048]{2,1,0:T(8,128)(2,1)}, bf16[8,256,2048]{2,1,0:T(8,128)(2,1)}, f32[1,2048]{1,0:T(1,128)}) custom-call(bf16[2304,512]{1,0:T(8,128)(2,1)} %get-tuple-element.23.dq_hbm, bf16[2,2304,512]{2,1,0:T(8,128)(2,1)} %get-tuple-element.24.dkv_hbm, ...), custom_call_target="tpu_custom_call" | custom-call | flops 53150220288 | bytes 75497472 | tf_op jit(solution)/shard_map/backward_norm/pallas_call | solution.py:999
  473.6 0.0 copy-start
  473.7 23.4 %finish.1 = (bf16[2304,2048]{1,0:T(8,128)(2,1)}, bf16[2304,2048]{1,0:T(8,128)(2,1)}, f32[2048,512]{1,0:T(8,128)}, f32[2048,512]{1,0:T(8,128)}, f32[2048,512]{1,0:T(8,128)}, /*index=5*/f32[512,2048]{1,0:T(8,128)}) custom-call(bf16[2304,2048]{1,0:T(8,128)(2,1)} %get-tuple-element.28.y_ref, bf16[2304,2048]{1,0:T(8,128)(2,1)} %get-tuple-element.29.gx_ref, ...), custom_call_target="tpu_custom_call" | custom-call | flops 8388608 | bytes 71303168 | tf_op jit(solution)/shard_map/finish/pallas_call | solution.py:1051
  497.1 0.0 copy-done
  497.1 0.6 copy.16
  (3 shorter events, 0.0 us)
Async XLA Ops:
  473.6 23.5 %copy-start = (f32[1,2048]{1,0:T(1,128)S(1)}, f32[1,2048]{1,0:T(1,128)}, u32[]{:S(2)}) copy-start(f32[1,2048]{1,0:T(1,128)} %get-tuple-element.34) | copy-start | bytes 24580

commit v7 on v6

--- a/solution.py
+++ b/solution.py
@@ -51,7 +51,7 @@
 
 MESH = pl.DeviceIdType.MESH
 SUB = 128
-ROWS = 32
+ROWS = 16
 WIDTH = 256
 RELAY_LAG = 2
 CHIP_BUFS = 3

time: 498 us -> 541 us (1.086)
  Pallas kernels: 489 us -> 530 us
    pallas_call x1, Pallas kernels: 259 us -> 300 us  [backward_norm(): pl.pallas_call(functools.partial(back_kernel, groups, rows, tp, cp), in_s...]
where the time goes in v7:
time: 541 us; the launch traced here: 539 us
  Pallas kernels  530 us (98%)
  other arithmetic  7.02 us (1%)
    pallas_call x1, Pallas kernels, backward_norm(): pl.pallas_call(functools.partial(back_kernel, groups, rows, tp, cp), in_s...  300 us
    pallas_call x1, Pallas kernels, front(): pl.pallas_call(functools.partial(front_kernel, batch, seq, tp, cp), in_sp...  206 us
    pallas_call x1, Pallas kernels, finish(): pl.pallas_call(finish_kernel, grid=(blocks,), in_specs=[tile, tile, block...  23.4 us

profile of v7, /device:TPU:0, one launch (start us, length us, event | category | flops | bytes accessed | tf_op | source)
XLA Modules:
  0.0 539.1 jit_solution(5455737348759713275)
XLA Ops:
  0.7 0.8 broadcast_subtract_fusion
  1.5 0.6 reshape.51.start_ref
  2.1 0.1 broadcast_in_dim.4
  2.1 0.1 mul.27
  2.3 6.2 %multiply_sine_fusion = (f32[2304,128]{1,0:T(8,128)}, f32[2304,128]{1,0:T(8,128)}) fusion(f32[128]{0:T(128)S(1)} %mul.27, f32[2304]{0:T(1024)S(1)} %convert_element_type.15), kind=kLoop, calls=%fused_computation | loop fusion | flops 294912 | bytes 2369024 | tf_op jit(solution)/shard_map/sin | solution.py:1076
  8.5 206.4 %front.1 = (bf16[2304,2048]{1,0:T(8,128)(2,1)}, bf16[4,2304,512]{2,1,0:T(8,128)(2,1)}, bf16[2304,512]{1,0:T(8,128)(2,1)}, bf16[2,2304,512]{2,1,0:T(8,128)(2,1)}, bf16[4,512,2048]{2,1,0:T(8,128)(2,1)}) custom-call(bf16[2304,2048]{1,0:T(8,128)(2,1)} %bitcast.7, bf16[2304,2048]{1,0:T(8,128)(2,1)} %bitcast.9, bf16[2048,512]{1,0:T(8,128)(2,1)} %wq_hbm.3, ...), custom_call_target="tpu_custom_call" | custom-call | flops 27179089920 | bytes 75497472 | tf_op jit(solution)/shard_map/front/pallas_call | solution.py:535
  214.9 300.1 %backward_norm.1 = (bf16[2304,2048]{1,0:T(8,128)(2,1)}, bf16[2304,2048]{1,0:T(8,128)(2,1)}, bf16[8,256,2048]{2,1,0:T(8,128)(2,1)}, bf16[8,256,2048]{2,1,0:T(8,128)(2,1)}, f32[1,2048]{1,0:T(1,128)}) custom-call(bf16[2304,512]{1,0:T(8,128)(2,1)} %get-tuple-element.23.dq_hbm, bf16[2,2304,512]{2,1,0:T(8,128)(2,1)} %get-tuple-element.24.dkv_hbm, ...), custom_call_target="tpu_custom_call" | custom-call | flops 53150220288 | bytes 75497472 | tf_op jit(solution)/shard_map/backward_norm/pallas_call | solution.py:999
  515.0 0.0 copy-start
  515.0 23.4 %finish.1 = (bf16[2304,2048]{1,0:T(8,128)(2,1)}, bf16[2304,2048]{1,0:T(8,128)(2,1)}, f32[2048,512]{1,0:T(8,128)}, f32[2048,512]{1,0:T(8,128)}, f32[2048,512]{1,0:T(8,128)}, /*index=5*/f32[512,2048]{1,0:T(8,128)}) custom-call(bf16[2304,2048]{1,0:T(8,128)(2,1)} %get-tuple-element.28.y_ref, bf16[2304,2048]{1,0:T(8,128)(2,1)} %get-tuple-element.29.gx_ref, ...), custom_call_target="tpu_custom_call" | custom-call | flops 8388608 | bytes 71303168 | tf_op jit(solution)/shard_map/finish/pallas_call | solution.py:1051
  538.5 0.0 copy-done
  538.5 0.6 copy.16
  (3 shorter events, 0.0 us)
Async XLA Ops:
  515.0 23.5 %copy-start = (f32[1,2048]{1,0:T(1,128)S(1)}, f32[1,2048]{1,0:T(1,128)}, u32[]{:S(2)}) copy-start(f32[1,2048]{1,0:T(1,128)} %get-tuple-element.34) | copy-start | bytes 24580

commit v8 on v6

--- a/solution.py
+++ b/solution.py
@@ -53,17 +53,18 @@
 SUB = 128
 ROWS = 32
 WIDTH = 256
-RELAY_LAG = 2
-CHIP_BUFS = 3
-W_TWIN = 1
-W_PARTNER = 4
+HALVES = 2
+RELAY_LAG = 4
+CHIP_BUFS = 4
+W_TWIN = 3
+W_PARTNER = 6
 
 
 def front_kernel(batch, seq, tp, cp, x_hbm, dy_hbm, wq_hbm, wk_hbm, wv_hbm, wo_hbm, cos_ref, sin_ref, start_ref, gain_ref,
                  n_hbm, o_all, dq_hbm, dkv_hbm, w_all,
                  big, wo_ref, q_row, do_row, a_in, b_in, kv_own, kvr, s_scr, dp_scr, m_scr, l_scr, d_scr, ot_scr, dqt_scr,
                  o_buf, dq_buf, g_part, g_chip, g_far, xin, part_in,
-                 w_sem, wl_sem, wz_send, wz_recv, wx_send, wx_recv, wp_send, wp_recv, wf_send, wf_recv,
+                 w_sem, wl_sem, wz_send, wz_recv, wx_send, wx_recv,
                  tile_sem, n_sem, kvs_part, kvs_chip, kvs_far, kv_recv, o_local, o_send, o_recv, relay_send, dq_sem,
                  far_send, part_send, chip_send, x_recv, part_recv, dkv_sem):
     z = lax.axis_index("tp")
@@ -97,6 +98,15 @@
     def x_load(t, par):
         return pltpu.make_async_copy(x_hbm.at[tile_rows(t), :], a_in.at[par], tile_sem.at[par, 0])
 
+    units = batch * HALVES
+    half = hidden // HALVES
+
+    def where(u):
+        return lax.div(u, HALVES), lax.rem(u, HALVES)
+
+    def half_cols(g):
+        return pl.ds(pl.multiple_of(g * half, half), half)
+
     def n_load(t, par):
         return pltpu.make_async_copy(n_hbm.at[tile_rows(t), :], a_in.at[par], tile_sem.at[par, 0])
 
@@ -116,12 +126,13 @@
     def remote(src, dst, ssem, rsem, dev):
         return pltpu.make_async_remote_copy(src_ref=src, dst_ref=dst, send_sem=ssem, recv_sem=rsem, device_id=dev, device_id_type=MESH)
 
-    share = hidden // 4
-
-    def share_rows(c, g):
-        return pl.ds(pl.multiple_of((2 * c + g) * share, share), share)
-
-    mine, twins = share_rows(core, dp), share_rows(core, 1 - dp)
+    share = hidden // 8
+
+    def share_rows(y, c, g):
+        return pl.ds(pl.multiple_of((4 * y + 2 * c + g) * share, share), share)
+
+    mine, twins = share_rows(chip, core, dp), share_rows(chip, core, 1 - dp)
+    peers, peer_twins = share_rows(1 - chip, core, dp), share_rows(1 - chip, core, 1 - dp)
 
     def wz_copy(d):
         return remote(wo_hbm.at[mine, :], w_all.at[z, mine, :], wz_send.at[d], wz_recv.at[z], {"tp": lax.rem(z + d, tp)})
@@ -130,29 +141,27 @@
         src = lax.rem(z + d, tp)
         remote(wo_hbm.at[mine, :], w_all.at[src, mine, :], wz_send.at[d], wz_recv.at[src], partner).wait_recv()
 
-    def w_slice(d, rows):
-        return w_all.at[lax.rem(z + d, tp), rows, :]
-
-    def wx_copy(d):
-        return remote(w_slice(d, mine), w_slice(d, mine), wx_send.at[d], wx_recv.at[d], twin)
-
-    def wp_copy(d):
-        return remote(w_slice(d, mine), w_slice(d, mine), wp_send.at[d], wp_recv.at[d], partner)
-
-    def wf_copy(d):
-        return remote(w_slice(d, twins), w_slice(d, twins), wf_send.at[d], wf_recv.at[d], partner)
+    def w_copy(k, d, rows, dev):
+        place = w_all.at[lax.rem(z + d, tp), rows, :]
+        return remote(place, place, wx_send.at[k, d], wx_recv.at[k, d], dev)
+
+    def w_move(k, d):
+        rows, dev = ((mine, twin), (mine, partner), (twins, partner), (mine, peer), (twins, peer), (peers, partner), (peer_twins, partner))[k]
+        return w_copy(k, d, rows, dev)
+
+    w_steps = range(1, tp)
 
     for d in range(1, tp):
         wz_copy(d).start()
 
-    def kv_to_partner(b):
-        return remote(kv_own.at[b], kvr.at[0, b], kvs_part.at[b], kv_recv.at[0, b], partner)
-
-    def kv_to_chip(b):
-        return remote(kv_own.at[b], kvr.at[1, b], kvs_chip.at[b], kv_recv.at[1, b], peer)
-
-    def kv_forward(b):
-        return remote(kvr.at[1, b], kvr.at[2, b], kvs_far.at[b], kv_recv.at[2, b], partner)
+    def kv_to_partner(u):
+        return remote(kv_own.at[u], kvr.at[0, u], kvs_part.at[u], kv_recv.at[0, u], partner)
+
+    def kv_to_chip(u):
+        return remote(kv_own.at[u], kvr.at[1, u], kvs_chip.at[u], kv_recv.at[1, u], peer)
+
+    def kv_forward(u):
+        return remote(kvr.at[1, u], kvr.at[2, u], kvs_far.at[u], kv_recv.at[2, u], partner)
 
     for copy in weight_loads:
         copy.wait()
@@ -181,18 +190,21 @@
         part = lax.rem(t, per_row)
         inside = pl.ds(pl.multiple_of(part * tile, tile), tile)
         rows = tile_rows(t)
-        put_rope(kv_own.at[b, 0, inside, :], dot_nn(normed, big[0]), cos_ref[rows, :], sin_ref[rows, :])
-        kv_own[b, 1, inside, :] = dot_nn(normed, big[1]).astype(BF16)
-
-        @pl.when(part == per_row - 1)
-        def _():
-            @pl.when(first_chip)
-            def _():
-                kv_to_chip(b).start()
-
-            @pl.when(first_core)
-            def _():
-                kv_to_partner(b).start()
+        for g in range(HALVES):
+            u = b * HALVES + g
+            cols = slice(g * half, (g + 1) * half)
+            put_rope(kv_own.at[u, 0, inside, :], dot_nn(normed, big[0, :, cols]), cos_ref[rows, :], sin_ref[rows, :])
+            kv_own[u, 1, inside, :] = dot_nn(normed, big[1, :, cols]).astype(BF16)
+
+            @pl.when(part == per_row - 1)
+            def _(u=u):
+                @pl.when(first_chip)
+                def _():
+                    kv_to_chip(u).start()
+
+                @pl.when(first_core)
+                def _():
+                    kv_to_partner(u).start()
 
         return carry
 
@@ -225,15 +237,19 @@
 
     fit = d_model // seq
 
-    def g_own(b, which):
+    def g_own(b, which, cols):
         k = 2 * b + which
-        return big.at[lax.div(k, fit), pl.ds(pl.multiple_of(lax.rem(k, fit) * seq, seq), seq), :]
+        return big.at[lax.div(k, fit), pl.ds(pl.multiple_of(lax.rem(k, fit) * seq, seq), seq), cols]
+
+    def o_place(src, u):
+        b, g = where(u)
+        return o_all.at[src, row(b), half_cols(g)]
 
     def o_local_copy(b):
-        return pltpu.make_async_copy(o_buf.at[b], o_all.at[z, row(b), :], o_local.at[b])
+        return pltpu.make_async_copy(o_buf.at[b], o_place(z, b), o_local.at[b])
 
     def o_copy(b, k, step):
-        return remote(o_buf.at[b], o_all.at[z, row(b), :], o_send.at[k, b], o_recv.at[z, b], {"tp": jnp.clip(z + step, 0, tp - 1)})
+        return remote(o_buf.at[b], o_place(z, b), o_send.at[k, b], o_recv.at[z, b], {"tp": jnp.clip(z + step, 0, tp - 1)})
 
     hops = [(k, step, jnp.logical_and(z + step >= 0, z + step < tp)) for k, step in enumerate((1, -1, 2, -2))]
 
@@ -245,10 +261,10 @@
                 o_copy(b, k, step).start()
 
     def o_arrived(src, b):
-        remote(o_all.at[src, row(b), :], o_all.at[src, row(b), :], relay_send.at[b], o_recv.at[src, b], partner).wait_recv()
+        remote(o_place(src, b), o_place(src, b), relay_send.at[b], o_recv.at[src, b], partner).wait_recv()
 
     def relay_copy(b, src, dst):
-        return remote(o_all.at[src, row(b), :], o_all.at[src, row(b), :], relay_send.at[b], o_recv.at[src, b], {"tp": dst})
+        return remote(o_place(src, b), o_place(src, b), relay_send.at[b], o_recv.at[src, b], {"tp": dst})
 
     def relay(b):
         @pl.when(z == tp - 2)
@@ -279,45 +295,52 @@
             g_chip[par] = (g_chip[par].astype(F32) + xin[b].astype(F32)).astype(BF16)
             chip_copy(b).start()
 
-    def dkv_store(b, which):
-        return pltpu.make_async_copy(g_own(b, which), dkv_hbm.at[which, row(b), :], dkv_sem.at[b, which])
-
-    def key_grads(b):
+    def own_half(u, which):
+        b, g = where(u)
+        return g_own(b, which, half_cols(g))
+
+    def dkv_store(u, which):
+        b, g = where(u)
+        return pltpu.make_async_copy(own_half(u, which), dkv_hbm.at[which, row(b), half_cols(g)], dkv_sem.at[u, which])
+
+    def key_grads(u):
         @pl.when(first_core)
         def _():
-            part_copy(b, 0).wait_recv()
+            part_copy(u, 0).wait_recv()
 
         @pl.when(first_chip)
         def _():
-            chip_copy(b).wait_recv()
-
+            chip_copy(u).wait_recv()
+
+        b, g = where(u)
         rows = row(b)
         for which in range(2):
-            own = g_own(b, which)
-            for h in range(heads):
+            for h in range(half // HEAD_DIM):
                 cols = slice(h * HEAD_DIM, (h + 1) * HEAD_DIM)
-                acc = own[:, cols].astype(F32)
-                acc = acc + jnp.where(first_core, part_in[b, which, :, cols].astype(F32), 0.0)
-                acc = (acc + jnp.where(first_chip, xin[b, which, :, cols].astype(F32), 0.0)).astype(BF16)
+                own = g_own(b, which, pl.ds(pl.multiple_of(g * half + h * HEAD_DIM, HEAD_DIM), HEAD_DIM))
+                acc = own[...].astype(F32)
+                acc = acc + jnp.where(first_core, part_in[u, which, :, cols].astype(F32), 0.0)
+                acc = (acc + jnp.where(first_chip, xin[u, which, :, cols].astype(F32), 0.0)).astype(BF16)
                 if which == 0:
                     acc = rope(acc.astype(F32), cos_ref[rows, :], sin_ref[rows, :], -1.0).astype(BF16)
-                own[:, cols] = acc
-            dkv_store(b, which).start()
+                own[...] = acc
+            dkv_store(u, which).start()
 
     def dq_store(b, par):
-        return pltpu.make_async_copy(dq_buf.at[par], dq_hbm.at[row(b), :], dq_sem.at[par])
+        return pltpu.make_async_copy(dq_buf.at[par], dq_hbm.at[row(where(b)[0]), half_cols(where(b)[1])], dq_sem.at[par])
 
     subs = range(0, seq, SUB)
 
-    def attend_row(i, par):
-        rows = row(i)
-        start = start_ref[i]
+    def attend_unit(i, par):
+        b, g = where(i)
+        rows = row(b)
+        start = start_ref[b]
         chip_par = lax.rem(i, CHIP_BUFS)
         keys_of = [kv_own.at[i]] + [kvr.at[s, i] for s in range(3)]
         places = [g_part.at[par], g_chip.at[chip_par], g_far.at[par]]
 
-        def grad(slot, which):
-            return places[slot - 1].at[which] if slot else g_own(i, which)
+        def grad(slot, which, cols, full):
+            return places[slot - 1].at[which, :, cols] if slot else g_own(b, which, full)
 
         live = [None, second_core, second_chip, second_chip]
         piece = [r, r + 1 - 2 * core, r + 2 - 4 * chip, r + 3 - 2 * core - 4 * chip]
@@ -329,8 +352,9 @@
 
         def one_head(h, carry):
             cols = pl.ds(pl.multiple_of(h * HEAD_DIM, HEAD_DIM), HEAD_DIM)
-            q = q_row[:, cols]
-            do = do_row[:, cols]
+            full = pl.ds(pl.multiple_of(g * half + h * HEAD_DIM, HEAD_DIM), HEAD_DIM)
+            q = q_row[:, full]
+            do = do_row[:, full]
             m_scr[...] = jnp.full(m_scr.shape, NEG_BIG, F32)
             l_scr[...] = jnp.zeros_like(l_scr)
             d_scr[...] = jnp.zeros_like(d_scr)
@@ -364,14 +388,14 @@
                     s_scr[slot, s:s + SUB, :] = prob
                     dp_scr[slot, s:s + SUB, :] = dp
                     d_scr[...] += jnp.sum(prob * dp, axis=0, keepdims=True)
-                    grad(slot, 1)[s:s + SUB, cols] = dot_nn(low, do).astype(BF16)
+                    grad(slot, 1, cols, full)[s:s + SUB, :] = dot_nn(low, do).astype(BF16)
                     ot_scr[...] += dot_nn(v.T, low)
 
             def keys(slot):
                 for s in subs:
                     k = keys_of[slot][0, s:s + SUB, cols]
                     ds = (s_scr[slot, s:s + SUB, :] * (dp_scr[slot, s:s + SUB, :] - d_scr[...])).astype(BF16)
-                    grad(slot, 0)[s:s + SUB, cols] = (dot_nn(ds, q) * SCALE).astype(BF16)
+                    grad(slot, 0, cols, full)[s:s + SUB, :] = (dot_nn(ds, q) * SCALE).astype(BF16)
                     dqt_scr[...] += dot_nn(k.T, ds)
 
             each(scores)
@@ -383,11 +407,13 @@
             dq_buf[par, :, cols] = rope(dqt_scr[...].T * SCALE, cos_ref[rows, :], sin_ref[rows, :], -1.0).astype(BF16)
             return carry
 
-        lax.fori_loop(0, heads, one_head, 0)
+        lax.fori_loop(0, heads // HALVES, one_head, 0)
 
     def step(i, carry):
         par = lax.rem(i, 2)
-        query_row(i)
+        @pl.when(lax.rem(i, HALVES) == 0)
+        def _():
+            query_row(lax.div(i, HALVES))
 
         @pl.when(second_chip)
         def _():
@@ -418,7 +444,7 @@
         def _():
             chip_copy(i - CHIP_BUFS).wait_send()
 
-        attend_row(i, par)
+        attend_unit(i, par)
         o_start(i)
         dq_store(i, par).start()
 
@@ -438,74 +464,98 @@
         def _():
             relay(i - RELAY_LAG)
 
-        @pl.when(i == min(W_TWIN, batch - 1))
-        def _():
-            for d in range(1, tp):
+        @pl.when(i == min(W_TWIN, units - 1))
+        def _():
+            for d in w_steps:
                 wz_wait(d)
-                wx_copy(d).start()
-                wp_copy(d).start()
-
-        @pl.when(i == min(W_PARTNER, batch - 1))
-        def _():
-            for d in range(1, tp):
-                wx_copy(d).wait_recv()
-                wf_copy(d).start()
+                w_move(0, d).start()
+                w_move(1, d).start()
+
+                @pl.when(second_chip)
+                def _(d=d):
+                    w_move(3, d).start()
+
+        @pl.when(i == min(W_PARTNER, units - 1))
+        def _():
+            for d in w_steps:
+                w_move(0, d).wait_recv()
+                w_move(2, d).start()
+
+                @pl.when(second_chip)
+                def _(d=d):
+                    w_move(4, d).start()
 
         return carry
 
-    lax.fori_loop(0, batch, step, 0)
-    chip_sum(batch - 1)
-    lag = min(RELAY_LAG, batch)
-    for k in range(lag):
-        relay(batch - lag + k)
-
-    def finish(b, carry):
-        key_grads(b)
+    lax.fori_loop(0, units, step, 0)
+    chip_sum(units - 1)
+
+    @pl.when(first_chip)
+    def _():
+        for u in range(units):
+            kv_to_chip(u).wait_send()
+        for k in (3, 4):
+            for d in w_steps:
+                w_move(k, d).start()
+
+    lag = min(RELAY_LAG, units)
+
+    def finish(u, carry):
+        @pl.when(u < lag)
+        def _():
+            relay(units - lag + u)
+
+        key_grads(u)
         return carry
 
-    lax.fori_loop(0, batch, finish, 0)
+    lax.fori_loop(0, units, finish, 0)
+    for k in (3, 4):
+        for d in w_steps:
+            w_move(k, d).wait_recv()
+            w_move(k + 2, d).start()
 
     w_local.wait()
-    for d in range(1, tp):
+    for d in w_steps:
         wz_copy(d).wait_send()
-        wx_copy(d).wait_send()
-        for copy in (wp_copy(d), wf_copy(d)):
-            copy.wait_send()
-            copy.wait_recv()
-    for b in range(batch):
+        for k in range(7):
+            w_move(k, d).wait_send()
+            if k in (1, 2, 5, 6):
+                w_move(k, d).wait_recv()
+
+    def drain(b, carry):
         for which in range(2):
             dkv_store(b, which).wait()
 
-        @pl.when(first_chip)
-        def _(b=b):
-            kv_to_chip(b).wait_send()
-
         @pl.when(first_core)
-        def _(b=b):
+        def _():
             kv_to_partner(b).wait_send()
 
         @pl.when(second_chip)
-        def _(b=b):
+        def _():
             kv_forward(b).wait_send()
 
         o_local_copy(b).wait()
         for k, step_, ok in hops:
             @pl.when(ok)
-            def _(b=b, k=k, step_=step_):
+            def _(k=k, step_=step_):
                 o_copy(b, k, step_).wait_send()
 
         @pl.when(jnp.logical_or(z == 1, z == tp - 2))
-        def _(b=b):
+        def _():
             relay_copy(b, 0, tp - 1).wait_send()
 
         for src in range(tp):
             taken = jnp.logical_or(jnp.logical_and(z == tp - 2, src == 0), jnp.logical_and(z == 1, src == tp - 1))
 
             @pl.when(jnp.logical_and(z != src, jnp.logical_not(taken)))
-            def _(b=b, src=src):
+            def _(src=src):
                 o_arrived(src, b)
 
-    for b in range(max(0, batch - 2), batch):
+        return carry
+
+    lax.fori_loop(0, units, drain, 0)
+
+    for b in range(max(0, units - 2), units):
         dq_store(b, b % 2).wait()
 
         @pl.when(second_core)
@@ -516,7 +566,7 @@
         def _(b=b):
             far_copy(b, b % 2).wait_send()
 
-    for b in range(max(0, batch - CHIP_BUFS), batch):
+    for b in range(max(0, units - CHIP_BUFS), units):
         @pl.when(second_chip)
         def _(b=b):
             chip_copy(b).wait_send()
@@ -526,6 +576,8 @@
     tokens, d_model = x.shape
     hidden = wq.shape[1]
     batch = tokens // seq
+    units = batch * HALVES
+    half = hidden // HALVES
     tile = seq // 2
     hbm = pl.BlockSpec(memory_space=pl.ANY)
     vmem = pl.BlockSpec(memory_space=pltpu.VMEM)
@@ -545,15 +597,15 @@
         ],
         scratch_shapes=[
             bf(3, d_model, hidden), bf(hidden, d_model), bf(seq, hidden), bf(seq, hidden), bf(2, tile, d_model), bf(2, tile, d_model),
-            bf(batch, 2, seq, hidden), bf(3, batch, 2, seq, hidden),
+            bf(units, 2, seq, half), bf(3, units, 2, seq, half),
             f32(4, seq, seq), f32(4, seq, seq), f32(1, seq), f32(1, seq), f32(1, seq), f32(HEAD_DIM, seq), f32(HEAD_DIM, seq),
-            bf(batch, seq, hidden), bf(2, seq, hidden),
-            bf(2, 2, seq, hidden), bf(CHIP_BUFS, 2, seq, hidden), bf(2, 2, seq, hidden),
-            bf(batch, 2, seq, hidden), bf(batch, 2, seq, hidden),
-            dma((4,)), dma((1,)), dma((tp,)), dma((tp,)), dma((tp,)), dma((tp,)), dma((tp,)), dma((tp,)), dma((tp,)), dma((tp,)),
-            dma((2, 2)), dma((2,)), dma((batch,)), dma((batch,)), dma((batch,)), dma((3, batch)),
-            dma((batch,)), dma((4, batch)), dma((tp, batch)), dma((batch,)), dma((2,)),
-            dma((2,)), dma((2,)), dma((CHIP_BUFS,)), dma((batch,)), dma((batch,)), dma((batch, 2)),
+            bf(units, seq, half), bf(2, seq, half),
+            bf(2, 2, seq, half), bf(CHIP_BUFS, 2, seq, half), bf(2, 2, seq, half),
+            bf(units, 2, seq, half), bf(units, 2, seq, half),
+            dma((4,)), dma((1,)), dma((tp,)), dma((tp,)), dma((7, tp)), dma((7, tp)),
+            dma((2, 2)), dma((2,)), dma((units,)), dma((units,)), dma((units,)), dma((3, units)),
+            dma((units,)), dma((4, units)), dma((tp, units)), dma((units,)), dma((2,)),
+            dma((2,)), dma((2,)), dma((CHIP_BUFS,)), dma((units,)), dma((units,)), dma((units, 2)),
         ],
         compiler_params=pltpu.CompilerParams(collective_id=1, has_side_effects=True, vmem_limit_bytes=63 << 20),
         cost_estimate=pl.CostEstimate(flops=60 * tokens * seq * hidden, bytes_accessed=16 * tokens * d_model, transcendentals=4 * tokens * seq * (hidden // HEAD_DIM)),
@@ -878,6 +930,9 @@
         copy.wait()
 
     def step(i, carry):
+        for k in reversed(range(1, slots)):
+            rs_send(i - k, k)
+
         @pl.when(i == EARLY)
         def _():
             for copy in rest_loads:
@@ -887,14 +942,14 @@
         def _():
             partial_norm(i)
 
+        rs_send(i, 0)
+
+        @pl.when(jnp.logical_and(i >= slots, i < groups + slots))
+        def _():
+            finalize(i - slots)
+
         for a in range(1, slots + 1):
             ag_step(i - slots - a, a)
-        for s in reversed(range(slots)):
-            rs_send(i - s, s)
-
-        @pl.when(jnp.logical_and(i >= slots, i < groups + slots))
-        def _():
-            finalize(i - slots)
 
         @pl.when(i == groups + slots - 1)
         def _():

time: 498 us -> 481 us (0.966)
  Pallas kernels: 489 us -> 471 us
    pallas_call x1, Pallas kernels: 259 us -> 248 us  [backward_norm(): pl.pallas_call(functools.partial(back_kernel, groups, rows, tp, cp), in_s...]
    pallas_call x1, Pallas kernels: 206 us -> 200 us  [front(): pl.pallas_call(functools.partial(front_kernel, batch, seq, tp, cp), in_sp...]
where the time goes in v8:
time: 481 us
  Pallas kernels  471 us (98%)
  other arithmetic  7.02 us (1%)
    pallas_call x1, Pallas kernels, backward_norm(): pl.pallas_call(functools.partial(back_kernel, groups, rows, tp, cp), in_s...  248 us
    pallas_call x1, Pallas kernels, front(): pl.pallas_call(functools.partial(front_kernel, batch, seq, tp, cp), in_sp...  200 us
    pallas_call x1, Pallas kernels, finish(): pl.pallas_call(finish_kernel, grid=(blocks,), in_specs=[tile, tile, block...  23.4 us

profile of v8, /device:TPU:0, one launch (start us, length us, event | category | flops | bytes accessed | tf_op | source)
XLA Modules:
  0.0 480.5 jit_solution(4937147889821600942)
XLA Ops:
  0.7 0.8 broadcast_subtract_fusion
  1.5 0.6 reshape.51.start_ref
  2.1 0.1 broadcast_in_dim.4
  2.1 0.1 mul.27
  2.3 6.2 %multiply_sine_fusion = (f32[2304,128]{1,0:T(8,128)}, f32[2304,128]{1,0:T(8,128)}) fusion(f32[128]{0:T(128)S(1)} %mul.27, f32[2304]{0:T(1024)S(1)} %convert_element_type.15), kind=kLoop, calls=%fused_computation | loop fusion | flops 294912 | bytes 2369024 | tf_op jit(solution)/shard_map/sin | solution.py:1131
  8.5 200.5 %front.1 = (bf16[2304,2048]{1,0:T(8,128)(2,1)}, bf16[4,2304,512]{2,1,0:T(8,128)(2,1)}, bf16[2304,512]{1,0:T(8,128)(2,1)}, bf16[2,2304,512]{2,1,0:T(8,128)(2,1)}, bf16[4,512,2048]{2,1,0:T(8,128)(2,1)}) custom-call(bf16[2304,2048]{1,0:T(8,128)(2,1)} %bitcast.7, bf16[2304,2048]{1,0:T(8,128)(2,1)} %bitcast.9, bf16[2048,512]{1,0:T(8,128)(2,1)} %wq_hbm.3, ...), custom_call_target="tpu_custom_call" | custom-call | flops 27179089920 | bytes 75497472 | tf_op jit(solution)/shard_map/front/pallas_call | solution.py:587
  209.0 247.5 %backward_norm.1 = (bf16[2304,2048]{1,0:T(8,128)(2,1)}, bf16[2304,2048]{1,0:T(8,128)(2,1)}, bf16[8,256,2048]{2,1,0:T(8,128)(2,1)}, bf16[8,256,2048]{2,1,0:T(8,128)(2,1)}, f32[1,2048]{1,0:T(1,128)}) custom-call(bf16[2304,512]{1,0:T(8,128)(2,1)} %get-tuple-element.23.dq_hbm, bf16[2,2304,512]{2,1,0:T(8,128)(2,1)} %get-tuple-element.24.dkv_hbm, ...), custom_call_target="tpu_custom_call" | custom-call | flops 53150220288 | bytes 75497472 | tf_op jit(solution)/shard_map/backward_norm/pallas_call | solution.py:1054
  456.5 0.0 copy-start
  456.5 23.4 %finish.1 = (bf16[2304,2048]{1,0:T(8,128)(2,1)}, bf16[2304,2048]{1,0:T(8,128)(2,1)}, f32[2048,512]{1,0:T(8,128)}, f32[2048,512]{1,0:T(8,128)}, f32[2048,512]{1,0:T(8,128)}, /*index=5*/f32[512,2048]{1,0:T(8,128)}) custom-call(bf16[2304,2048]{1,0:T(8,128)(2,1)} %get-tuple-element.28.y_ref, bf16[2304,2048]{1,0:T(8,128)(2,1)} %get-tuple-element.29.gx_ref, ...), custom_call_target="tpu_custom_call" | custom-call | flops 8388608 | bytes 71303168 | tf_op jit(solution)/shard_map/finish/pallas_call | solution.py:1106
  479.9 0.0 copy-done
  479.9 0.6 copy.16
  (3 shorter events, 0.0 us)
Async XLA Ops:
  456.5 23.5 %copy-start = (f32[1,2048]{1,0:T(1,128)S(1)}, f32[1,2048]{1,0:T(1,128)}, u32[]{:S(2)}) copy-start(f32[1,2048]{1,0:T(1,128)} %get-tuple-element.34) | copy-start | bytes 24580

commit v9 on v8

--- a/solution.py
+++ b/solution.py
@@ -3,6 +3,7 @@
 
 import jax
 import jax.numpy as jnp
+import numpy as np
 from jax import lax
 from jax.experimental import pallas as pl
 from jax.experimental.pallas import tpu as pltpu
@@ -43,6 +44,22 @@
     return t * cos_t + swap_pairs(t, sign) * sin_t
 
 
+def angle_table():
+    inv_freq = ROPE_THETA ** (-np.arange(0, HEAD_DIM, 2, dtype=np.float32) / np.float32(HEAD_DIM))
+    freq = np.repeat(inv_freq.astype(np.float64), 2)[None, :]
+    low = np.arange(POS_LOW)[:, None] * freq
+    high = POS_LOW * np.arange(HEAD_DIM - POS_LOW)[:, None] * freq
+    table = np.zeros((HEAD_DIM, 12 * HEAD_DIM), np.float32)
+    for k, (first, value) in enumerate(((0, np.cos(low)), (0, np.sin(low)), (POS_LOW, np.cos(high)), (POS_LOW, np.sin(high)))):
+        rest = value.astype(np.float32)
+        for p in range(3):
+            piece = rest.astype(BF16).astype(np.float32)
+            at = (3 * k + p) * HEAD_DIM
+            table[first:first + value.shape[0], at:at + HEAD_DIM] = piece
+            rest = rest - piece
+    return table
+
+
 def put_rope(dst, raw, cos_t, sin_t):
     for h in range(raw.shape[1] // HEAD_DIM):
         cols = slice(h * HEAD_DIM, (h + 1) * HEAD_DIM)
@@ -51,21 +68,25 @@
 
 MESH = pl.DeviceIdType.MESH
 SUB = 128
-ROWS = 32
+ROWS = 16
 WIDTH = 256
 HALVES = 2
 RELAY_LAG = 4
 CHIP_BUFS = 4
+OWN_RING = 6
+Q_RING = 3
+AHEAD = 2
+POS_LOW = 64
 W_TWIN = 3
 W_PARTNER = 6
 
 
-def front_kernel(batch, seq, tp, cp, x_hbm, dy_hbm, wq_hbm, wk_hbm, wv_hbm, wo_hbm, cos_ref, sin_ref, start_ref, gain_ref,
+def front_kernel(batch, seq, tp, cp, x_hbm, dy_hbm, wq_hbm, wk_hbm, wv_hbm, wo_hbm, pos_ref, table_ref, gain_ref,
                  n_hbm, o_all, dq_hbm, dkv_hbm, w_all,
-                 big, wo_ref, q_row, do_row, a_in, b_in, kv_own, kvr, s_scr, dp_scr, m_scr, l_scr, d_scr, ot_scr, dqt_scr,
-                 o_buf, dq_buf, g_part, g_chip, g_far, xin, part_in,
+                 big, wo_ref, cos_ref, sin_ref, q_ring, do_ring, x_in, dy_in, n_buf, kv_own, kvr, s_scr, dp_scr, m_scr, l_scr, d_scr, ot_scr, dqt_scr,
+                 o_buf, dq_buf, g_own, g_part, g_chip, g_far, xin, part_in,
                  w_sem, wl_sem, wz_send, wz_recv, wx_send, wx_recv,
-                 tile_sem, n_sem, kvs_part, kvs_chip, kvs_far, kv_recv, o_local, o_send, o_recv, relay_send, dq_sem,
+                 x_sem, dy_sem, n_sem, kvs_part, kvs_chip, kvs_far, kv_recv, o_local, o_send, o_recv, relay_send, dq_sem,
                  far_send, part_send, chip_send, x_recv, part_recv, dkv_sem):
     z = lax.axis_index("tp")
     r = lax.axis_index("cp")
@@ -81,22 +102,34 @@
     peer = {"cp": r + 2 - 4 * chip}
     twin = {"dp": 1 - dp}
 
-    weight_loads = [pltpu.make_async_copy(src, dst, w_sem.at[k]) for k, (src, dst) in enumerate(((wk_hbm, big.at[0]), (wv_hbm, big.at[1]), (wq_hbm, big.at[2]), (wo_hbm, wo_ref)))]
-    for copy in weight_loads:
-        copy.start()
-
-    tile = a_in.shape[1]
+    tile = x_in.shape[1]
     per_row = seq // tile
-    tiles = batch * per_row
-
-    def tile_rows(t):
-        return pl.ds(pl.multiple_of(t * tile, tile), tile)
 
     def row(b):
         return pl.ds(pl.multiple_of(b * seq, seq), seq)
 
-    def x_load(t, par):
-        return pltpu.make_async_copy(x_hbm.at[tile_rows(t), :], a_in.at[par], tile_sem.at[par, 0])
+    def tile_rows(b, k):
+        return pl.ds(pl.multiple_of(b * seq + k * tile, tile), tile)
+
+    def x_load(b, k):
+        return pltpu.make_async_copy(x_hbm.at[tile_rows(b, k), :], x_in.at[k], x_sem.at[k])
+
+    def dy_load(b, k):
+        return pltpu.make_async_copy(dy_hbm.at[tile_rows(b, k), :], dy_in.at[k], dy_sem.at[k])
+
+    def n_store(b, k):
+        return pltpu.make_async_copy(n_buf.at[k], n_hbm.at[tile_rows(b, k), :], n_sem.at[k])
+
+    weight_loads = [pltpu.make_async_copy(src, dst, w_sem.at[k]) for k, (src, dst) in enumerate(((wk_hbm, big.at[0]), (wv_hbm, big.at[1]), (wq_hbm, big.at[2]), (wo_hbm, wo_ref)))]
+    x_load(0, 0).start()
+    for copy in weight_loads[:2]:
+        copy.start()
+    for k in range(1, per_row):
+        x_load(0, k).start()
+    for copy in weight_loads[2:]:
+        copy.start()
+    for k in range(per_row):
+        dy_load(0, k).start()
 
     units = batch * HALVES
     half = hidden // HALVES
@@ -106,17 +139,6 @@
 
     def half_cols(g):
         return pl.ds(pl.multiple_of(g * half, half), half)
-
-    def n_load(t, par):
-        return pltpu.make_async_copy(n_hbm.at[tile_rows(t), :], a_in.at[par], tile_sem.at[par, 0])
-
-    def dy_load(t, par):
-        return pltpu.make_async_copy(dy_hbm.at[tile_rows(t), :], b_in.at[par], tile_sem.at[par, 1])
-
-    def n_store(t, par):
-        return pltpu.make_async_copy(b_in.at[par], n_hbm.at[tile_rows(t), :], n_sem.at[par])
-
-    x_load(0, 0).start()
 
     barrier = pltpu.get_barrier_semaphore()
     for dev in [partner, peer, twin] + [{"tp": lax.rem(z + dt, tp)} for dt in range(1, tp)]:
@@ -163,83 +185,81 @@
     def kv_forward(u):
         return remote(kvr.at[1, u], kvr.at[2, u], kvs_far.at[u], kv_recv.at[2, u], partner)
 
-    for copy in weight_loads:
+    w_local = pltpu.make_async_copy(wo_ref, w_all.at[z], wl_sem.at[0])
+    for copy in weight_loads[:2]:
         copy.wait()
-    w_local = pltpu.make_async_copy(wo_ref, w_all.at[z], wl_sem.at[0])
-    w_local.start()
-
-    def key_tile(t, carry):
-        par = lax.rem(t, 2)
-        x_load(t, par).wait()
-
-        @pl.when(t + 1 < tiles)
-        def _():
-            x_load(t + 1, 1 - par).start()
-
-        @pl.when(t >= 2)
-        def _():
-            n_store(t - 2, par).wait()
-
-        x = a_in[par].astype(F32)
-        centred = x - jnp.mean(x, axis=-1, keepdims=True)
-        inv_std = lax.rsqrt(jnp.mean(centred * centred, axis=-1, keepdims=True) + LN_EPS)
-        normed = ((centred * inv_std) * gain_ref[...]).astype(BF16)
-        b_in[par] = normed
-        n_store(t, par).start()
-        b = lax.div(t, per_row)
-        part = lax.rem(t, per_row)
-        inside = pl.ds(pl.multiple_of(part * tile, tile), tile)
-        rows = tile_rows(t)
+
+    def angles(b, k):
+        rows = tile_rows(b, k)
+        pos = jnp.broadcast_to(pos_ref[b, :, k * tile:(k + 1) * tile], (HEAD_DIM, tile)).T
+        lane = lax.broadcasted_iota(jnp.int32, (tile, HEAD_DIM), 1)
+        low = lane < POS_LOW
+        pick = jnp.where(low, lax.rem(pos, POS_LOW), POS_LOW + lax.div(pos, POS_LOW)) == lane
+        found = dot_nn(jnp.where(pick, 1.0, 0.0).astype(BF16), table_ref[...])
+
+        def part(k):
+            at = 3 * k * HEAD_DIM
+            return found[:, at:at + HEAD_DIM] + found[:, at + HEAD_DIM:at + 2 * HEAD_DIM] + found[:, at + 2 * HEAD_DIM:at + 3 * HEAD_DIM]
+
+        cos_b, sin_b, cos_a, sin_a = part(0), part(1), part(2), part(3)
+        cos_ref[rows, :] = cos_a * cos_b - sin_a * sin_b
+        sin_ref[rows, :] = sin_a * cos_b + cos_a * sin_b
+
+    def project_row(b):
+        ring = lax.rem(b, Q_RING)
+        for k in range(per_row):
+            rows = tile_rows(b, k)
+            inside = slice(k * tile, (k + 1) * tile)
+            x_load(b, k).wait()
+
+            @pl.when(b > 0)
+            def _(k=k):
+                n_store(b - 1, k).wait()
+
+            angles(b, k)
+            x = x_in[k].astype(F32)
+            centred = x - jnp.mean(x, axis=-1, keepdims=True)
+            inv_std = lax.rsqrt(jnp.mean(centred * centred, axis=-1, keepdims=True) + LN_EPS)
+            n_buf[k] = ((centred * inv_std) * gain_ref[...]).astype(BF16)
+            n_store(b, k).start()
+
+            @pl.when(b + 1 < batch)
+            def _(k=k):
+                x_load(b + 1, k).start()
+
+            for g in range(HALVES):
+                u = b * HALVES + g
+                cols = slice(g * half, (g + 1) * half)
+                put_rope(kv_own.at[u, 0, inside, :], dot_nn(n_buf[k], big[0, :, cols]), cos_ref[rows, :], sin_ref[rows, :])
+                kv_own[u, 1, inside, :] = dot_nn(n_buf[k], big[1, :, cols]).astype(BF16)
+
         for g in range(HALVES):
             u = b * HALVES + g
-            cols = slice(g * half, (g + 1) * half)
-            put_rope(kv_own.at[u, 0, inside, :], dot_nn(normed, big[0, :, cols]), cos_ref[rows, :], sin_ref[rows, :])
-            kv_own[u, 1, inside, :] = dot_nn(normed, big[1, :, cols]).astype(BF16)
-
-            @pl.when(part == per_row - 1)
+
+            @pl.when(first_chip)
             def _(u=u):
-                @pl.when(first_chip)
-                def _():
-                    kv_to_chip(u).start()
-
-                @pl.when(first_core)
-                def _():
-                    kv_to_partner(u).start()
-
-        return carry
-
-    lax.fori_loop(0, tiles, key_tile, 0)
-    for t in range(tiles - 2, tiles):
-        n_store(t, t % 2).wait()
-
-    def query_loads(t, par):
-        return [n_load(t, par), dy_load(t, par)]
-
-    for copy in query_loads(0, 0):
-        copy.start()
-
-    def query_row(i):
+                kv_to_chip(u).start()
+
+            @pl.when(first_core)
+            def _(u=u):
+                kv_to_partner(u).start()
+
+        @pl.when(b == 0)
+        def _():
+            for copy in weight_loads[2:]:
+                copy.wait()
+            w_local.start()
+
         for k in range(per_row):
-            t = i * per_row + k
-            par = lax.rem(t, 2)
-            for copy in query_loads(t, par):
-                copy.wait()
-
-            @pl.when(t + 1 < tiles)
-            def _(t=t, par=par):
-                for copy in query_loads(t + 1, 1 - par):
-                    copy.start()
-
-            rows = tile_rows(t)
+            rows = tile_rows(b, k)
             inside = slice(k * tile, (k + 1) * tile)
-            put_rope(q_row.at[inside, :], dot_nn(a_in[par], big[2]), cos_ref[rows, :], sin_ref[rows, :])
-            do_row[inside, :] = dot_nt(b_in[par], wo_ref[...]).astype(BF16)
-
-    fit = d_model // seq
-
-    def g_own(b, which, cols):
-        k = 2 * b + which
-        return big.at[lax.div(k, fit), pl.ds(pl.multiple_of(lax.rem(k, fit) * seq, seq), seq), cols]
+            dy_load(b, k).wait()
+            put_rope(q_ring.at[ring, inside, :], dot_nn(n_buf[k], big[2]), cos_ref[rows, :], sin_ref[rows, :])
+            do_ring[ring, inside, :] = dot_nt(dy_in[k], wo_ref[...]).astype(BF16)
+
+            @pl.when(b + 1 < batch)
+            def _(k=k):
+                dy_load(b + 1, k).start()
 
     def o_place(src, u):
         b, g = where(u)
@@ -295,13 +315,9 @@
             g_chip[par] = (g_chip[par].astype(F32) + xin[b].astype(F32)).astype(BF16)
             chip_copy(b).start()
 
-    def own_half(u, which):
-        b, g = where(u)
-        return g_own(b, which, half_cols(g))
-
     def dkv_store(u, which):
         b, g = where(u)
-        return pltpu.make_async_copy(own_half(u, which), dkv_hbm.at[which, row(b), half_cols(g)], dkv_sem.at[u, which])
+        return pltpu.make_async_copy(g_own.at[lax.rem(u, OWN_RING), which], dkv_hbm.at[which, row(b), half_cols(g)], dkv_sem.at[u, which])
 
     def key_grads(u):
         @pl.when(first_core)
@@ -317,7 +333,7 @@
         for which in range(2):
             for h in range(half // HEAD_DIM):
                 cols = slice(h * HEAD_DIM, (h + 1) * HEAD_DIM)
-                own = g_own(b, which, pl.ds(pl.multiple_of(g * half + h * HEAD_DIM, HEAD_DIM), HEAD_DIM))
+                own = g_own.at[lax.rem(u, OWN_RING), which, :, cols]
                 acc = own[...].astype(F32)
                 acc = acc + jnp.where(first_core, part_in[u, which, :, cols].astype(F32), 0.0)
                 acc = (acc + jnp.where(first_chip, xin[u, which, :, cols].astype(F32), 0.0)).astype(BF16)
@@ -334,13 +350,14 @@
     def attend_unit(i, par):
         b, g = where(i)
         rows = row(b)
-        start = start_ref[b]
+        ring = lax.rem(b, Q_RING)
+        start = r * seq + lax.broadcasted_iota(jnp.int32, (1, seq), 1) - pos_ref[b]
         chip_par = lax.rem(i, CHIP_BUFS)
         keys_of = [kv_own.at[i]] + [kvr.at[s, i] for s in range(3)]
         places = [g_part.at[par], g_chip.at[chip_par], g_far.at[par]]
 
-        def grad(slot, which, cols, full):
-            return places[slot - 1].at[which, :, cols] if slot else g_own(b, which, full)
+        def grad(slot, which, cols):
+            return places[slot - 1].at[which, :, cols] if slot else g_own.at[lax.rem(i, OWN_RING), which, :, cols]
 
         live = [None, second_core, second_chip, second_chip]
         piece = [r, r + 1 - 2 * core, r + 2 - 4 * chip, r + 3 - 2 * core - 4 * chip]
@@ -353,8 +370,8 @@
         def one_head(h, carry):
             cols = pl.ds(pl.multiple_of(h * HEAD_DIM, HEAD_DIM), HEAD_DIM)
             full = pl.ds(pl.multiple_of(g * half + h * HEAD_DIM, HEAD_DIM), HEAD_DIM)
-            q = q_row[:, full]
-            do = do_row[:, full]
+            q = q_ring[ring, :, full]
+            do = do_ring[ring, :, full]
             m_scr[...] = jnp.full(m_scr.shape, NEG_BIG, F32)
             l_scr[...] = jnp.zeros_like(l_scr)
             d_scr[...] = jnp.zeros_like(d_scr)
@@ -388,14 +405,14 @@
                     s_scr[slot, s:s + SUB, :] = prob
                     dp_scr[slot, s:s + SUB, :] = dp
                     d_scr[...] += jnp.sum(prob * dp, axis=0, keepdims=True)
-                    grad(slot, 1, cols, full)[s:s + SUB, :] = dot_nn(low, do).astype(BF16)
+                    grad(slot, 1, cols)[s:s + SUB, :] = dot_nn(low, do).astype(BF16)
                     ot_scr[...] += dot_nn(v.T, low)
 
             def keys(slot):
                 for s in subs:
                     k = keys_of[slot][0, s:s + SUB, cols]
                     ds = (s_scr[slot, s:s + SUB, :] * (dp_scr[slot, s:s + SUB, :] - d_scr[...])).astype(BF16)
-                    grad(slot, 0, cols, full)[s:s + SUB, :] = (dot_nn(ds, q) * SCALE).astype(BF16)
+                    grad(slot, 0, cols)[s:s + SUB, :] = (dot_nn(ds, q) * SCALE).astype(BF16)
                     dqt_scr[...] += dot_nn(k.T, ds)
 
             each(scores)
@@ -411,9 +428,14 @@
 
     def step(i, carry):
         par = lax.rem(i, 2)
-        @pl.when(lax.rem(i, HALVES) == 0)
-        def _():
-            query_row(lax.div(i, HALVES))
+        @pl.when(jnp.logical_and(lax.rem(i, HALVES) == 0, lax.div(i, HALVES) + AHEAD < batch))
+        def _():
+            project_row(lax.div(i, HALVES) + AHEAD)
+
+        @pl.when(i >= OWN_RING)
+        def _():
+            for which in range(2):
+                dkv_store(i - OWN_RING, which).wait()
 
         @pl.when(second_chip)
         def _():
@@ -462,6 +484,7 @@
 
         @pl.when(i >= RELAY_LAG)
         def _():
+            key_grads(i - RELAY_LAG)
             relay(i - RELAY_LAG)
 
         @pl.when(i == min(W_TWIN, units - 1))
@@ -487,6 +510,8 @@
 
         return carry
 
+    for b in range(min(AHEAD, batch)):
+        project_row(b)
     lax.fori_loop(0, units, step, 0)
     chip_sum(units - 1)
 
@@ -499,20 +524,14 @@
                 w_move(k, d).start()
 
     lag = min(RELAY_LAG, units)
-
-    def finish(u, carry):
-        @pl.when(u < lag)
-        def _():
-            relay(units - lag + u)
-
-        key_grads(u)
-        return carry
-
-    lax.fori_loop(0, units, finish, 0)
-    for k in (3, 4):
-        for d in w_steps:
-            w_move(k, d).wait_recv()
-            w_move(k + 2, d).start()
+    for u in range(lag):
+        key_grads(units - lag + u)
+        relay(units - lag + u)
+        if u == min(1, lag - 1):
+            for k in (3, 4):
+                for d in w_steps:
+                    w_move(k, d).wait_recv()
+                    w_move(k + 2, d).start()
 
     w_local.wait()
     for d in w_steps:
@@ -522,10 +541,13 @@
             if k in (1, 2, 5, 6):
                 w_move(k, d).wait_recv()
 
+    for k in range(per_row):
+        n_store(batch - 1, k).wait()
+    for u in range(max(0, units - OWN_RING), units):
+        for which in range(2):
+            dkv_store(u, which).wait()
+
     def drain(b, carry):
-        for which in range(2):
-            dkv_store(b, which).wait()
-
         @pl.when(first_core)
         def _():
             kv_to_partner(b).wait_send()
@@ -572,7 +594,7 @@
             chip_copy(b).wait_send()
 
 
-def front(x, dy, wq, wk, wv, wo, cos_t, sin_t, start, gain, seq, tp, cp):
+def front(x, dy, wq, wk, wv, wo, pos, table, gain, seq, tp, cp):
     tokens, d_model = x.shape
     hidden = wq.shape[1]
     batch = tokens // seq
@@ -586,7 +608,7 @@
     f32 = lambda *shape: pltpu.VMEM(shape, F32)
     return pl.pallas_call(
         functools.partial(front_kernel, batch, seq, tp, cp),
-        in_specs=[hbm] * 6 + [vmem] * 4,
+        in_specs=[hbm] * 6 + [vmem] * 3,
         out_specs=[hbm] * 5,
         out_shape=[
             jax.ShapeDtypeStruct((tokens, d_model), BF16),
@@ -596,21 +618,22 @@
             jax.ShapeDtypeStruct((tp, hidden, d_model), BF16),
         ],
         scratch_shapes=[
-            bf(3, d_model, hidden), bf(hidden, d_model), bf(seq, hidden), bf(seq, hidden), bf(2, tile, d_model), bf(2, tile, d_model),
+            bf(3, d_model, hidden), bf(hidden, d_model), f32(tokens, HEAD_DIM), f32(tokens, HEAD_DIM),
+            bf(Q_RING, seq, hidden), bf(Q_RING, seq, hidden), bf(2, tile, d_model), bf(2, tile, d_model), bf(2, tile, d_model),
             bf(units, 2, seq, half), bf(3, units, 2, seq, half),
             f32(4, seq, seq), f32(4, seq, seq), f32(1, seq), f32(1, seq), f32(1, seq), f32(HEAD_DIM, seq), f32(HEAD_DIM, seq),
             bf(units, seq, half), bf(2, seq, half),
-            bf(2, 2, seq, half), bf(CHIP_BUFS, 2, seq, half), bf(2, 2, seq, half),
+            bf(OWN_RING, 2, seq, half), bf(2, 2, seq, half), bf(CHIP_BUFS, 2, seq, half), bf(2, 2, seq, half),
             bf(units, 2, seq, half), bf(units, 2, seq, half),
             dma((4,)), dma((1,)), dma((tp,)), dma((tp,)), dma((7, tp)), dma((7, tp)),
-            dma((2, 2)), dma((2,)), dma((units,)), dma((units,)), dma((units,)), dma((3, units)),
+            dma((2,)), dma((2,)), dma((2,)), dma((units,)), dma((units,)), dma((units,)), dma((3, units)),
             dma((units,)), dma((4, units)), dma((tp, units)), dma((units,)), dma((2,)),
             dma((2,)), dma((2,)), dma((CHIP_BUFS,)), dma((units,)), dma((units,)), dma((units, 2)),
         ],
         compiler_params=pltpu.CompilerParams(collective_id=1, has_side_effects=True, vmem_limit_bytes=63 << 20),
         cost_estimate=pl.CostEstimate(flops=60 * tokens * seq * hidden, bytes_accessed=16 * tokens * d_model, transcendentals=4 * tokens * seq * (hidden // HEAD_DIM)),
         name="front",
-    )(x, dy, wq, wk, wv, wo, cos_t, sin_t, start, gain)
+    )(x, dy, wq, wk, wv, wo, pos, table, gain)
 
 
 PART_RING = 4
@@ -1122,17 +1145,11 @@
     def device_step(x_in, segment_ids, positions, w_query, w_key, w_value, w_out, norm_gain, grad_out):
         batch, seq, d_model = x_in.shape
         tokens = batch * seq
-        rank = lax.axis_index("cp")
         x = x_in.reshape(tokens, d_model)
         dy = grad_out.reshape(tokens, d_model)
 
-        inv_freq = ROPE_THETA ** (-jnp.arange(0, HEAD_DIM, 2).astype(F32) / HEAD_DIM)
-        angles = positions.reshape(tokens, 1).astype(F32) * jnp.repeat(inv_freq, 2)[None, :]
-        cos_t, sin_t = jnp.cos(angles), jnp.sin(angles)
-        start = (rank * seq + jnp.arange(seq, dtype=jnp.int32))[None, :] - positions
-
         gain = norm_gain.reshape(1, d_model)
-        normed, o_all, dq, dkv, w_all = front(x, dy, w_query, w_key, w_value, w_out, cos_t, sin_t, start.reshape(batch, 1, seq), gain, seq, tp_size, cp_size)
+        normed, o_all, dq, dkv, w_all = front(x, dy, w_query, w_key, w_value, w_out, positions.reshape(batch, 1, seq), jnp.asarray(angle_table(), BF16), gain, seq, tp_size, cp_size)
         grad_x, y_out, sum_a, sum_b, grad_gain = backward_norm(dq, dkv, x, dy, o_all, normed, w_query, w_key, w_value, w_all, gain, ROWS, tp_size, cp_size)
         grad_gain = grad_gain.reshape(d_model)
         y_out, grad_x, grad_wq, grad_wk, grad_wv, grad_wo = finish(y_out, grad_x, sum_a, sum_b)

time: 481 us -> 495 us (1.029)
  Pallas kernels: 471 us -> 493 us
  other arithmetic: 7.02 us -> 0 us
    pallas_call x1, Pallas kernels: 248 us -> 272 us  [backward_norm(): pl.pallas_call(functools.partial(back_kernel, groups, rows, tp, cp), in_s...]
    sin x1 -> x0, other arithmetic: 6.22 us -> none  [device_step(): cos_t, sin_t = (jnp.cos(angles), jnp.sin(angles))]
where the time goes in v9:
time: 495 us
  Pallas kernels  493 us (100%)
    pallas_call x1, Pallas kernels, backward_norm(): pl.pallas_call(functools.partial(back_kernel, groups, rows, tp, cp), in_s...  272 us
    pallas_call x1, Pallas kernels, front(): pl.pallas_call(functools.partial(front_kernel, batch, seq, tp, cp), in_sp...  197 us
    pallas_call x1, Pallas kernels, finish(): pl.pallas_call(finish_kernel, grid=(blocks,), in_specs=[tile, tile, block...  23.4 us

profile of v9, /device:TPU:0, one launch (start us, length us, event | category | flops | bytes accessed | tf_op | source)
XLA Modules:
  0.0 495.1 jit_solution(16741151262373951607)
XLA Ops:
  0.6 1.3 reshape.37.pos_ref
  1.9 197.3 %front.1 = (bf16[2304,2048]{1,0:T(8,128)(2,1)}, bf16[4,2304,512]{2,1,0:T(8,128)(2,1)}, bf16[2304,512]{1,0:T(8,128)(2,1)}, bf16[2,2304,512]{2,1,0:T(8,128)(2,1)}, bf16[4,512,2048]{2,1,0:T(8,128)(2,1)}) custom-call(bf16[2304,2048]{1,0:T(8,128)(2,1)} %bitcast.7, bf16[2304,2048]{1,0:T(8,128)(2,1)} %bitcast.9, bf16[2048,512]{1,0:T(8,128)(2,1)} %wq_hbm.3, ...), custom_call_target="tpu_custom_call" | custom-call | flops 27179089920 | bytes 75497472 | tf_op jit(solution)/shard_map/front/pallas_call | solution.py:609
  199.3 271.8 %backward_norm.1 = (bf16[2304,2048]{1,0:T(8,128)(2,1)}, bf16[2304,2048]{1,0:T(8,128)(2,1)}, bf16[8,256,2048]{2,1,0:T(8,128)(2,1)}, bf16[8,256,2048]{2,1,0:T(8,128)(2,1)}, f32[1,2048]{1,0:T(1,128)}) custom-call(bf16[2304,512]{1,0:T(8,128)(2,1)} %get-tuple-element.23.dq_hbm, bf16[2,2304,512]{2,1,0:T(8,128)(2,1)} %get-tuple-element.24.dkv_hbm, ...), custom_call_target="tpu_custom_call" | custom-call | flops 53150220288 | bytes 75497472 | tf_op jit(solution)/shard_map/backward_norm/pallas_call | solution.py:1077
  471.1 0.0 copy-start
  471.1 23.4 %finish.1 = (bf16[2304,2048]{1,0:T(8,128)(2,1)}, bf16[2304,2048]{1,0:T(8,128)(2,1)}, f32[2048,512]{1,0:T(8,128)}, f32[2048,512]{1,0:T(8,128)}, f32[2048,512]{1,0:T(8,128)}, /*index=5*/f32[512,2048]{1,0:T(8,128)}) custom-call(bf16[2304,2048]{1,0:T(8,128)(2,1)} %get-tuple-element.28.y_ref, bf16[2304,2048]{1,0:T(8,128)(2,1)} %get-tuple-element.29.gx_ref, ...), custom_call_target="tpu_custom_call" | custom-call | flops 8388608 | bytes 71303168 | tf_op jit(solution)/shard_map/finish/pallas_call | solution.py:1129
  494.5 0.0 copy-done
  494.5 0.6 copy.17
Async XLA Ops:
  471.1 23.5 %copy-start = (f32[1,2048]{1,0:T(1,128)S(1)}, f32[1,2048]{1,0:T(1,128)}, u32[]{:S(2)}) copy-start(f32[1,2048]{1,0:T(1,128)} %get-tuple-element.34) | copy-start | bytes 24580

commit v10 on v9

--- a/solution.py
+++ b/solution.py
@@ -68,10 +68,11 @@
 
 MESH = pl.DeviceIdType.MESH
 SUB = 128
-ROWS = 16
+ROWS = 32
 WIDTH = 256
 HALVES = 2
-RELAY_LAG = 4
+RELAY_LAG = 2
+SUM_LAG = 4
 CHIP_BUFS = 4
 OWN_RING = 6
 Q_RING = 3
@@ -191,7 +192,7 @@
 
     def angles(b, k):
         rows = tile_rows(b, k)
-        pos = jnp.broadcast_to(pos_ref[b, :, k * tile:(k + 1) * tile], (HEAD_DIM, tile)).T
+        pos = jnp.broadcast_to(pos_ref[pl.ds(b, 1), k * tile:(k + 1) * tile], (HEAD_DIM, tile)).T
         lane = lax.broadcasted_iota(jnp.int32, (tile, HEAD_DIM), 1)
         low = lane < POS_LOW
         pick = jnp.where(low, lax.rem(pos, POS_LOW), POS_LOW + lax.div(pos, POS_LOW)) == lane
@@ -271,7 +272,7 @@
     def o_copy(b, k, step):
         return remote(o_buf.at[b], o_place(z, b), o_send.at[k, b], o_recv.at[z, b], {"tp": jnp.clip(z + step, 0, tp - 1)})
 
-    hops = [(k, step, jnp.logical_and(z + step >= 0, z + step < tp)) for k, step in enumerate((1, -1, 2, -2))]
+    hops = [(k, step, jnp.logical_and(z + step >= 0, z + step < tp)) for k, step in enumerate((1, -1))]
 
     def o_start(b):
         o_local_copy(b).start()
@@ -281,21 +282,22 @@
                 o_copy(b, k, step).start()
 
     def o_arrived(src, b):
-        remote(o_place(src, b), o_place(src, b), relay_send.at[b], o_recv.at[src, b], partner).wait_recv()
-
-    def relay_copy(b, src, dst):
-        return remote(o_place(src, b), o_place(src, b), relay_send.at[b], o_recv.at[src, b], {"tp": dst})
-
-    def relay(b):
-        @pl.when(z == tp - 2)
-        def _():
-            o_arrived(0, b)
-            relay_copy(b, 0, tp - 1).start()
-
-        @pl.when(z == 1)
-        def _():
-            o_arrived(tp - 1, b)
-            relay_copy(b, tp - 1, 0).start()
+        remote(o_place(src, b), o_place(src, b), relay_send.at[0, 0, b], o_recv.at[src, b], partner).wait_recv()
+
+    def relay_copy(b, age, step):
+        src = jnp.clip(z - age * step, 0, tp - 1)
+        return remote(o_place(src, b), o_place(src, b), relay_send.at[age - 1, (1 - step) // 2, b], o_recv.at[src, b], {"tp": jnp.clip(z + step, 0, tp - 1)})
+
+    def relays(age, step):
+        far = z if step > 0 else tp - 1 - z
+        return jnp.logical_and(far >= age, far < tp - 1)
+
+    def relay(b, age):
+        for step in (1, -1):
+            @pl.when(relays(age, step))
+            def _(step=step):
+                o_arrived(jnp.clip(z - age * step, 0, tp - 1), b)
+                relay_copy(b, age, step).start()
 
     def far_copy(b, par):
         return remote(g_far.at[par], xin.at[b], far_send.at[par], x_recv.at[b], partner)
@@ -351,7 +353,7 @@
         b, g = where(i)
         rows = row(b)
         ring = lax.rem(b, Q_RING)
-        start = r * seq + lax.broadcasted_iota(jnp.int32, (1, seq), 1) - pos_ref[b]
+        start = r * seq + lax.broadcasted_iota(jnp.int32, (1, seq), 1) - pos_ref[pl.ds(b, 1), :]
         chip_par = lax.rem(i, CHIP_BUFS)
         keys_of = [kv_own.at[i]] + [kvr.at[s, i] for s in range(3)]
         places = [g_part.at[par], g_chip.at[chip_par], g_far.at[par]]
@@ -482,10 +484,14 @@
         def _():
             chip_sum(i - 1)
 
-        @pl.when(i >= RELAY_LAG)
-        def _():
-            key_grads(i - RELAY_LAG)
-            relay(i - RELAY_LAG)
+        for age in range(1, tp - 1):
+            @pl.when(i >= age * RELAY_LAG)
+            def _(age=age):
+                relay(i - age * RELAY_LAG, age)
+
+        @pl.when(i >= SUM_LAG)
+        def _():
+            key_grads(i - SUM_LAG)
 
         @pl.when(i == min(W_TWIN, units - 1))
         def _():
@@ -523,11 +529,13 @@
             for d in w_steps:
                 w_move(k, d).start()
 
-    lag = min(RELAY_LAG, units)
-    for u in range(lag):
-        key_grads(units - lag + u)
-        relay(units - lag + u)
-        if u == min(1, lag - 1):
+    for i in range(units, units + max(SUM_LAG, (tp - 2) * RELAY_LAG)):
+        for age in range(1, tp - 1):
+            if 0 <= i - age * RELAY_LAG < units:
+                relay(i - age * RELAY_LAG, age)
+        if 0 <= i - SUM_LAG < units:
+            key_grads(i - SUM_LAG)
+        if i == units + 1:
             for k in (3, 4):
                 for d in w_steps:
                     w_move(k, d).wait_recv()
@@ -562,12 +570,17 @@
             def _(k=k, step_=step_):
                 o_copy(b, k, step_).wait_send()
 
-        @pl.when(jnp.logical_or(z == 1, z == tp - 2))
-        def _():
-            relay_copy(b, 0, tp - 1).wait_send()
+        for age in range(1, tp - 1):
+            for step_ in (1, -1):
+                @pl.when(relays(age, step_))
+                def _(age=age, step_=step_):
+                    relay_copy(b, age, step_).wait_send()
 
         for src in range(tp):
-            taken = jnp.logical_or(jnp.logical_and(z == tp - 2, src == 0), jnp.logical_and(z == 1, src == tp - 1))
+            way = jnp.where(z > src, 1, -1)
+            gone = jnp.abs(z - src)
+            far = jnp.where(way > 0, z, tp - 1 - z)
+            taken = jnp.logical_and(gone <= tp - 2, far < tp - 1)
 
             @pl.when(jnp.logical_and(z != src, jnp.logical_not(taken)))
             def _(src=src):
@@ -627,7 +640,7 @@
             bf(units, 2, seq, half), bf(units, 2, seq, half),
             dma((4,)), dma((1,)), dma((tp,)), dma((tp,)), dma((7, tp)), dma((7, tp)),
             dma((2,)), dma((2,)), dma((2,)), dma((units,)), dma((units,)), dma((units,)), dma((3, units)),
-            dma((units,)), dma((4, units)), dma((tp, units)), dma((units,)), dma((2,)),
+            dma((units,)), dma((2, units)), dma((tp, units)), dma((2, 2, units)), dma((2,)),
             dma((2,)), dma((2,)), dma((CHIP_BUFS,)), dma((units,)), dma((units,)), dma((units, 2)),
         ],
         compiler_params=pltpu.CompilerParams(collective_id=1, has_side_effects=True, vmem_limit_bytes=63 << 20),
@@ -1149,7 +1162,7 @@
         dy = grad_out.reshape(tokens, d_model)
 
         gain = norm_gain.reshape(1, d_model)
-        normed, o_all, dq, dkv, w_all = front(x, dy, w_query, w_key, w_value, w_out, positions.reshape(batch, 1, seq), jnp.asarray(angle_table(), BF16), gain, seq, tp_size, cp_size)
+        normed, o_all, dq, dkv, w_all = front(x, dy, w_query, w_key, w_value, w_out, positions, jnp.asarray(angle_table(), BF16), gain, seq, tp_size, cp_size)
         grad_x, y_out, sum_a, sum_b, grad_gain = backward_norm(dq, dkv, x, dy, o_all, normed, w_query, w_key, w_value, w_all, gain, ROWS, tp_size, cp_size)
         grad_gain = grad_gain.reshape(d_model)
         y_out, grad_x, grad_wq, grad_wk, grad_wv, grad_wo = finish(y_out, grad_x, sum_a, sum_b)

time: 495 us -> 475 us (0.960)
  Pallas kernels: 493 us -> 474 us
    pallas_call x1, Pallas kernels: 272 us -> 257 us  [backward_norm(): pl.pallas_call(functools.partial(back_kernel, groups, rows, tp, cp), in_s...]
where the time goes in v10:
time: 475 us
  Pallas kernels  474 us (100%)
    pallas_call x1, Pallas kernels, backward_norm(): pl.pallas_call(functools.partial(back_kernel, groups, rows, tp, cp), in_s...  257 us
    pallas_call x1, Pallas kernels, front(): pl.pallas_call(functools.partial(front_kernel, batch, seq, tp, cp), in_sp...  193 us
    pallas_call x1, Pallas kernels, finish(): pl.pallas_call(finish_kernel, grid=(blocks,), in_specs=[tile, tile, block...  23.4 us

profile of v10, /device:TPU:0, one launch (start us, length us, event | category | flops | bytes accessed | tf_op | source)
XLA Modules:
  0.0 474.9 jit_solution(2364686930579562710)
XLA Ops:
  0.6 192.9 %front.1 = (bf16[2304,2048]{1,0:T(8,128)(2,1)}, bf16[4,2304,512]{2,1,0:T(8,128)(2,1)}, bf16[2304,512]{1,0:T(8,128)(2,1)}, bf16[2,2304,512]{2,1,0:T(8,128)(2,1)}, bf16[4,512,2048]{2,1,0:T(8,128)(2,1)}) custom-call(bf16[2304,2048]{1,0:T(8,128)(2,1)} %bitcast.7, bf16[2304,2048]{1,0:T(8,128)(2,1)} %bitcast.9, bf16[2048,512]{1,0:T(8,128)(2,1)} %wq_hbm.3, ...), custom_call_target="tpu_custom_call" | custom-call | flops 27179089920 | bytes 75497472 | tf_op jit(solution)/shard_map/front/pallas_call | solution.py:622
  193.6 257.3 %backward_norm.1 = (bf16[2304,2048]{1,0:T(8,128)(2,1)}, bf16[2304,2048]{1,0:T(8,128)(2,1)}, bf16[8,256,2048]{2,1,0:T(8,128)(2,1)}, bf16[8,256,2048]{2,1,0:T(8,128)(2,1)}, f32[1,2048]{1,0:T(1,128)}) custom-call(bf16[2304,512]{1,0:T(8,128)(2,1)} %get-tuple-element.23.dq_hbm, bf16[2,2304,512]{2,1,0:T(8,128)(2,1)} %get-tuple-element.24.dkv_hbm, ...), custom_call_target="tpu_custom_call" | custom-call | flops 53150220288 | bytes 75497472 | tf_op jit(solution)/shard_map/backward_norm/pallas_call | solution.py:1090
  450.9 0.0 copy-start
  450.9 23.4 %finish.1 = (bf16[2304,2048]{1,0:T(8,128)(2,1)}, bf16[2304,2048]{1,0:T(8,128)(2,1)}, f32[2048,512]{1,0:T(8,128)}, f32[2048,512]{1,0:T(8,128)}, f32[2048,512]{1,0:T(8,128)}, /*index=5*/f32[512,2048]{1,0:T(8,128)}) custom-call(bf16[2304,2048]{1,0:T(8,128)(2,1)} %get-tuple-element.28.y_ref, bf16[2304,2048]{1,0:T(8,128)(2,1)} %get-tuple-element.29.gx_ref, ...), custom_call_target="tpu_custom_call" | custom-call | flops 8388608 | bytes 71303168 | tf_op jit(solution)/shard_map/finish/pallas_call | solution.py:1142
  474.3 0.0 copy-done
  474.3 0.6 copy.17
Async XLA Ops:
  450.9 23.5 %copy-start = (f32[1,2048]{1,0:T(1,128)S(1)}, f32[1,2048]{1,0:T(1,128)}, u32[]{:S(2)}) copy-start(f32[1,2048]{1,0:T(1,128)} %get-tuple-element.34) | copy-start | bytes 24580

commit v11 on v10

--- a/solution.py
+++ b/solution.py
@@ -78,8 +78,9 @@
 Q_RING = 3
 AHEAD = 2
 POS_LOW = 64
-W_TWIN = 3
-W_PARTNER = 6
+W_TWIN = 0
+W_PARTNER = 4
+W_CHIP = 7
 
 
 def front_kernel(batch, seq, tp, cp, x_hbm, dy_hbm, wq_hbm, wk_hbm, wv_hbm, wo_hbm, pos_ref, table_ref, gain_ref,
@@ -510,9 +511,11 @@
                 w_move(0, d).wait_recv()
                 w_move(2, d).start()
 
-                @pl.when(second_chip)
-                def _(d=d):
-                    w_move(4, d).start()
+        @pl.when(jnp.logical_and(first_chip, i == min(W_CHIP, units - 1)))
+        def _():
+            for k in (3, 4):
+                for d in w_steps:
+                    w_move(k, d).start()
 
         return carry
 
@@ -521,21 +524,19 @@
     lax.fori_loop(0, units, step, 0)
     chip_sum(units - 1)
 
-    @pl.when(first_chip)
+    @pl.when(second_chip)
     def _():
-        for u in range(units):
-            kv_to_chip(u).wait_send()
-        for k in (3, 4):
-            for d in w_steps:
-                w_move(k, d).start()
-
-    for i in range(units, units + max(SUM_LAG, (tp - 2) * RELAY_LAG)):
+        for d in w_steps:
+            w_move(4, d).start()
+
+    end = units + max(SUM_LAG, (tp - 2) * RELAY_LAG)
+    for i in range(units, end):
         for age in range(1, tp - 1):
             if 0 <= i - age * RELAY_LAG < units:
                 relay(i - age * RELAY_LAG, age)
         if 0 <= i - SUM_LAG < units:
             key_grads(i - SUM_LAG)
-        if i == units + 1:
+        if i == end - 1:
             for k in (3, 4):
                 for d in w_steps:
                     w_move(k, d).wait_recv()
@@ -556,6 +557,10 @@
             dkv_store(u, which).wait()
 
     def drain(b, carry):
+        @pl.when(first_chip)
+        def _():
+            kv_to_chip(b).wait_send()
+
         @pl.when(first_core)
         def _():
             kv_to_partner(b).wait_send()

time: 475 us -> 476 us (level)
    pallas_call x1, Pallas kernels: 193 us -> 202 us  [front(): pl.pallas_call(functools.partial(front_kernel, batch, seq, tp, cp), in_sp...]
    pallas_call x1, Pallas kernels: 257 us -> 249 us  [backward_norm(): pl.pallas_call(functools.partial(back_kernel, groups, rows, tp, cp), in_s...]
where the time goes in v11:
time: 476 us
  Pallas kernels  475 us (100%)
    pallas_call x1, Pallas kernels, backward_norm(): pl.pallas_call(functools.partial(back_kernel, groups, rows, tp, cp), in_s...  249 us
    pallas_call x1, Pallas kernels, front(): pl.pallas_call(functools.partial(front_kernel, batch, seq, tp, cp), in_sp...  202 us
    pallas_call x1, Pallas kernels, finish(): pl.pallas_call(finish_kernel, grid=(blocks,), in_specs=[tile, tile, block...  23.4 us

profile of v11, /device:TPU:0, one launch (start us, length us, event | category | flops | bytes accessed | tf_op | source)
XLA Modules:
  0.0 476.3 jit_solution(10603152636106441413)
XLA Ops:
  0.6 202.1 %front.1 = (bf16[2304,2048]{1,0:T(8,128)(2,1)}, bf16[4,2304,512]{2,1,0:T(8,128)(2,1)}, bf16[2304,512]{1,0:T(8,128)(2,1)}, bf16[2,2304,512]{2,1,0:T(8,128)(2,1)}, bf16[4,512,2048]{2,1,0:T(8,128)(2,1)}) custom-call(bf16[2304,2048]{1,0:T(8,128)(2,1)} %bitcast.7, bf16[2304,2048]{1,0:T(8,128)(2,1)} %bitcast.9, bf16[2048,512]{1,0:T(8,128)(2,1)} %wq_hbm.3, ...), custom_call_target="tpu_custom_call" | custom-call | flops 27179089920 | bytes 75497472 | tf_op jit(solution)/shard_map/front/pallas_call | solution.py:627
  202.8 249.4 %backward_norm.1 = (bf16[2304,2048]{1,0:T(8,128)(2,1)}, bf16[2304,2048]{1,0:T(8,128)(2,1)}, bf16[8,256,2048]{2,1,0:T(8,128)(2,1)}, bf16[8,256,2048]{2,1,0:T(8,128)(2,1)}, f32[1,2048]{1,0:T(1,128)}) custom-call(bf16[2304,512]{1,0:T(8,128)(2,1)} %get-tuple-element.23.dq_hbm, bf16[2,2304,512]{2,1,0:T(8,128)(2,1)} %get-tuple-element.24.dkv_hbm, ...), custom_call_target="tpu_custom_call" | custom-call | flops 53150220288 | bytes 75497472 | tf_op jit(solution)/shard_map/backward_norm/pallas_call | solution.py:1095
  452.2 0.0 copy-start
  452.2 23.4 %finish.1 = (bf16[2304,2048]{1,0:T(8,128)(2,1)}, bf16[2304,2048]{1,0:T(8,128)(2,1)}, f32[2048,512]{1,0:T(8,128)}, f32[2048,512]{1,0:T(8,128)}, f32[2048,512]{1,0:T(8,128)}, /*index=5*/f32[512,2048]{1,0:T(8,128)}) custom-call(bf16[2304,2048]{1,0:T(8,128)(2,1)} %get-tuple-element.28.y_ref, bf16[2304,2048]{1,0:T(8,128)(2,1)} %get-tuple-element.29.gx_ref, ...), custom_call_target="tpu_custom_call" | custom-call | flops 8388608 | bytes 71303168 | tf_op jit(solution)/shard_map/finish/pallas_call | solution.py:1147
  475.6 0.0 copy-done
  475.7 0.6 copy.17
Async XLA Ops:
  452.2 23.5 %copy-start = (f32[1,2048]{1,0:T(1,128)S(1)}, f32[1,2048]{1,0:T(1,128)}, u32[]{:S(2)}) copy-start(f32[1,2048]{1,0:T(1,128)} %get-tuple-element.34) | copy-start | bytes 24580

commit v12 on v11

--- a/solution.py
+++ b/solution.py
@@ -71,15 +71,16 @@
 ROWS = 32
 WIDTH = 256
 HALVES = 2
-RELAY_LAG = 2
+RELAY_LAG = 1
+LATE = 3
 SUM_LAG = 4
 CHIP_BUFS = 4
 OWN_RING = 6
 Q_RING = 3
 AHEAD = 2
 POS_LOW = 64
-W_TWIN = 0
-W_PARTNER = 4
+W_TWIN = 1
+W_PARTNER = 3
 W_CHIP = 7
 
 
@@ -275,10 +276,13 @@
 
     hops = [(k, step, jnp.logical_and(z + step >= 0, z + step < tp)) for k, step in enumerate((1, -1))]
 
+    def far_from_end(step):
+        return jnp.logical_and(z + step != 0, z + step != tp - 1)
+
     def o_start(b):
         o_local_copy(b).start()
         for k, step, ok in hops:
-            @pl.when(ok)
+            @pl.when(jnp.logical_and(ok, jnp.logical_or(b < units - LATE, far_from_end(step))))
             def _(k=k, step=step):
                 o_copy(b, k, step).start()
 
@@ -511,6 +515,10 @@
                 w_move(0, d).wait_recv()
                 w_move(2, d).start()
 
+                @pl.when(second_chip)
+                def _(d=d):
+                    w_move(4, d).start()
+
         @pl.when(jnp.logical_and(first_chip, i == min(W_CHIP, units - 1)))
         def _():
             for k in (3, 4):
@@ -523,11 +531,6 @@
         project_row(b)
     lax.fori_loop(0, units, step, 0)
     chip_sum(units - 1)
-
-    @pl.when(second_chip)
-    def _():
-        for d in w_steps:
-            w_move(4, d).start()
 
     end = units + max(SUM_LAG, (tp - 2) * RELAY_LAG)
     for i in range(units, end):
@@ -571,7 +574,7 @@
 
         o_local_copy(b).wait()
         for k, step_, ok in hops:
-            @pl.when(ok)
+            @pl.when(jnp.logical_and(ok, jnp.logical_or(b < units - LATE, far_from_end(step_))))
             def _(k=k, step_=step_):
                 o_copy(b, k, step_).wait_send()
 
@@ -586,8 +589,9 @@
             gone = jnp.abs(z - src)
             far = jnp.where(way > 0, z, tp - 1 - z)
             taken = jnp.logical_and(gone <= tp - 2, far < tp - 1)
-
-            @pl.when(jnp.logical_and(z != src, jnp.logical_not(taken)))
+            late = jnp.logical_and(b >= units - LATE, jnp.logical_and(gone == 1, far == tp - 1))
+
+            @pl.when(jnp.logical_and(z != src, jnp.logical_not(jnp.logical_or(taken, late))))
             def _(src=src):
                 o_arrived(src, b)
 
@@ -662,12 +666,13 @@
 EARLY = 4
 
 
-def back_kernel(groups, rows, tp, cp, dq_hbm, dkv_hbm, x_hbm, dy_hbm, o_hbm, n_hbm, wq_hbm, wk_hbm, wv_hbm, wo_hbm, gain_ref,
-                gx_hbm, y_hbm, ga_hbm, gb_hbm, gg_ref,
+def back_kernel(groups, rows, tp, cp, seq, dq_hbm, dkv_hbm, x_hbm, dy_hbm, o_old, n_hbm, wq_hbm, wk_hbm, wv_hbm, wo_hbm, gain_ref,
+                gx_hbm, y_hbm, ga_hbm, gb_hbm, gg_ref, o_out,
                 wq_ref, wk_ref, wv_ref, wo_ref, dq_all, dkv_all, o_t, part, rs_r, rs_l, send_r, send_l, tot, gx_buf,
                 o_in, x_in, xo_in, dyo_in, y_buf, n_in, dy_in, away, part_in, mine, gain_all,
                 w_sem, in_sem, fin_sem, job_sem, y_sem, own_sem, rss_r, rss_l, rsr_r, rsr_l, ag0_r, ag0_l, agf_r, agf_l, agr_r, agr_l,
-                away_send, away_recv, mine_own, mine_part, mine_chip, ga_recv, chip_recv, gb_send, gb_recv, gs_sem, gr_sem):
+                away_send, away_recv, mine_own, mine_part, mine_chip, ga_recv, chip_recv, gb_send, gb_recv, gs_sem, gr_sem, late_send, late_recv):
+    o_hbm = o_out
     z = lax.axis_index("tp")
     r = lax.axis_index("cp")
     core = lax.rem(r, 2)
@@ -967,30 +972,65 @@
         sender = lax.rem(z + dt, tp) * cp + lax.rem(r + dc, cp)
         remote(gain_all.at[sender], gain_all.at[sender], gs_sem.at[0], gr_sem.at[sender], right).wait_recv()
 
+    units = tokens // seq * HALVES
+    half = hidden // HALVES
+    late_units = range(max(0, units - LATE), units)
+    late_wait = max(0, late_units[0] // HALVES * seq // span + OUT_LAG - 2)
+    sends_late = jnp.logical_or(z == 1, z == last - 1)
+    gets_late = jnp.logical_or(z == 0, z == last)
+
+    def late_copy(n, src, dst):
+        u = late_units[n]
+        place = o_out.at[src, u // HALVES * seq:(u // HALVES + 1) * seq, u % HALVES * half:(u % HALVES + 1) * half]
+        return remote(place, place, late_send.at[n], late_recv.at[n], {"tp": dst})
+
+    def late_move(n):
+        return late_copy(n, z, jnp.where(z == 1, 0, last))
+
+    for n in range(len(late_units)):
+        @pl.when(sends_late)
+        def _(n=n):
+            late_move(n).start()
+
     for copy in weight_loads:
         copy.wait()
 
     def step(i, carry):
-        for k in reversed(range(1, slots)):
-            rs_send(i - k, k)
-
-        @pl.when(i == EARLY)
-        def _():
-            for copy in rest_loads:
+        @pl.when(jnp.logical_and(gets_late, i == late_wait))
+        def _():
+            for n in range(len(late_units)):
+                late_copy(n, jnp.where(z == 0, 1, last - 1), z).wait_recv()
+
+        for a in reversed(range(1, slots + 1)):
+            ag_step(i - slots - a, a)
+
+        @pl.when(i == OUT_LAG)
+        def _():
+            for copy in out_loads:
                 copy.wait()
 
-        @pl.when(i < groups)
-        def _():
-            partial_norm(i)
-
-        rs_send(i, 0)
+        @pl.when(jnp.logical_and(i >= OUT_LAG, i < groups + OUT_LAG))
+        def _():
+            j = i - OUT_LAG
+            at = lax.rem(j, 2)
+            for copy in inputs(j, at):
+                copy.wait()
+
+            @pl.when(j + 1 < groups)
+            def _():
+                for copy in inputs(j + 1, 1 - at):
+                    copy.start()
+
+            @pl.when(j >= 2)
+            def _():
+                y_copy(j - 2, at).wait()
+
+            project_out(at)
+            y_copy(j, at).start()
 
         @pl.when(jnp.logical_and(i >= slots, i < groups + slots))
         def _():
             finalize(i - slots)
-
-        for a in range(1, slots + 1):
-            ag_step(i - slots - a, a)
 
         @pl.when(i == groups + slots - 1)
         def _():
@@ -1002,6 +1042,15 @@
         def _():
             for copy in final_inputs(i - slots + 1, lax.rem(i - slots + 1, 2)):
                 copy.start()
+
+        @pl.when(i == EARLY)
+        def _():
+            for copy in rest_loads:
+                copy.wait()
+
+        @pl.when(i < groups)
+        def _():
+            partial_norm(i)
 
         @pl.when(i == JOB_LAG - 1)
         def _():
@@ -1011,33 +1060,12 @@
             for copy in job_loads(0, 0):
                 copy.start()
 
-        @pl.when(i == OUT_LAG)
-        def _():
-            for copy in out_loads:
-                copy.wait()
-
-        @pl.when(jnp.logical_and(i >= OUT_LAG, i < groups + OUT_LAG))
-        def _():
-            j = i - OUT_LAG
-            at = lax.rem(j, 2)
-            for copy in inputs(j, at):
-                copy.wait()
-
-            @pl.when(j + 1 < groups)
-            def _():
-                for copy in inputs(j + 1, 1 - at):
-                    copy.start()
-
-            @pl.when(j >= 2)
-            def _():
-                y_copy(j - 2, at).wait()
-
-            project_out(at)
-            y_copy(j, at).start()
-
         @pl.when(jnp.logical_and(i >= JOB_LAG, i < JOB_LAG + blocks))
         def _():
             job(i - JOB_LAG)
+
+        for k in reversed(range(slots)):
+            rs_send(i - k, k)
 
         @pl.when(jnp.logical_and(lax.rem(i, 2) == 1, jnp.logical_and(i >= FORWARD_LAG, i < FORWARD_LAG + 2 * pairs)))
         def _():
@@ -1062,6 +1090,11 @@
             @pl.when(jnp.logical_and(far >= a, far < last))
             def _(a=a, to_right=to_right):
                 ag_forward(groups - 1, a, to_right).wait_send()
+    for n in range(len(late_units)):
+        @pl.when(sends_late)
+        def _(n=n):
+            late_move(n).wait_send()
+
     away_copy(pairs - 1).wait_send()
     for p in range(max(0, pairs - 2), pairs):
         mine_done(p, p % 2)
@@ -1078,7 +1111,7 @@
     gg_ref[...] = total
 
 
-def backward_norm(dq, dkv, x, dy, o_all, normed, wq, wk, wv, wo_all, gain, rows, tp, cp):
+def backward_norm(dq, dkv, x, dy, o_all, normed, wq, wk, wv, wo_all, gain, rows, seq, tp, cp):
     tokens, hidden = dq.shape
     d_model = x.shape[1]
     span = tp * rows
@@ -1093,15 +1126,17 @@
     bf = lambda *shape: pltpu.VMEM(shape, BF16)
     f32 = lambda *shape: pltpu.VMEM(shape, F32)
     return pl.pallas_call(
-        functools.partial(back_kernel, groups, rows, tp, cp),
+        functools.partial(back_kernel, groups, rows, tp, cp, seq),
         in_specs=[hbm] * 10 + [vmem],
-        out_specs=[hbm, hbm, hbm, hbm, vmem],
+        out_specs=[hbm, hbm, hbm, hbm, vmem, hbm],
+        input_output_aliases={4: 5},
         out_shape=[
             jax.ShapeDtypeStruct((tokens, d_model), BF16),
             jax.ShapeDtypeStruct((tokens, d_model), BF16),
             jax.ShapeDtypeStruct((blocks, width, 4 * hidden), BF16),
             jax.ShapeDtypeStruct((blocks, width, 4 * hidden), BF16),
             jax.ShapeDtypeStruct((1, d_model), F32),
+            jax.ShapeDtypeStruct(o_all.shape, BF16),
         ],
         scratch_shapes=[
             bf(d_model, hidden), bf(d_model, hidden), bf(d_model, hidden), bf(tp, hidden, d_model),
@@ -1115,7 +1150,7 @@
             dma((slots,)), dma((slots,)), dma((RS_RING, slots)), dma((RS_RING, slots)),
             dma((2,)), dma((2,)), dma((slots,)), dma((slots,)), dma((groups, slots)), dma((groups, slots)),
             dma((1,)), dma((2,)), dma((2,)), dma((2,)), dma((2,)), dma((pairs,)), dma((pairs,)), dma((pairs,)), dma((pairs,)),
-            dma((tp * cp,)), dma((tp * cp,)),
+            dma((tp * cp,)), dma((tp * cp,)), dma((max(LATE, 1),)), dma((max(LATE, 1),)),
         ],
         compiler_params=pltpu.CompilerParams(collective_id=0, has_side_effects=True, vmem_limit_bytes=63 << 20),
         cost_estimate=pl.CostEstimate(flops=22 * tokens * hidden * d_model, bytes_accessed=16 * tokens * d_model, transcendentals=0),
@@ -1168,7 +1203,7 @@
 
         gain = norm_gain.reshape(1, d_model)
         normed, o_all, dq, dkv, w_all = front(x, dy, w_query, w_key, w_value, w_out, positions, jnp.asarray(angle_table(), BF16), gain, seq, tp_size, cp_size)
-        grad_x, y_out, sum_a, sum_b, grad_gain = backward_norm(dq, dkv, x, dy, o_all, normed, w_query, w_key, w_value, w_all, gain, ROWS, tp_size, cp_size)
+        grad_x, y_out, sum_a, sum_b, grad_gain, _ = backward_norm(dq, dkv, x, dy, o_all, normed, w_query, w_key, w_value, w_all, gain, ROWS, seq, tp_size, cp_size)
         grad_gain = grad_gain.reshape(d_model)
         y_out, grad_x, grad_wq, grad_wk, grad_wv, grad_wo = finish(y_out, grad_x, sum_a, sum_b)
         return y_out.reshape(x_in.shape), grad_x.reshape(x_in.shape), grad_gain, grad_wq, grad_wk, grad_wv, grad_wo

time: 476 us -> 444 us (0.933)
  Pallas kernels: 475 us -> 442 us
    pallas_call x1, Pallas kernels: 249 us -> 231 us  [backward_norm(): pl.pallas_call(functools.partial(back_kernel, groups, rows, tp, cp, seq),...]
    pallas_call x1, Pallas kernels: 202 us -> 187 us  [front(): pl.pallas_call(functools.partial(front_kernel, batch, seq, tp, cp), in_sp...]
where the time goes in v12:
time: 444 us
  Pallas kernels  442 us (100%)
    pallas_call x1, Pallas kernels, backward_norm(): pl.pallas_call(functools.partial(back_kernel, groups, rows, tp, cp, seq),...  231 us
    pallas_call x1, Pallas kernels, front(): pl.pallas_call(functools.partial(front_kernel, batch, seq, tp, cp), in_sp...  187 us
    pallas_call x1, Pallas kernels, finish(): pl.pallas_call(finish_kernel, grid=(blocks,), in_specs=[tile, tile, block...  23.4 us

profile of v12, /device:TPU:0, one launch (start us, length us, event | category | flops | bytes accessed | tf_op | source)
XLA Modules:
  0.0 443.6 jit_solution(6924574682718245996)
XLA Ops:
  0.6 187.5 %front.1 = (bf16[2304,2048]{1,0:T(8,128)(2,1)}, bf16[4,2304,512]{2,1,0:T(8,128)(2,1)}, bf16[2304,512]{1,0:T(8,128)(2,1)}, bf16[2,2304,512]{2,1,0:T(8,128)(2,1)}, bf16[4,512,2048]{2,1,0:T(8,128)(2,1)}) custom-call(bf16[2304,2048]{1,0:T(8,128)(2,1)} %bitcast.7, bf16[2304,2048]{1,0:T(8,128)(2,1)} %bitcast.9, bf16[2048,512]{1,0:T(8,128)(2,1)} %wq_hbm.3, ...), custom_call_target="tpu_custom_call" | custom-call | flops 27179089920 | bytes 75497472 | tf_op jit(solution)/shard_map/front/pallas_call | solution.py:631
  188.1 231.4 %backward_norm.1 = (bf16[2304,2048]{1,0:T(8,128)(2,1)}, bf16[2304,2048]{1,0:T(8,128)(2,1)}, bf16[8,256,2048]{2,1,0:T(8,128)(2,1)}, bf16[8,256,2048]{2,1,0:T(8,12...) custom-call(bf16[2304,512]{1,0:T(8,128)(2,1)} %get-tuple-element.23.dq_hbm, ...), custom_call_target="tpu_custom_call", output_to_operand_aliasing={{5}: (4, {})} | custom-call | flops 53150220288 | bytes 75497472 | tf_op jit(solution)/shard_map/backward_norm/pallas_call | solution.py:1128
  419.5 0.0 copy-start
  419.5 23.4 %finish.1 = (bf16[2304,2048]{1,0:T(8,128)(2,1)}, bf16[2304,2048]{1,0:T(8,128)(2,1)}, f32[2048,512]{1,0:T(8,128)}, f32[2048,512]{1,0:T(8,128)}, f32[2048,512]{1,0:T(8,128)}, /*index=5*/f32[512,2048]{1,0:T(8,128)}) custom-call(bf16[2304,2048]{1,0:T(8,128)(2,1)} %get-tuple-element.28.y_ref, bf16[2304,2048]{1,0:T(8,128)(2,1)} %get-tuple-element.29.gx_ref, ...), custom_call_target="tpu_custom_call" | custom-call | flops 8388608 | bytes 71303168 | tf_op jit(solution)/shard_map/finish/pallas_call | solution.py:1182
  442.9 0.0 copy-done
  442.9 0.6 copy.19
Async XLA Ops:
  419.5 23.5 %copy-start = (f32[1,2048]{1,0:T(1,128)S(1)}, f32[1,2048]{1,0:T(1,128)}, u32[]{:S(2)}) copy-start(f32[1,2048]{1,0:T(1,128)} %get-tuple-element.34) | copy-start | bytes 24580

commit v13 on v12

--- a/solution.py
+++ b/solution.py
@@ -67,9 +67,10 @@
 
 
 MESH = pl.DeviceIdType.MESH
-SUB = 128
+SUB = 384
 ROWS = 32
 WIDTH = 256
+PARTS = 2
 HALVES = 2
 RELAY_LAG = 1
 LATE = 3
@@ -387,6 +388,7 @@
 
             def scores(slot):
                 base = piece[slot] * seq
+                top = None
                 for s in subs:
                     raw = dot_nt(keys_of[slot][0, s:s + SUB, cols], q)
                     local = lax.broadcasted_iota(jnp.int32, raw.shape, 0) + s
@@ -395,32 +397,47 @@
                         allowed = jnp.logical_and(allowed, local <= lax.broadcasted_iota(jnp.int32, raw.shape, 1))
                     raw = jnp.where(allowed, raw, NEG_BIG)
                     s_scr[slot, s:s + SUB, :] = raw
-                    m_scr[...] = jnp.maximum(m_scr[...], jnp.max(raw, axis=0, keepdims=True))
+                    high = jnp.max(raw, axis=0, keepdims=True)
+                    top = high if top is None else jnp.maximum(top, high)
+                m_scr[...] = jnp.maximum(m_scr[...], top)
 
             def exps(slot):
+                top = m_scr[...]
+                total = None
                 for s in subs:
-                    e = jnp.exp2((s_scr[slot, s:s + SUB, :] - m_scr[...]) * EXP2_SCALE)
+                    e = jnp.exp2((s_scr[slot, s:s + SUB, :] - top) * EXP2_SCALE)
                     s_scr[slot, s:s + SUB, :] = e
-                    l_scr[...] += jnp.sum(e, axis=0, keepdims=True)
+                    part = jnp.sum(e, axis=0, keepdims=True)
+                    total = part if total is None else total + part
+                l_scr[...] += total
 
             def values(slot):
+                inv = l_scr[...]
+                total, out = None, None
                 for s in subs:
                     v = keys_of[slot][1, s:s + SUB, cols]
-                    prob = s_scr[slot, s:s + SUB, :] * l_scr[...]
+                    prob = s_scr[slot, s:s + SUB, :] * inv
                     low = prob.astype(BF16)
                     dp = dot_nt(v, do)
-                    s_scr[slot, s:s + SUB, :] = prob
                     dp_scr[slot, s:s + SUB, :] = dp
-                    d_scr[...] += jnp.sum(prob * dp, axis=0, keepdims=True)
+                    part = jnp.sum(prob * dp, axis=0, keepdims=True)
+                    total = part if total is None else total + part
                     grad(slot, 1, cols)[s:s + SUB, :] = dot_nn(low, do).astype(BF16)
-                    ot_scr[...] += dot_nn(v.T, low)
+                    piece_out = dot_nn(v.T, low)
+                    out = piece_out if out is None else out + piece_out
+                d_scr[...] += total
+                ot_scr[...] += out
 
             def keys(slot):
+                inv, mean = l_scr[...], d_scr[...]
+                out = None
                 for s in subs:
                     k = keys_of[slot][0, s:s + SUB, cols]
-                    ds = (s_scr[slot, s:s + SUB, :] * (dp_scr[slot, s:s + SUB, :] - d_scr[...])).astype(BF16)
+                    ds = ((s_scr[slot, s:s + SUB, :] * inv) * (dp_scr[slot, s:s + SUB, :] - mean)).astype(BF16)
                     grad(slot, 0, cols)[s:s + SUB, :] = (dot_nn(ds, q) * SCALE).astype(BF16)
-                    dqt_scr[...] += dot_nn(k.T, ds)
+                    piece_out = dot_nn(k.T, ds)
+                    out = piece_out if out is None else out + piece_out
+                dqt_scr[...] += out
 
             each(scores)
             each(exps)
@@ -1161,29 +1178,31 @@
 def finish_kernel(y_ref, gx_ref, ga_ref, gb_ref, yo_ref, gxo_ref, wq_ref, wk_ref, wv_ref, wo_ref):
     yo_ref[...] = y_ref[...]
     gxo_ref[...] = gx_ref[...]
-    width = ga_ref.shape[1]
+    rows = ga_ref.shape[1]
+    width = rows * PARTS
     hidden = wq_ref.shape[1]
     for k, ref in enumerate((wq_ref, wk_ref, wv_ref)):
         cols = slice(k * hidden, (k + 1) * hidden)
         ref[...] = ga_ref[0, :, cols].astype(F32) + gb_ref[0, :, cols].astype(F32)
     for k in range(hidden // width):
         cols = slice(3 * hidden + k * width, 3 * hidden + (k + 1) * width)
-        wo_ref[k * width:(k + 1) * width, :] = ga_ref[0, :, cols].astype(F32) + gb_ref[0, :, cols].astype(F32)
+        at = k * width + lax.rem(pl.program_id(0), PARTS) * rows
+        wo_ref[pl.ds(pl.multiple_of(at, rows), rows), :] = ga_ref[0, :, cols].astype(F32) + gb_ref[0, :, cols].astype(F32)
 
 
 def finish(y, gx, ga, gb):
     tokens, d_model = y.shape
     blocks, width, packed = ga.shape
     hidden = packed // 4
-    rows = tokens // blocks
-    tile = pl.BlockSpec((rows, d_model), lambda j: (j, 0))
-    block = pl.BlockSpec((1, width, packed), lambda j: (j, 0, 0))
-    wide = pl.BlockSpec((width, hidden), lambda j: (j, 0))
+    steps = blocks * PARTS
+    tile = pl.BlockSpec((tokens // steps, d_model), lambda j: (j, 0))
+    block = pl.BlockSpec((1, width // PARTS, packed), lambda j: (j // PARTS, j % PARTS, 0))
+    wide = pl.BlockSpec((width // PARTS, hidden), lambda j: (j, 0))
     return pl.pallas_call(
         finish_kernel,
-        grid=(blocks,),
+        grid=(steps,),
         in_specs=[tile, tile, block, block],
-        out_specs=[tile, tile, wide, wide, wide, pl.BlockSpec((hidden, width), lambda j: (0, j))],
+        out_specs=[tile, tile, wide, wide, wide, pl.BlockSpec((hidden, width), lambda j: (0, j // PARTS))],
         out_shape=[jax.ShapeDtypeStruct((tokens, d_model), BF16)] * 2 + [jax.ShapeDtypeStruct((d_model, hidden), F32)] * 3 + [jax.ShapeDtypeStruct((hidden, d_model), F32)],
         compiler_params=pltpu.CompilerParams(dimension_semantics=("arbitrary",), vmem_limit_bytes=48 << 20),
         cost_estimate=pl.CostEstimate(flops=8 * d_model * hidden, bytes_accessed=8 * tokens * d_model + 32 * d_model * hidden, transcendentals=0),

time: 444 us -> 447 us (level)
  no operation moved by 1% of the time
where the time goes in v13:
time: 447 us
  Pallas kernels  445 us (100%)
    pallas_call x1, Pallas kernels, backward_norm(): pl.pallas_call(functools.partial(back_kernel, groups, rows, tp, cp, seq),...  231 us
    pallas_call x1, Pallas kernels, front(): pl.pallas_call(functools.partial(front_kernel, batch, seq, tp, cp), in_sp...  186 us
    pallas_call x1, Pallas kernels, finish(): pl.pallas_call(finish_kernel, grid=(steps,), in_specs=[tile, tile, block,...  27.6 us

profile of v13, /device:TPU:0, one launch (start us, length us, event | category | flops | bytes accessed | tf_op | source)
XLA Modules:
  0.0 446.5 jit_solution(14041928041343997520)
XLA Ops:
  0.6 186.5 %front.1 = (bf16[2304,2048]{1,0:T(8,128)(2,1)}, bf16[4,2304,512]{2,1,0:T(8,128)(2,1)}, bf16[2304,512]{1,0:T(8,128)(2,1)}, bf16[2,2304,512]{2,1,0:T(8,128)(2,1)}, bf16[4,512,2048]{2,1,0:T(8,128)(2,1)}) custom-call(bf16[2304,2048]{1,0:T(8,128)(2,1)} %bitcast.7, bf16[2304,2048]{1,0:T(8,128)(2,1)} %bitcast.9, bf16[2048,512]{1,0:T(8,128)(2,1)} %wq_hbm.3, ...), custom_call_target="tpu_custom_call" | custom-call | flops 27179089920 | bytes 75497472 | tf_op jit(solution)/shard_map/front/pallas_call | solution.py:648
  187.1 231.1 %backward_norm.1 = (bf16[2304,2048]{1,0:T(8,128)(2,1)}, bf16[2304,2048]{1,0:T(8,128)(2,1)}, bf16[8,256,2048]{2,1,0:T(8,128)(2,1)}, bf16[8,256,2048]{2,1,0:T(8,12...) custom-call(bf16[2304,512]{1,0:T(8,128)(2,1)} %get-tuple-element.23.dq_hbm, ...), custom_call_target="tpu_custom_call", output_to_operand_aliasing={{5}: (4, {})} | custom-call | flops 53150220288 | bytes 75497472 | tf_op jit(solution)/shard_map/backward_norm/pallas_call | solution.py:1145
  418.2 0.0 copy-start
  418.2 27.6 %finish.1 = (bf16[2304,2048]{1,0:T(8,128)(2,1)}, bf16[2304,2048]{1,0:T(8,128)(2,1)}, f32[2048,512]{1,0:T(8,128)}, f32[2048,512]{1,0:T(8,128)}, f32[2048,512]{1,0:T(8,128)}, /*index=5*/f32[512,2048]{1,0:T(8,128)}) custom-call(bf16[2304,2048]{1,0:T(8,128)(2,1)} %get-tuple-element.28.y_ref, bf16[2304,2048]{1,0:T(8,128)(2,1)} %get-tuple-element.29.gx_ref, ...), custom_call_target="tpu_custom_call" | custom-call | flops 8388608 | bytes 71303168 | tf_op jit(solution)/shard_map/finish/pallas_call | solution.py:1201
  445.9 0.0 copy-done
  445.9 0.6 copy.19
Async XLA Ops:
  418.2 27.7 %copy-start = (f32[1,2048]{1,0:T(1,128)S(1)}, f32[1,2048]{1,0:T(1,128)}, u32[]{:S(2)}) copy-start(f32[1,2048]{1,0:T(1,128)} %get-tuple-element.34) | copy-start | bytes 24580

commit v14 on v13

--- a/solution.py
+++ b/solution.py
@@ -70,7 +70,7 @@
 SUB = 384
 ROWS = 32
 WIDTH = 256
-PARTS = 2
+PARTS = 1
 HALVES = 2
 RELAY_LAG = 1
 LATE = 3
@@ -147,7 +147,6 @@
     barrier = pltpu.get_barrier_semaphore()
     for dev in [partner, peer, twin] + [{"tp": lax.rem(z + dt, tp)} for dt in range(1, tp)]:
         pl.semaphore_signal(barrier, inc=1, device_id=dev, device_id_type=MESH)
-    pl.semaphore_wait(barrier, tp + 2)
 
     def remote(src, dst, ssem, rsem, dev):
         return pltpu.make_async_remote_copy(src_ref=src, dst_ref=dst, send_sem=ssem, recv_sem=rsem, device_id=dev, device_id_type=MESH)
@@ -177,9 +176,6 @@
 
     w_steps = range(1, tp)
 
-    for d in range(1, tp):
-        wz_copy(d).start()
-
     def kv_to_partner(u):
         return remote(kv_own.at[u], kvr.at[0, u], kvs_part.at[u], kv_recv.at[0, u], partner)
 
@@ -190,8 +186,6 @@
         return remote(kvr.at[1, u], kvr.at[2, u], kvs_far.at[u], kv_recv.at[2, u], partner)
 
     w_local = pltpu.make_async_copy(wo_ref, w_all.at[z], wl_sem.at[0])
-    for copy in weight_loads[:2]:
-        copy.wait()
 
     def angles(b, k):
         rows = tile_rows(b, k)
@@ -209,7 +203,7 @@
         cos_ref[rows, :] = cos_a * cos_b - sin_a * sin_b
         sin_ref[rows, :] = sin_a * cos_b + cos_a * sin_b
 
-    def project_row(b):
+    def project_row(b, first=False):
         ring = lax.rem(b, Q_RING)
         for k in range(per_row):
             rows = tile_rows(b, k)
@@ -231,12 +225,17 @@
             def _(k=k):
                 x_load(b + 1, k).start()
 
+            if first and k == 0:
+                for copy in weight_loads[:2]:
+                    copy.wait()
             for g in range(HALVES):
                 u = b * HALVES + g
                 cols = slice(g * half, (g + 1) * half)
                 put_rope(kv_own.at[u, 0, inside, :], dot_nn(n_buf[k], big[0, :, cols]), cos_ref[rows, :], sin_ref[rows, :])
                 kv_own[u, 1, inside, :] = dot_nn(n_buf[k], big[1, :, cols]).astype(BF16)
 
+        if first:
+            pl.semaphore_wait(barrier, tp + 2)
         for g in range(HALVES):
             u = b * HALVES + g
 
@@ -248,8 +247,9 @@
             def _(u=u):
                 kv_to_partner(u).start()
 
-        @pl.when(b == 0)
-        def _():
+        if first:
+            for d in range(1, tp):
+                wz_copy(d).start()
             for copy in weight_loads[2:]:
                 copy.wait()
             w_local.start()
@@ -545,7 +545,7 @@
         return carry
 
     for b in range(min(AHEAD, batch)):
-        project_row(b)
+        project_row(b, b == 0)
     lax.fori_loop(0, units, step, 0)
     chip_sum(units - 1)
 
@@ -721,7 +721,6 @@
     peers = [(dt, dc) for dt in range(tp) for dc in range(cp) if dt or dc]
     for dt, dc in peers:
         pl.semaphore_signal(barrier, inc=1, device_id={"tp": lax.rem(z + dt, tp), "cp": lax.rem(r + dc, cp)}, device_id_type=MESH)
-    pl.semaphore_wait(barrier, len(peers))
 
     def remote(src, dst, ssem, rsem, dev):
         return pltpu.make_async_remote_copy(src_ref=src, dst_ref=dst, send_sem=ssem, recv_sem=rsem, device_id=dev, device_id_type=MESH)
@@ -973,12 +972,6 @@
 
     gg_ref[...] = jnp.zeros_like(gg_ref)
     o_loads = [pltpu.make_async_copy(o_hbm.at[z, :, k * width:(k + 1) * width], n_in.at[k], job_sem.at[k, 0]) for k in range(hidden // width)]
-    for copy in o_loads:
-        copy.start()
-    for copy in inputs(0, 0):
-        copy.start()
-    for copy in rest_loads + out_loads:
-        copy.start()
     me = z * cp + r
 
     def gain_copy(dt, dc):
@@ -1004,14 +997,17 @@
     def late_move(n):
         return late_copy(n, z, jnp.where(z == 1, 0, last))
 
+    for copy in weight_loads:
+        copy.wait()
+    for copy in inputs(0, 0) + o_loads + rest_loads + out_loads:
+        copy.start()
+    partial_norm(0)
+    pl.semaphore_wait(barrier, len(peers))
     for n in range(len(late_units)):
         @pl.when(sends_late)
         def _(n=n):
             late_move(n).start()
 
-    for copy in weight_loads:
-        copy.wait()
-
     def step(i, carry):
         @pl.when(jnp.logical_and(gets_late, i == late_wait))
         def _():
@@ -1065,7 +1061,7 @@
             for copy in rest_loads:
                 copy.wait()
 
-        @pl.when(i < groups)
+        @pl.when(jnp.logical_and(i >= 1, i < groups))
         def _():
             partial_norm(i)
 
@@ -1175,7 +1171,8 @@
     )(dq, dkv, x, dy, o_all, normed, wq, wk, wv, wo_all, gain)
 
 
-def finish_kernel(y_ref, gx_ref, ga_ref, gb_ref, yo_ref, gxo_ref, wq_ref, wk_ref, wv_ref, wo_ref):
+def finish_kernel(y_ref, gx_ref, ga_ref, gb_ref, gg_ref, yo_ref, gxo_ref, wq_ref, wk_ref, wv_ref, wo_ref, ggo_ref):
+    ggo_ref[...] = gg_ref[...]
     yo_ref[...] = y_ref[...]
     gxo_ref[...] = gx_ref[...]
     rows = ga_ref.shape[1]
@@ -1190,7 +1187,7 @@
         wo_ref[pl.ds(pl.multiple_of(at, rows), rows), :] = ga_ref[0, :, cols].astype(F32) + gb_ref[0, :, cols].astype(F32)
 
 
-def finish(y, gx, ga, gb):
+def finish(y, gx, ga, gb, gg):
     tokens, d_model = y.shape
     blocks, width, packed = ga.shape
     hidden = packed // 4
@@ -1198,16 +1195,17 @@
     tile = pl.BlockSpec((tokens // steps, d_model), lambda j: (j, 0))
     block = pl.BlockSpec((1, width // PARTS, packed), lambda j: (j // PARTS, j % PARTS, 0))
     wide = pl.BlockSpec((width // PARTS, hidden), lambda j: (j, 0))
+    line = pl.BlockSpec((1, d_model), lambda j: (0, 0))
     return pl.pallas_call(
         finish_kernel,
         grid=(steps,),
-        in_specs=[tile, tile, block, block],
-        out_specs=[tile, tile, wide, wide, wide, pl.BlockSpec((hidden, width), lambda j: (0, j // PARTS))],
-        out_shape=[jax.ShapeDtypeStruct((tokens, d_model), BF16)] * 2 + [jax.ShapeDtypeStruct((d_model, hidden), F32)] * 3 + [jax.ShapeDtypeStruct((hidden, d_model), F32)],
+        in_specs=[tile, tile, block, block, line],
+        out_specs=[tile, tile, wide, wide, wide, pl.BlockSpec((hidden, width), lambda j: (0, j // PARTS)), line],
+        out_shape=[jax.ShapeDtypeStruct((tokens, d_model), BF16)] * 2 + [jax.ShapeDtypeStruct((d_model, hidden), F32)] * 3 + [jax.ShapeDtypeStruct((hidden, d_model), F32), jax.ShapeDtypeStruct((1, d_model), F32)],
         compiler_params=pltpu.CompilerParams(dimension_semantics=("arbitrary",), vmem_limit_bytes=48 << 20),
         cost_estimate=pl.CostEstimate(flops=8 * d_model * hidden, bytes_accessed=8 * tokens * d_model + 32 * d_model * hidden, transcendentals=0),
         name="finish",
-    )(y, gx, ga, gb)
+    )(y, gx, ga, gb, gg)
 
 
 def solution(mesh):
@@ -1223,8 +1221,8 @@
         gain = norm_gain.reshape(1, d_model)
         normed, o_all, dq, dkv, w_all = front(x, dy, w_query, w_key, w_value, w_out, positions, jnp.asarray(angle_table(), BF16), gain, seq, tp_size, cp_size)
         grad_x, y_out, sum_a, sum_b, grad_gain, _ = backward_norm(dq, dkv, x, dy, o_all, normed, w_query, w_key, w_value, w_all, gain, ROWS, seq, tp_size, cp_size)
+        y_out, grad_x, grad_wq, grad_wk, grad_wv, grad_wo, grad_gain = finish(y_out, grad_x, sum_a, sum_b, grad_gain)
         grad_gain = grad_gain.reshape(d_model)
-        y_out, grad_x, grad_wq, grad_wk, grad_wv, grad_wo = finish(y_out, grad_x, sum_a, sum_b)
         return y_out.reshape(x_in.shape), grad_x.reshape(x_in.shape), grad_gain, grad_wq, grad_wk, grad_wv, grad_wo
 
     in_specs = (P("dp", "cp", None), P("dp", "cp"), P("dp", "cp"), P(None, "tp"), P(None, "tp"), P(None, "tp"), P("tp", None), P(None), P("dp", "cp", None))

time: 447 us -> 443 us (level)
  no operation moved by 1% of the time
where the time goes in v14:
time: 443 us; the launch traced here: 442 us
  Pallas kernels  441 us (100%)
    pallas_call x1, Pallas kernels, backward_norm(): pl.pallas_call(functools.partial(back_kernel, groups, rows, tp, cp, seq),...  232 us
    pallas_call x1, Pallas kernels, front(): pl.pallas_call(functools.partial(front_kernel, batch, seq, tp, cp), in_sp...  185 us
    pallas_call x1, Pallas kernels, finish(): pl.pallas_call(finish_kernel, grid=(steps,), in_specs=[tile, tile, block,...  23.4 us

profile of v14, /device:TPU:0, one launch (start us, length us, event | category | flops | bytes accessed | tf_op | source)
XLA Modules:
  0.0 442.2 jit_solution(9363036870694257383)
XLA Ops:
  0.6 185.4 %front.1 = (bf16[2304,2048]{1,0:T(8,128)(2,1)}, bf16[4,2304,512]{2,1,0:T(8,128)(2,1)}, bf16[2304,512]{1,0:T(8,128)(2,1)}, bf16[2,2304,512]{2,1,0:T(8,128)(2,1)}, bf16[4,512,2048]{2,1,0:T(8,128)(2,1)}) custom-call(bf16[2304,2048]{1,0:T(8,128)(2,1)} %bitcast.6, bf16[2304,2048]{1,0:T(8,128)(2,1)} %bitcast.8, bf16[2048,512]{1,0:T(8,128)(2,1)} %wq_hbm.3, ...), custom_call_target="tpu_custom_call" | custom-call | flops 27179089920 | bytes 75497472 | tf_op jit(solution)/shard_map/front/pallas_call | solution.py:648
  186.0 231.9 %backward_norm.1 = (bf16[2304,2048]{1,0:T(8,128)(2,1)}, bf16[2304,2048]{1,0:T(8,128)(2,1)}, bf16[8,256,2048]{2,1,0:T(8,128)(2,1)}, bf16[8,256,2048]{2,1,0:T(8,12...) custom-call(bf16[2304,512]{1,0:T(8,128)(2,1)} %get-tuple-element.24.dq_hbm, ...), custom_call_target="tpu_custom_call", output_to_operand_aliasing={{5}: (4, {})} | custom-call | flops 53150220288 | bytes 75497472 | tf_op jit(solution)/shard_map/backward_norm/pallas_call | solution.py:1141
  418.0 0.0 copy-start
  418.0 0.7 copy-done
  418.7 23.4 %finish.1 = (bf16[2304,2048]{1,0:T(8,128)(2,1)}, bf16[2304,2048]{1,0:T(8,128)(2,1)}, f32[2048,512]{1,0:T(8,128)}, f32[2048,512]{1,0:T(8,128)}, f32[2048,512]{1,0...) custom-call(bf16[2304,2048]{1,0:T(8,128)(2,1)} %get-tuple-element.29.y_ref, ...), custom_call_target="tpu_custom_call" | custom-call | flops 8388608 | bytes 71303168 | tf_op jit(solution)/shard_map/finish/pallas_call | solution.py:1199
Async XLA Ops:
  418.0 0.7 copy-start

commit v15 on v14

--- a/solution.py
+++ b/solution.py
@@ -267,7 +267,7 @@
 
     def o_place(src, u):
         b, g = where(u)
-        return o_all.at[src, row(b), half_cols(g)]
+        return o_all.at[src, b, g]
 
     def o_local_copy(b):
         return pltpu.make_async_copy(o_buf.at[b], o_place(z, b), o_local.at[b])
@@ -651,7 +651,7 @@
         out_specs=[hbm] * 5,
         out_shape=[
             jax.ShapeDtypeStruct((tokens, d_model), BF16),
-            jax.ShapeDtypeStruct((tp, tokens, hidden), BF16),
+            jax.ShapeDtypeStruct((tp, batch, HALVES, seq, half), BF16),
             jax.ShapeDtypeStruct((tokens, hidden), BF16),
             jax.ShapeDtypeStruct((2, tokens, hidden), BF16),
             jax.ShapeDtypeStruct((tp, hidden, d_model), BF16),
@@ -688,7 +688,7 @@
                 wq_ref, wk_ref, wv_ref, wo_ref, dq_all, dkv_all, o_t, part, rs_r, rs_l, send_r, send_l, tot, gx_buf,
                 o_in, x_in, xo_in, dyo_in, y_buf, n_in, dy_in, away, part_in, mine, gain_all,
                 w_sem, in_sem, fin_sem, job_sem, y_sem, own_sem, rss_r, rss_l, rsr_r, rsr_l, ag0_r, ag0_l, agf_r, agf_l, agr_r, agr_l,
-                away_send, away_recv, mine_own, mine_part, mine_chip, ga_recv, chip_recv, gb_send, gb_recv, gs_sem, gr_sem, late_send, late_recv):
+                away_send, away_recv, mine_own, mine_part, mine_chip, ga_recv, chip_recv, gb_send, gb_recv, gs_sem, gr_sem, late_send, late_recv, o_sem):
     o_hbm = o_out
     z = lax.axis_index("tp")
     r = lax.axis_index("cp")
@@ -702,6 +702,7 @@
     chunk = min(512, d_model)
     blocks = ga_hbm.shape[0]
     width = ga_hbm.shape[1]
+    half = hidden // HALVES
     pairs = blocks // 2
     partner = {"cp": r + 1 - 2 * core}
     peer = {"cp": r + 2 - 4 * chip}
@@ -737,7 +738,7 @@
     def inputs(i, slot):
         g = group_rows(i)
         return [
-            pltpu.make_async_copy(o_hbm.at[:, g, :], o_in.at[slot], in_sem.at[slot, 0]),
+            pltpu.make_async_copy(o_hbm.at[:, lax.div(i, seq // span), :, pl.ds(pl.multiple_of(lax.rem(i, seq // span) * span, span), span), :], o_in.at[slot], in_sem.at[slot, 0]),
             pltpu.make_async_copy(x_hbm.at[g, :], x_in.at[slot], in_sem.at[slot, 1]),
         ]
 
@@ -855,7 +856,8 @@
             cols = slice(c, c + chunk)
             acc = x_in[cur, :, cols].astype(F32)
             for t in range(tp):
-                acc += dot_nn(o_in[cur, t], wo_ref[t, :, cols])
+                for h in range(HALVES):
+                    acc += dot_nn(o_in[cur, t, h], wo_ref[t, h * half:(h + 1) * half, cols])
             y_buf[cur, :, cols] = acc.astype(BF16)
 
     def finalize(i):
@@ -971,7 +973,7 @@
             mine_to_own(p, slot).start()
 
     gg_ref[...] = jnp.zeros_like(gg_ref)
-    o_loads = [pltpu.make_async_copy(o_hbm.at[z, :, k * width:(k + 1) * width], n_in.at[k], job_sem.at[k, 0]) for k in range(hidden // width)]
+    o_loads = [pltpu.make_async_copy(o_hbm.at[z, b, k], n_in.at[k, b * seq:(b + 1) * seq, :], o_sem.at[k, b]) for k in range(HALVES) for b in range(tokens // seq)]
     me = z * cp + r
 
     def gain_copy(dt, dc):
@@ -983,7 +985,6 @@
         remote(gain_all.at[sender], gain_all.at[sender], gs_sem.at[0], gr_sem.at[sender], right).wait_recv()
 
     units = tokens // seq * HALVES
-    half = hidden // HALVES
     late_units = range(max(0, units - LATE), units)
     late_wait = max(0, late_units[0] // HALVES * seq // span + OUT_LAG - 2)
     sends_late = jnp.logical_or(z == 1, z == last - 1)
@@ -991,7 +992,7 @@
 
     def late_copy(n, src, dst):
         u = late_units[n]
-        place = o_out.at[src, u // HALVES * seq:(u // HALVES + 1) * seq, u % HALVES * half:(u % HALVES + 1) * half]
+        place = o_out.at[src, u // HALVES, u % HALVES]
         return remote(place, place, late_send.at[n], late_recv.at[n], {"tp": dst})
 
     def late_move(n):
@@ -1067,9 +1068,10 @@
 
         @pl.when(i == JOB_LAG - 1)
         def _():
-            for k, copy in enumerate(o_loads):
+            for copy in o_loads:
                 copy.wait()
-                o_t[k * width:(k + 1) * width, :] = n_in[k].T
+            for k in range(HALVES):
+                o_t[k * half:(k + 1) * half, :] = n_in[k].T
             for copy in job_loads(0, 0):
                 copy.start()
 
@@ -1156,14 +1158,14 @@
             bf(tokens, hidden), bf(2, tokens, hidden), bf(hidden, tokens),
             f32(PART_RING, span, d_model), bf(RS_RING, slots, rows, d_model), bf(RS_RING, slots, rows, d_model),
             bf(slots, rows, d_model), bf(slots, rows, d_model), f32(rows, d_model), bf(2, rows, d_model),
-            bf(2, tp, span, hidden), bf(2, span, d_model), bf(2, rows, d_model), bf(2, rows, d_model), bf(2, span, d_model),
+            bf(2, tp, HALVES, span, hidden // HALVES), bf(2, span, d_model), bf(2, rows, d_model), bf(2, rows, d_model), bf(2, span, d_model),
             bf(2, tokens, width), bf(2, tokens, width),
             f32(width, 4 * hidden), f32(2, width, 4 * hidden), bf(2, width, 4 * hidden), f32(tp * cp, 1, d_model),
             dma((8,)), dma((2, 2)), dma((2, 2)), dma((2, 2)), dma((2,)), dma((2,)),
             dma((slots,)), dma((slots,)), dma((RS_RING, slots)), dma((RS_RING, slots)),
             dma((2,)), dma((2,)), dma((slots,)), dma((slots,)), dma((groups, slots)), dma((groups, slots)),
             dma((1,)), dma((2,)), dma((2,)), dma((2,)), dma((2,)), dma((pairs,)), dma((pairs,)), dma((pairs,)), dma((pairs,)),
-            dma((tp * cp,)), dma((tp * cp,)), dma((max(LATE, 1),)), dma((max(LATE, 1),)),
+            dma((tp * cp,)), dma((tp * cp,)), dma((max(LATE, 1),)), dma((max(LATE, 1),)), dma((HALVES, tokens // seq)),
         ],
         compiler_params=pltpu.CompilerParams(collective_id=0, has_side_effects=True, vmem_limit_bytes=63 << 20),
         cost_estimate=pl.CostEstimate(flops=22 * tokens * hidden * d_model, bytes_accessed=16 * tokens * d_model, transcendentals=0),

time: 443 us -> 443 us (level)
  no operation moved by 1% of the time
where the time goes in v15:
time: 443 us; the launch traced here: 442 us
  Pallas kernels  441 us (100%)
    pallas_call x1, Pallas kernels, backward_norm(): pl.pallas_call(functools.partial(back_kernel, groups, rows, tp, cp, seq),...  232 us
    pallas_call x1, Pallas kernels, front(): pl.pallas_call(functools.partial(front_kernel, batch, seq, tp, cp), in_sp...  185 us
    pallas_call x1, Pallas kernels, finish(): pl.pallas_call(finish_kernel, grid=(steps,), in_specs=[tile, tile, block,...  23.4 us

profile of v15, /device:TPU:0, one launch (start us, length us, event | category | flops | bytes accessed | tf_op | source)
XLA Modules:
  0.0 442.4 jit_solution(10417868395034973327)
XLA Ops:
  0.6 185.5 %front.1 = (bf16[2304,2048]{1,0:T(8,128)(2,1)}, bf16[4,6,2,384,256]{4,3,2,1,0:T(8,128)(2,1)}, bf16[2304,512]{1,0:T(8,128)(2,1)}, bf16[2,2304,512]{2,1,0:T(8,128)(2,1)}, bf16[4,512,2048]{2,1,0:T(8,128)(2,1)}) custom-call(bf16[2304,2048]{1,0:T(8,128)(2,1)} %bitcast.6, bf16[2304,2048]{1,0:T(8,128)(2,1)} %bitcast.8, bf16[2048,512]{1,0:T(8,128)(2,1)} %wq_hbm.3, ...), custom_call_target="tpu_custom_call" | custom-call | flops 27179089920 | bytes 75497472 | tf_op jit(solution)/shard_map/front/pallas_call | solution.py:648
  186.1 232.0 %backward_norm.1 = (bf16[2304,2048]{1,0:T(8,128)(2,1)}, bf16[2304,2048]{1,0:T(8,128)(2,1)}, bf16[8,256,2048]{2,1,0:T(8,128)(2,1)}, bf16[8,256,2048]{2,1,0:T(8,12...) custom-call(bf16[2304,512]{1,0:T(8,128)(2,1)} %get-tuple-element.24.dq_hbm, ...), custom_call_target="tpu_custom_call", output_to_operand_aliasing={{5}: (4, {})} | custom-call | flops 53150220288 | bytes 75497472 | tf_op jit(solution)/shard_map/backward_norm/pallas_call | solution.py:1143
  418.1 0.0 copy-start
  418.1 0.7 copy-done
  418.8 23.4 %finish.1 = (bf16[2304,2048]{1,0:T(8,128)(2,1)}, bf16[2304,2048]{1,0:T(8,128)(2,1)}, f32[2048,512]{1,0:T(8,128)}, f32[2048,512]{1,0:T(8,128)}, f32[2048,512]{1,0...) custom-call(bf16[2304,2048]{1,0:T(8,128)(2,1)} %get-tuple-element.29.y_ref, ...), custom_call_target="tpu_custom_call" | custom-call | flops 8388608 | bytes 71303168 | tf_op jit(solution)/shard_map/finish/pallas_call | solution.py:1201
Async XLA Ops:
  418.1 0.7 copy-start

commit v16 on v14

--- a/solution.py
+++ b/solution.py
@@ -532,10 +532,6 @@
                 w_move(0, d).wait_recv()
                 w_move(2, d).start()
 
-                @pl.when(second_chip)
-                def _(d=d):
-                    w_move(4, d).start()
-
         @pl.when(jnp.logical_and(first_chip, i == min(W_CHIP, units - 1)))
         def _():
             for k in (3, 4):
@@ -548,6 +544,11 @@
         project_row(b, b == 0)
     lax.fori_loop(0, units, step, 0)
     chip_sum(units - 1)
+
+    @pl.when(second_chip)
+    def _():
+        for d in w_steps:
+            w_move(4, d).start()
 
     end = units + max(SUM_LAG, (tp - 2) * RELAY_LAG)
     for i in range(units, end):

time: 443 us -> 451 us (1.018)
  Pallas kernels: 441 us -> 450 us
    pallas_call x1, Pallas kernels: 185 us -> 194 us  [front(): pl.pallas_call(functools.partial(front_kernel, batch, seq, tp, cp), in_sp...]
where the time goes in v16:
time: 451 us
  Pallas kernels  450 us (100%)
    pallas_call x1, Pallas kernels, backward_norm(): pl.pallas_call(functools.partial(back_kernel, groups, rows, tp, cp, seq),...  233 us
    pallas_call x1, Pallas kernels, front(): pl.pallas_call(functools.partial(front_kernel, batch, seq, tp, cp), in_sp...  194 us
    pallas_call x1, Pallas kernels, finish(): pl.pallas_call(finish_kernel, grid=(steps,), in_specs=[tile, tile, block,...  23.4 us

profile of v16, /device:TPU:0, one launch (start us, length us, event | category | flops | bytes accessed | tf_op | source)
XLA Modules:
  0.0 451.0 jit_solution(17886013699438184863)
XLA Ops:
  0.6 193.5 %front.1 = (bf16[2304,2048]{1,0:T(8,128)(2,1)}, bf16[4,2304,512]{2,1,0:T(8,128)(2,1)}, bf16[2304,512]{1,0:T(8,128)(2,1)}, bf16[2,2304,512]{2,1,0:T(8,128)(2,1)}, bf16[4,512,2048]{2,1,0:T(8,128)(2,1)}) custom-call(bf16[2304,2048]{1,0:T(8,128)(2,1)} %bitcast.6, bf16[2304,2048]{1,0:T(8,128)(2,1)} %bitcast.8, bf16[2048,512]{1,0:T(8,128)(2,1)} %wq_hbm.3, ...), custom_call_target="tpu_custom_call" | custom-call | flops 27179089920 | bytes 75497472 | tf_op jit(solution)/shard_map/front/pallas_call | solution.py:649
  194.2 232.6 %backward_norm.1 = (bf16[2304,2048]{1,0:T(8,128)(2,1)}, bf16[2304,2048]{1,0:T(8,128)(2,1)}, bf16[8,256,2048]{2,1,0:T(8,128)(2,1)}, bf16[8,256,2048]{2,1,0:T(8,12...) custom-call(bf16[2304,512]{1,0:T(8,128)(2,1)} %get-tuple-element.24.dq_hbm, ...), custom_call_target="tpu_custom_call", output_to_operand_aliasing={{5}: (4, {})} | custom-call | flops 53150220288 | bytes 75497472 | tf_op jit(solution)/shard_map/backward_norm/pallas_call | solution.py:1142
  426.8 0.0 copy-start
  426.8 0.7 copy-done
  427.5 23.4 %finish.1 = (bf16[2304,2048]{1,0:T(8,128)(2,1)}, bf16[2304,2048]{1,0:T(8,128)(2,1)}, f32[2048,512]{1,0:T(8,128)}, f32[2048,512]{1,0:T(8,128)}, f32[2048,512]{1,0...) custom-call(bf16[2304,2048]{1,0:T(8,128)(2,1)} %get-tuple-element.29.y_ref, ...), custom_call_target="tpu_custom_call" | custom-call | flops 8388608 | bytes 71303168 | tf_op jit(solution)/shard_map/finish/pallas_call | solution.py:1200
Async XLA Ops:
  426.8 0.7 copy-start
